TPU v7x, 32 devices: a whole 2x2x4 slice. The times are simulated.
32 devices in a mesh: patch: 8 (over z, y), sub: 4 (over x, core).
Axes of the slice: x: 2, y: 2, z: 4, core: 2. Of those that a mesh axis runs over, the one named last changes fastest.
Arguments:
- heat: float32 [262144], P(('patch', 'sub')), may hold values from -6 to 6
- basis: bfloat16 [9, 524288], P(None, ('patch', 'sub')), may hold values from -3 to 3
- area: float32 [524288], P(('patch', 'sub')), may hold values from 0.2 to 2
- corners: int32 [3, 524288], P(None, ('patch', 'sub')), may hold values from 0 to 9215, as said below
- send_sub: int32 [4096], P(('patch', 'sub')), may hold values from 0 to 8191
- send_pat: int32 [4, 4096], P(None, ('patch', 'sub')), may hold values from 0 to 8191
- live_faces: int32 [32], P(('patch', 'sub')), may hold values from 12288 to 16384, as said below
Outputs:
- divergence: float32 [262144], P(('patch', 'sub'))
Inputs may be any that keep to these rules, and one draw needn't show every extreme that they name: Face slot f of a device lies in tile t = f // 128; each of its corners is either an owned position in [64 t - 128, 64 t + 128) or a remote position from 8192 + 256 (t mod (4)) up to 255 beyond that; every position of the device's table is read by some face of the device. `live_faces`: some device has all 16384 slots live.
All inputs are finite; a program needn't handle non-finite values.
Results may differ from a plain program's by a relative error of at most 0.0003.
Values sent between devices are 32-bit elements; how exact they have to be, the bound alone decides.
No kernel may reach another device: no remote copies, remote signals or barrier semaphores. Data moves between devices by JAX's collectives and lax.ppermute only.
A program may use at most 64 MiB of HBM per device.

v0:
```python
import jax
import jax.numpy as jnp
from jax import lax
from jax.sharding import PartitionSpec as P

RADIUS = 2


def from_behind(x, axis, by):
    length = lax.axis_size(axis)
    return lax.ppermute(x, axis, [(i, (i + by) % length) for i in range(length)])


def offset_list():
    return [k + 1 for k in range(RADIUS)] + [-(k + 1) for k in range(RADIUS)]


def tile_terms(
    window,
    remote_window,
    corner_tile,
    basis_tile,
    area_tile,
    start,
    remote_start,
    first_slot,
    live_count,
):
    window_pos = jnp.arange(window.shape[0])
    remote_pos = jnp.arange(remote_window.shape[0])
    onehot_near = (corner_tile[:, :, None] - start == window_pos).astype(jnp.float32)
    onehot_far = (corner_tile[:, :, None] - remote_start == remote_pos).astype(jnp.float32)
    values = jnp.einsum("kfw,w->kf", onehot_near, window, precision=lax.Precision.HIGHEST)
    values = values + jnp.einsum(
        "kfw,w->kf", onehot_far, remote_window, precision=lax.Precision.HIGHEST
    )
    width = corner_tile.shape[1]
    gradients = basis_tile.astype(jnp.float32).reshape(3, 3, width)
    gradient = jnp.sum(gradients * values[:, None, :], axis=0)
    length = jnp.sqrt(jnp.sum(gradient * gradient, axis=0))
    field = -gradient / jnp.maximum(length, 1.0)
    projected = jnp.sum(gradients * field[None, :, :], axis=1)
    live_mask = first_slot + jnp.arange(width) < live_count
    weight = jnp.where(live_mask, area_tile, 0.0)
    terms = projected * weight[None, :]
    near_sums = jnp.einsum("kfw,kf->w", onehot_near, terms, precision=lax.Precision.HIGHEST)
    far_sums = jnp.einsum("kfw,kf->w", onehot_far, terms, precision=lax.Precision.HIGHEST)
    return (near_sums, far_sums)


def face_terms(heat, remote, corners, basis, area, live_count):
    owned = heat.shape[0]
    slots = corners.shape[1]
    tiles = slots // 128
    remote_len = remote.shape[0]
    remote_win = min(256, remote_len)
    remote_blocks = remote_len // remote_win
    padded = jnp.pad(heat, (128, 128))
    pieces = padded.reshape(tiles + 4, 64)
    windows = jnp.concatenate([pieces[shift : shift + tiles] for shift in range(4)], axis=1)
    remote_tiles = jnp.tile(remote.reshape(remote_blocks, remote_win), (tiles // remote_blocks, 1))
    tile_ids = jnp.arange(tiles)
    starts = 64 * tile_ids - 128
    remote_starts = owned + remote_win * (tile_ids % remote_blocks)
    first_slots = 128 * tile_ids
    corner_tiles = corners.reshape(3, tiles, 128).transpose(1, 0, 2)
    basis_tiles = basis.reshape(9, tiles, 128).transpose(1, 0, 2)
    area_tiles = area.reshape(tiles, 128)
    batch = 1
    limit = max(1, tiles // 16)
    while batch * 2 <= limit and tiles % (batch * 2) == 0:
        batch = batch * 2
    groups = tiles // batch
    packed = (
        windows,
        remote_tiles,
        corner_tiles,
        basis_tiles,
        area_tiles,
        starts,
        remote_starts,
        first_slots,
    )
    packed = jax.tree.map(lambda array: array.reshape((groups, batch) + array.shape[1:]), packed)

    def run_group(pack):
        return jax.vmap(
            lambda w, r, c, b, a, s, q, f: tile_terms(w, r, c, b, a, s, q, f, live_count)
        )(*pack)

    near_sums, far_sums = lax.map(run_group, packed)
    near_sums = near_sums.reshape(tiles, 4, 64)
    summed = jnp.zeros((tiles + 4, 64), jnp.float32)
    for shift in range(4):
        summed = summed + jnp.pad(near_sums[:, shift], ((shift, 4 - shift), (0, 0)))
    owned_sums = summed.reshape(-1)[128 : 128 + owned]
    far_sums = far_sums.reshape(tiles // remote_blocks, remote_blocks, remote_win)
    remote_sums = jnp.sum(far_sums, axis=0).reshape(-1)
    return (owned_sums, remote_sums)


def per_device(heat, basis, area, corners, send_sub, send_pat, live_faces):
    sub_count = lax.axis_size("sub")
    group_size = send_sub.shape[0]
    block_size = send_pat.shape[1]
    offsets = offset_list()
    group_send = jnp.take(heat, send_sub)
    group_values = lax.all_gather(group_send, "sub", axis=0, tiled=True)
    outgoing = jnp.take(heat, send_pat)
    incoming = jnp.stack(
        [
            from_behind(outgoing[block_index], "patch", offset)
            for block_index, offset in enumerate(offsets)
        ]
    )
    remote = jnp.concatenate([group_values, incoming.reshape(-1)])
    result, remote_sums = face_terms(heat, remote, corners, basis, area, live_faces[0])
    group_part = remote_sums[: sub_count * group_size]
    patch_part = remote_sums[sub_count * group_size :].reshape(2 * RADIUS, block_size)
    group_back = lax.psum_scatter(group_part, "sub", scatter_dimension=0, tiled=True)
    returned = jnp.stack(
        [
            from_behind(patch_part[block_index], "patch", -offset)
            for block_index, offset in enumerate(offsets)
        ]
    )
    result = result.at[send_sub].add(group_back)
    result = result.at[send_pat.reshape(-1)].add(returned.reshape(-1))
    return result


def solution(mesh):
    placed = (
        P(("patch", "sub")),
        P(None, ("patch", "sub")),
        P(("patch", "sub")),
        P(None, ("patch", "sub")),
        P(("patch", "sub")),
        P(None, ("patch", "sub")),
        P(("patch", "sub")),
    )
    return jax.shard_map(
        per_device, mesh=mesh, in_specs=placed, out_specs=P(("patch", "sub")), check_vma=False
    )
```

profile of v0, /device:TPU:0, one launch (start us, length us, event | category | flops | bytes accessed | tf_op | source)
XLA Modules:
  0.0 180.9 jit_solution(4505595029857006863)
XLA Ops:
  0.7 3.5 %gather_fusion.1 = f32[512]{0:T(512)S(1)} fusion(f32[8192]{0:T(1024)} %param.9, s32[1024]{0:T(1024)S(1)} %pad_clamp_fusion), kind=kCustom, calls=%fused_computation.1 | custom fusion | bytes 6144 | tf_op jit(solution)/shard_map/jit(_take)/gather | solution.py:109
  4.2 3.0 %collective-permute-start = (f32[128]{0:T(128)S(1)}, f32[128]{0:T(128)S(1)}, u32[]{:S(2)}, u32[]{:S(2)}) collective-permute-start(f32[128]{0:T(128)S(1)} %get-tuple-element.135), channel_id=1, source_target_pairs={{0,4},{4,8},{8,12},{12,16},{16,20},{20,24},{24,28},{28,0},{1,5},{5... | collective-permute-start | bytes 1544 | tf_op jit(solution)/shard_map/ppermute | solution.py:11
  7.3 1.6 collective-permute-start.1
  8.9 3.2 %collective-permute-start.2 = (f32[128]{0:T(128)S(1)}, f32[128]{0:T(128)S(1)}, u32[]{:S(2)}, u32[]{:S(2)}) collective-permute-start(f32[128]{0:T(128)S(1)} %get-tuple-element.137), channel_id=1, source_target_pairs={{0,28},{4,0},{8,4},{12,8},{16,12},{20,16},{24,20},{28,24},{1,29},{... | collective-permute-start | bytes 1544 | tf_op jit(solution)/shard_map/ppermute | solution.py:11
  13.9 5.1 %all-gather = f32[4,1,128]{2,1,0:T(1,128)S(1)} all-gather(f32[1,1,128]{2,1,0:T(1,128)S(1)} %fusion.22), channel_id=1, replica_groups=mesh['patch'=8,'sub'=4] {'sub'}, dimensions={0}, use_global_device_ids=true | all-gather | bytes 2560 | tf_op jit(solution)/shard_map/all_gather | solution.py:108
  22.6 140.8 %while.12 = (s32[]{:T(128)}, f32[16,8,256]{2,1,0:T(8,128)S(1)}, f32[16,8,256]{2,1,0:T(8,128)S(1)}, s32[16,8,3,128]{3,2,1,0:T(4,128)}, s32[16,8]{1,0:T(8,128)S(1)...) while((s32[]{:T(128)}, f32[16,8,256]{2,1,0:T(8,128)S(1)}, ...), condition=%wide.region_4.5_spmd, body=%wide.region_0.4_spmd.sunk | while | flops 40971264 | bytes 483781 | solution.py:91
  23.5 1.7 fusion.44
  25.2 1.7 fusion.45
  29.9 1.5 fusion.49
  32.3 1.7 fusion.44
  34.0 1.7 fusion.45
  38.7 1.5 fusion.49
  41.1 1.7 fusion.44
  42.8 1.7 fusion.45
  47.5 1.5 fusion.49
  49.9 1.7 fusion.44
  51.6 1.7 fusion.45
  56.3 1.5 fusion.49
  58.7 1.7 fusion.44
  60.4 1.7 fusion.45
  65.1 1.5 fusion.49
  67.5 1.7 fusion.44
  69.2 1.7 fusion.45
  73.9 1.5 fusion.49
  76.3 1.7 fusion.44
  78.0 1.7 fusion.45
  85.1 1.7 fusion.44
  86.8 1.7 fusion.45
  93.9 1.7 fusion.44
  95.6 1.7 fusion.45
  102.7 1.7 fusion.44
  104.4 1.7 fusion.45
  111.5 1.7 fusion.44
  113.2 1.7 fusion.45
  120.3 1.7 fusion.44
  122.0 1.7 fusion.45
  129.1 1.7 fusion.44
  130.8 1.7 fusion.45
  137.9 1.7 fusion.44
  139.6 1.7 fusion.45
  146.7 1.7 fusion.44
  148.4 1.7 fusion.45
  155.5 1.7 fusion.44
  157.2 1.7 fusion.45
  163.9 2.0 %collective-permute-start.4 = (f32[128]{0:T(128)S(1)}, f32[128]{0:T(128)S(1)}, u32[]{:S(2)}, u32[]{:S(2)}) collective-permute-start(f32[128]{0:T(128)S(1)} %get-tuple-element.131), channel_id=1, source_target_pairs={{0,28},{4,0},{8,4},{12,8},{16,12},{20,16},{24,20},{28,24},{1,29},{... | collective-permute-start | bytes 1544 | tf_op jit(solution)/shard_map/ppermute | solution.py:11
  166.4 1.5 collective-permute-start.6
  168.1 6.5 %all-reduce.5 = f32[512]{0:T(512)S(1)} all-reduce(f32[512]{0:T(512)S(1)} %bitcast.134), channel_id=2, replica_groups=mesh['patch'=8,'sub'=4] {'sub'}, use_global_device_ids=true, to_apply=%region_6.7.clone | all-reduce | flops 512 | bytes 4096
  176.6 4.4 %scatter_fusion.1 = f32[8192]{0:T(1024)} fusion(f32[8192]{0:T(1024)} %copy-done.1, s32[512]{0:T(512)S(1)} %bitcast.133, f32[512]{0:T(512)S(1)} %maximum_bitcast_fusion), kind=kCustom, calls=%fused_computation.3 | custom fusion | flops 512 | bytes 8192 | tf_op jit(solution)/shard_map/scatter-add | solution.py:128
  (348 shorter events, 84.1 us)
Async XLA Ops:
  0.7 3.5 %copy-start.3 = (s32[4,128]{1,0:T(4,128)S(1)}, s32[4,128]{1,0:T(4,128)}, u32[]{:S(2)}) copy-start(s32[4,128]{1,0:T(4,128)} %param.14) | copy-start | bytes 6148
  0.7 11.7 %copy-start = (f32[8192]{0:T(1024)S(1)}, f32[8192]{0:T(1024)}, u32[]{:S(2)}) copy-start(f32[8192]{0:T(1024)} %param.9) | copy-start | bytes 98308
  0.7 11.9 %copy-start.4 = (s32[128]{0:T(128)S(1)}, s32[128]{0:T(128)}, u32[]{:S(2)}) copy-start(s32[128]{0:T(128)} %param.13) | copy-start | bytes 1540
  4.2 18.2 %collective-permute-start = (f32[128]{0:T(128)S(1)}, f32[128]{0:T(128)S(1)}, u32[]{:S(2)}, u32[]{:S(2)}) collective-permute-start(f32[128]{0:T(128)S(1)} %get-tuple-element.135), channel_id=1, source_target_pairs={{0,4},{4,8},{8,12},{12,16},{16,20},{20,24},{24,28},{28,0},{1,5},{5... | collective-permute-start | bytes 1544 | tf_op jit(solution)/shard_map/ppermute | solution.py:11
  7.3 15.2 %collective-permute-start.1 = (f32[128]{0:T(128)S(1)}, f32[128]{0:T(128)S(1)}, u32[]{:S(2)}, u32[]{:S(2)}) collective-permute-start(f32[128]{0:T(128)S(1)} %get-tuple-element.138), channel_id=1, source_target_pairs={{0,8},{4,12},{8,16},{12,20},{16,24},{20,28},{24,0},{28,4},{1,9},{5... | collective-permute-start | bytes 1544 | tf_op jit(solution)/shard_map/ppermute | solution.py:11
  8.9 13.6 %collective-permute-start.2 = (f32[128]{0:T(128)S(1)}, f32[128]{0:T(128)S(1)}, u32[]{:S(2)}, u32[]{:S(2)}) collective-permute-start(f32[128]{0:T(128)S(1)} %get-tuple-element.137), channel_id=1, source_target_pairs={{0,28},{4,0},{8,4},{12,8},{16,12},{20,16},{24,20},{28,24},{1,29},{... | collective-permute-start | bytes 1544 | tf_op jit(solution)/shard_map/ppermute | solution.py:11
  12.1 10.4 %collective-permute-start.3 = (f32[128]{0:T(128)S(1)}, f32[128]{0:T(128)S(1)}, u32[]{:S(2)}, u32[]{:S(2)}) collective-permute-start(f32[128]{0:T(128)S(1)} %get-tuple-element.136), channel_id=1, source_target_pairs={{0,24},{4,28},{8,0},{12,4},{16,8},{20,12},{24,16},{28,20},{1,25},{... | collective-permute-start | bytes 1544 | tf_op jit(solution)/shard_map/ppermute | solution.py:11
  12.5 7.8 %copy-start.2 = (bf16[9,16384]{1,0:T(8,128)(2,1)S(1)}, bf16[9,16384]{1,0:T(8,128)(2,1)}, u32[]{:S(2)}) copy-start(bf16[9,16384]{1,0:T(8,128)(2,1)} %param.10) | copy-start | bytes 884740
  20.4 0.7 copy-start.5
  163.9 12.1 %collective-permute-start.4 = (f32[128]{0:T(128)S(1)}, f32[128]{0:T(128)S(1)}, u32[]{:S(2)}, u32[]{:S(2)}) collective-permute-start(f32[128]{0:T(128)S(1)} %get-tuple-element.131), channel_id=1, source_target_pairs={{0,28},{4,0},{8,4},{12,8},{16,12},{20,16},{24,20},{28,24},{1,29},{... | collective-permute-start | bytes 1544 | tf_op jit(solution)/shard_map/ppermute | solution.py:11
  165.9 10.1 %collective-permute-start.5 = (f32[128]{0:T(128)S(1)}, f32[128]{0:T(128)S(1)}, u32[]{:S(2)}, u32[]{:S(2)}) collective-permute-start(f32[128]{0:T(128)S(1)} %get-tuple-element.134), channel_id=1, source_target_pairs={{0,24},{4,28},{8,0},{12,4},{16,8},{20,12},{24,16},{28,20},{1,25},{... | collective-permute-start | bytes 1544 | tf_op jit(solution)/shard_map/ppermute | solution.py:11
  166.4 9.6 %collective-permute-start.6 = (f32[128]{0:T(128)S(1)}, f32[128]{0:T(128)S(1)}, u32[]{:S(2)}, u32[]{:S(2)}) collective-permute-start(f32[128]{0:T(128)S(1)} %get-tuple-element.133), channel_id=1, source_target_pairs={{0,4},{4,8},{8,12},{12,16},{16,20},{20,24},{24,28},{28,0},{1,5},{5... | collective-permute-start | bytes 1544 | tf_op jit(solution)/shard_map/ppermute | solution.py:11
  167.9 8.1 %collective-permute-start.7 = (f32[128]{0:T(128)S(1)}, f32[128]{0:T(128)S(1)}, u32[]{:S(2)}, u32[]{:S(2)}) collective-permute-start(f32[128]{0:T(128)S(1)} %get-tuple-element.132), channel_id=1, source_target_pairs={{0,8},{4,12},{8,16},{12,20},{16,24},{20,28},{24,0},{28,4},{1,9},{5... | collective-permute-start | bytes 1544 | tf_op jit(solution)/shard_map/ppermute | solution.py:11
  176.0 0.6 copy-start.1
where the time goes:
time: 183 us; the launch traced here: 181 us
  matrix products  102 us (56%)
  other arithmetic  43.4 us (24%)
  starting transfers between devices  12.3 us (7%)
  blocking collectives  11.5 us (6%)
  local copies, waits for them, and re-layouts  9.11 us (5%)
  loops' own time  1.96 us (1%)
    dot_general x16, matrix products, tile_terms(): jnp.einsum('kfw,w->kf', onehot_far, remote_window, precision=lax.Precisio...  27.1 us
    dot_general x16, matrix products, tile_terms(): jnp.einsum('kfw,w->kf', onehot_near, window, precision=lax.Precision.HIGH...  27 us
    dot_general x16, matrix products, tile_terms(): jnp.einsum('kfw,kf->w', onehot_far, terms, precision=lax.Precision.HIGHEST)  23.9 us
    dot_general x16, matrix products, tile_terms(): jnp.einsum('kfw,kf->w', onehot_near, terms, precision=lax.Precision.HIGHEST)  23.6 us
    select_n x16, other arithmetic, tile_terms(): weight = jnp.where(live_mask, area_tile, 0.0)  22.5 us
    sub x16, other arithmetic, tile_terms(): corner_tile[:, :, None] - remote_start == remote_pos  12.8 us
    ppermute x8, starting transfers between devices, from_behind(): lax.ppermute(x, axis, [(i, (i + by) % length) for i in range(length)])  12.3 us
    unnamed x1, blocking collectives  6.48 us
  transfers between devices with their start and end apart: 8, of which 0 were waited for; matrix products, arithmetic and copies ran while one was open for 3% of the time, Pallas kernels for 0%

commit v1 on v0

v1 whole, which is shorter than its diff:
```python
import jax
import jax.numpy as jnp
from jax import lax
from jax.experimental import pallas as pl
from jax.experimental.pallas import tpu as pltpu
from jax.sharding import PartitionSpec as P

LANES = 128
HALF = 64
VMEM = pl.BlockSpec(memory_space=pltpu.VMEM)
SMEM = pl.BlockSpec(memory_space=pltpu.SMEM)


def shift(x, axis, by):
    n = lax.axis_size(axis)
    return lax.ppermute(x, axis, [(i, (i + by) % n) for i in range(n)])


def swap(x, axis, bit):
    n = lax.axis_size(axis)
    return lax.ppermute(x, axis, [(i, i ^ bit) for i in range(n)])


def iota(shape, dim, dtype=jnp.int32):
    return lax.broadcasted_iota(jnp.int32, shape, dim).astype(dtype)


def lane_gather(table, lanes):
    return jnp.take_along_axis(table, lanes, axis=1, mode="promise_in_bounds")


def send_kernel(rows, heat_ref, sub_ref, pat_ref, out_ref):
    blocks = rows // 8
    sub_iota = iota((8, LANES), 0)
    for j in range(5):
        index = sub_ref[0:1, :] if j == 0 else pat_ref[j - 1 : j, :]
        index = jnp.broadcast_to(index, (8, LANES))
        lane = index & (LANES - 1)
        row = index >> 7
        total = jnp.zeros((8, LANES), jnp.float32)
        for a in range(blocks):
            got = lane_gather(heat_ref[8 * a : 8 * a + 8, :], lane)
            total = jnp.where(row == sub_iota + 8 * a, got, total)
        total = jnp.where((row & 7) == sub_iota, total, 0.0)
        out_ref[j : j + 1, :] = jnp.sum(total, axis=0, keepdims=True)


def faces_kernel(
    owned,
    tiles,
    blocks,
    live_ref,
    heat_ref,
    remote_ref,
    corner_ref,
    basis_ref,
    area_ref,
    own_out,
    remote_out,
    win,
    lane_s,
    half_s,
    hi_s,
    lo_s,
    sums_s,
):
    rows = owned // LANES
    live = live_ref[0]
    lane_iota = iota((8, LANES), 1)
    sub_iota = iota((8, LANES), 0)
    zero = jnp.zeros((8, LANES), jnp.float32)
    win[0:8, :] = zero
    win[2 * rows : 2 * rows + 8, :] = zero
    for a in range(rows // 8):
        here = heat_ref[8 * a : 8 * a + 8, :]
        if a + 1 < rows // 8:
            after = heat_ref[8 * a + 1 : 8 * a + 9, :]
        else:
            after = jnp.concatenate([heat_ref[8 * a + 1 : 8 * a + 8, :], zero[0:1]], axis=0)
        both = jnp.where(lane_iota < HALF, after, here)
        win[pl.ds(16 * a + 2, 8, stride=2), :] = here
        win[pl.ds(16 * a + 3, 8, stride=2), :] = pltpu.roll(both, HALF, 1)
    first = pltpu.roll(jnp.broadcast_to(heat_ref[0:1, :], (8, LANES)), HALF, 1)
    win[1:2, :] = jnp.where(lane_iota < HALF, 0.0, first)[0:1]
    remote_rows = [
        jnp.concatenate([remote_ref[2 * (t % blocks) + i : 2 * (t % blocks) + i + 1, :] for t in range(8)], axis=0)
        for i in range(2)
    ]
    half_iota = iota((HALF, LANES), 0, jnp.float32).astype(jnp.bfloat16)
    one = jnp.ones((HALF, LANES), jnp.bfloat16)
    nil = jnp.zeros((HALF, LANES), jnp.bfloat16)
    pad = jnp.zeros((16, LANES), jnp.bfloat16)

    def group(g, remote_sums):
        t0 = pl.multiple_of(8 * g, 8)
        tile = t0 + sub_iota
        near = [win[pl.ds(t0, 8), :], win[pl.ds(t0 + 2, 8), :]]
        slot = tile * LANES + lane_iota
        near_start = HALF * tile - LANES
        far_start = owned + 2 * LANES * (sub_iota % blocks)
        values, offs = [], []
        for k in range(3):
            pos = corner_ref[k, pl.ds(t0, 8), :]
            far = pos >= owned
            off = pos - jnp.where(far, far_start, near_start)
            lane = off & (LANES - 1)
            upper = off >= LANES
            got_near = jnp.where(upper, lane_gather(near[1], lane), lane_gather(near[0], lane))
            got_far = jnp.where(upper, lane_gather(remote_rows[1], lane), lane_gather(remote_rows[0], lane))
            values.append(jnp.where(far, got_far, got_near))
            offs.append(jnp.where(far, off + 2 * LANES, off))
        basis = [basis_ref[i, pl.ds(t0, 8), :].astype(jnp.float32) for i in range(9)]
        grad = [sum(basis[3 * k + c] * values[k] for k in range(3)) for c in range(3)]
        square = grad[0] * grad[0] + grad[1] * grad[1] + grad[2] * grad[2]
        scale = -area_ref[pl.ds(t0, 8), :] / jnp.maximum(jnp.sqrt(square), 1.0)
        scale = jnp.where(slot < live, scale, 0.0)
        field = [grad[c] * scale for c in range(3)]
        for k in range(3):
            term = sum(basis[3 * k + c] * field[c] for c in range(3))
            hi = term.astype(jnp.bfloat16).astype(jnp.float32)
            hi_s[k] = hi
            lo_s[k] = term - hi
            half_s[k] = offs[k] >> 6
            lane_s[k] = (offs[k] & (HALF - 1)).astype(jnp.float32)
        out = []
        for pair in range(4):
            left, right = [], []
            for t in range(2):
                for k in range(3):
                    at = pl.ds(2 * pair + t, 1)
                    half = jnp.broadcast_to(half_s[k, at, :], (8, LANES))
                    match = half == sub_iota
                    a_hi = jnp.where(match, jnp.broadcast_to(hi_s[k, at, :], (8, LANES)), 0.0)
                    a_lo = jnp.where(match, jnp.broadcast_to(lo_s[k, at, :], (8, LANES)), 0.0)
                    a = jnp.concatenate([a_hi, a_lo], axis=0).astype(jnp.bfloat16)
                    left.append(jnp.concatenate([a, pad] if t == 0 else [pad, a], axis=0))
                    lane = jnp.broadcast_to(lane_s[k, at, :], (HALF, LANES)).astype(jnp.bfloat16)
                    right.append(jnp.where(lane == half_iota, one, nil))
            product = lax.dot_general(
                jnp.concatenate(left, axis=1),
                jnp.concatenate(right, axis=1),
                (((1,), (1,)), ((), ())),
                preferred_element_type=jnp.float32,
            )
            for t in range(2):
                total = product[16 * t : 16 * t + 8] + product[16 * t + 8 : 16 * t + 16]
                sums_s[pl.ds(pl.multiple_of(8 * (t0 + 2 * pair + t), 8), 8), 0:HALF] = total
                out.append(total)
        return tuple(
            acc + sum(out[t] for t in range(8) if t % blocks == b)
            for b, acc in enumerate(remote_sums)
        )

    start = tuple(jnp.zeros((8, HALF), jnp.float32) for _ in range(blocks))
    remote_sums = lax.fori_loop(0, tiles // 8, group, start)
    for b in range(blocks):
        for i in range(2):
            both = jnp.concatenate([remote_sums[b][4 + 2 * i : 5 + 2 * i], remote_sums[b][5 + 2 * i : 6 + 2 * i]], axis=1)
            remote_out[2 * b + i : 2 * b + i + 1, :] = both
    sums_s[8 * tiles : 8 * tiles + 32, :] = jnp.zeros((32, LANES), jnp.float32)
    for a in range(rows // 8):
        parts = []
        for odd in range(2):
            total = jnp.zeros((8, LANES), jnp.float32)
            for i in range(4):
                lowest = 16 * a + odd + 2 - i
                if lowest >= 0:
                    got = sums_s[pl.ds(8 * lowest + i, 8, stride=16), :]
                else:
                    got = sums_s[pl.ds(8 * (lowest + 2) + i, 8, stride=16), :]
                    got = jnp.where(sub_iota == 0, 0.0, pltpu.roll(got, 1, 0))
                total = total + got
            parts.append(total)
        own_out[8 * a : 8 * a + 8, :] = jnp.where(lane_iota < HALF, parts[0], pltpu.roll(parts[1], HALF, 1))


def faces_call(live_faces, heat2, remote, corners, basis, area):
    rows = heat2.shape[0]
    tiles = corners.shape[1] // LANES
    blocks = remote.shape[0] // 2
    return pl.pallas_call(
        lambda *refs: faces_kernel(rows * LANES, tiles, blocks, *refs),
        out_shape=(
            jax.ShapeDtypeStruct((rows, LANES), jnp.float32),
            jax.ShapeDtypeStruct((2 * blocks, LANES), jnp.float32),
        ),
        in_specs=[SMEM] + [VMEM] * 5,
        out_specs=(VMEM, VMEM),
        scratch_shapes=[
            pltpu.VMEM((2 * rows + 8, LANES), jnp.float32),
            pltpu.VMEM((3, 8, LANES), jnp.float32),
            pltpu.VMEM((3, 8, LANES), jnp.int32),
            pltpu.VMEM((3, 8, LANES), jnp.float32),
            pltpu.VMEM((3, 8, LANES), jnp.float32),
            pltpu.VMEM((8 * tiles + 128, LANES), jnp.float32),
        ],
        name="faces",
    )(
        live_faces,
        heat2,
        remote,
        corners.reshape(3, tiles, LANES),
        basis.reshape(9, tiles, LANES),
        area.reshape(tiles, LANES),
    )


def scatter_kernel(rows, own_ref, back_ref, sub_ref, pat_ref, out_ref):
    row_iota = iota((rows, LANES), 0)
    lane_iota = iota((LANES, LANES), 0)
    left, right = [], []
    for j in range(5):
        index = sub_ref[0:1, :] if j == 0 else pat_ref[j - 1 : j, :]
        value = back_ref[j : j + 1, :]
        hi = value.astype(jnp.bfloat16).astype(jnp.float32)
        match = jnp.broadcast_to(index >> 7, (rows, LANES)) == row_iota
        a_hi = jnp.where(match, jnp.broadcast_to(hi, (rows, LANES)), 0.0)
        a_lo = jnp.where(match, jnp.broadcast_to(value - hi, (rows, LANES)), 0.0)
        left.append(jnp.concatenate([a_hi, a_lo], axis=0).astype(jnp.bfloat16))
        spot = jnp.broadcast_to(index & (LANES - 1), (LANES, LANES)) == lane_iota
        right.append(jnp.where(spot, 1.0, 0.0).astype(jnp.bfloat16))
    product = lax.dot_general(
        jnp.concatenate(left, axis=1),
        jnp.concatenate(right, axis=1),
        (((1,), (1,)), ((), ())),
        preferred_element_type=jnp.float32,
    )
    out_ref[...] = own_ref[...] + product[:rows] + product[rows:]


def per_device(heat, basis, area, corners, send_sub, send_pat, live_faces):
    owned = heat.shape[0]
    slots = corners.shape[1]
    tiles = slots // LANES
    rows = owned // LANES
    group = lax.axis_size("sub")
    group_size = send_sub.shape[0]
    block_size = send_pat.shape[1]
    offsets = send_pat.shape[0]
    remote_len = group * group_size + offsets * block_size
    blocks = remote_len // (2 * LANES)
    assert offsets == 4 and block_size == LANES and group_size <= LANES
    assert group & (group - 1) == 0 and 8 % blocks == 0 and remote_len == 2 * LANES * blocks
    odd = lax.axis_index("patch") % 2 == 1
    me = lax.axis_index("sub")
    heat2 = heat.reshape(rows, LANES)
    sub2 = jnp.pad(send_sub, (0, LANES - group_size)).reshape(1, LANES)

    sent = pl.pallas_call(
        lambda *refs: send_kernel(rows, *refs),
        out_shape=jax.ShapeDtypeStruct((5, LANES), jnp.float32),
        in_specs=[VMEM, VMEM, VMEM],
        out_specs=VMEM,
        name="send_gather",
    )(heat2, sub2, send_pat)

    near_first = jnp.where(odd, sent[jnp.array([3, 1])], sent[jnp.array([1, 3])])
    direct = swap(near_first, "patch", 1)
    relay = direct[1:2]
    up = shift(jnp.concatenate([sent[2:3], relay]), "patch", 2)
    down = shift(jnp.concatenate([sent[4:5], relay]), "patch", -2)
    from_below = jnp.where(odd, direct[0], up[1])
    from_above = jnp.where(odd, down[1], direct[0])
    values = sent[0:1, :group_size]
    bit = 1
    while bit < group:
        values = jnp.concatenate([values, swap(values, "sub", bit)], axis=0)
        bit = bit * 2
    order = me ^ jnp.arange(group)
    group_values = values[order].reshape(-1)
    remote = jnp.concatenate([group_values, from_below, up[0], from_above, down[0]]).reshape(2 * blocks, LANES)

    own_sums, remote_sums = faces_call(live_faces, heat2, remote, corners, basis, area)

    flat = remote_sums.reshape(-1)
    patch_sums = flat[group * group_size :].reshape(4, LANES)
    near_first = jnp.where(odd, patch_sums[jnp.array([0, 2])], patch_sums[jnp.array([2, 0])])
    direct = swap(near_first, "patch", 1)
    relay = direct[1:2]
    down = shift(jnp.concatenate([patch_sums[1:2], relay]), "patch", -2)
    up = shift(jnp.concatenate([patch_sums[3:4], relay]), "patch", 2)
    back_above = jnp.where(odd, down[1], direct[0])
    back_below = jnp.where(odd, direct[0], up[1])
    group_sums = flat[: group * group_size].reshape(group, group_size)[order]
    bit = group // 2
    while bit >= 1:
        group_sums = group_sums[:bit] + swap(group_sums[bit:], "sub", bit)
        bit = bit // 2
    group_back = jnp.pad(group_sums, ((0, 0), (0, LANES - group_size)))
    back = jnp.concatenate([group_back, jnp.stack([back_above, down[0], back_below, up[0]])])

    result = pl.pallas_call(
        lambda *refs: scatter_kernel(rows, *refs),
        out_shape=jax.ShapeDtypeStruct((rows, LANES), jnp.float32),
        in_specs=[VMEM] * 4,
        out_specs=VMEM,
        name="scatter_back",
    )(own_sums, back, sub2, send_pat)
    return result.reshape(-1)


def solution(mesh):
    placed = (
        P(("patch", "sub")),
        P(None, ("patch", "sub")),
        P(("patch", "sub")),
        P(None, ("patch", "sub")),
        P(("patch", "sub")),
        P(None, ("patch", "sub")),
        P(("patch", "sub")),
    )
    return jax.shard_map(
        per_device, mesh=mesh, in_specs=placed, out_specs=P(("patch", "sub")), check_vma=False
    )
```

time: 183 us -> 46.6 us (0.25)
  matrix products: 102 us -> 0 us
  other arithmetic: 43.4 us -> 0.12 us
  blocking collectives: 11.5 us -> 0 us
  Pallas kernels: 0 us -> 10.8 us
  waiting for transfers between devices: 0.02 us -> 9.6 us
  local copies, waits for them, and re-layouts: 9.11 us -> 11.6 us
  loops' own time: 1.96 us -> 0 us
    dot_general x64 -> x0, matrix products: 102 us -> none  [the longest x16 27.1 us: tile_terms(): jnp.einsum('kfw,w->kf', onehot_far, remote_window, precision=lax.Precisio...]
    select_n x19 -> x4, other arithmetic: 22.5 us -> 0.02 us  [the longest x1 0.01 us: per_device(): jnp.where(odd, sent[jnp.array([3, 1])], sent[jnp.array([1, 3])])]
    sub x16 -> x0, other arithmetic: 12.8 us -> none  [tile_terms(): corner_tile[:, :, None] - remote_start == remote_pos]
    pallas_call x0 -> x3, Pallas kernels: none -> 10.8 us  [the longest x1 7.65 us: faces_call(): pl.pallas_call(lambda *refs: faces_kernel(rows * LANES, tiles, blocks, *r...]
    ppermute x8 -> x10, waiting for transfers between devices: 0.02 us -> 9.6 us  [the longest x4 6.33 us: shift(): return lax.ppermute(x, axis, [(i, (i + by) % n) for i in range(n)])]
    unnamed x1 -> x0, blocking collectives: 6.48 us -> none
    scatter-add x2 -> x0, other arithmetic: 5.62 us -> none  [the longest x1 4.35 us: per_device(): result = result.at[send_pat.reshape(-1)].add(returned.reshape(-1))]
    all_gather x1 -> x0, blocking collectives: 5.06 us -> none  [per_device(): group_values = lax.all_gather(group_send, 'sub', axis=0, tiled=True)]
  transfers between devices with their start and end apart: 8 -> 10, of which waited for: 0 -> 5; matrix products, arithmetic and copies ran while one was open for 3% -> 7% of each run, Pallas kernels for 0% -> 0%
where the time goes in v1:
time: 46.6 us; the launch traced here: 46.1 us
  starting transfers between devices  13.2 us (28%)
  local copies, waits for them, and re-layouts  11.6 us (25%)
  Pallas kernels  10.8 us (23%)
  waiting for transfers between devices  9.6 us (21%)
  between operations  0.8 us (2%)
    ppermute x4, starting transfers between devices, shift(): return lax.ppermute(x, axis, [(i, (i + by) % n) for i in range(n)])  7.71 us
    pallas_call x1, Pallas kernels, faces_call(): pl.pallas_call(lambda *refs: faces_kernel(rows * LANES, tiles, blocks, *r...  7.65 us
    ppermute x4, waiting for transfers between devices, shift(): return lax.ppermute(x, axis, [(i, (i + by) % n) for i in range(n)])  6.33 us
    ppermute x6, starting transfers between devices, swap(): return lax.ppermute(x, axis, [(i, i ^ bit) for i in range(n)])  5.51 us
    unnamed x16, local copies, waits for them, and re-layouts  4.64 us
    ppermute x6, waiting for transfers between devices, swap(): return lax.ppermute(x, axis, [(i, i ^ bit) for i in range(n)])  3.28 us
    pallas_call x1, Pallas kernels, per_device(): pl.pallas_call(lambda *refs: scatter_kernel(rows, *refs), out_shape=jax.S...  1.61 us
    pallas_call x1, Pallas kernels, per_device(): pl.pallas_call(lambda *refs: send_kernel(rows, *refs), out_shape=jax.Shap...  1.52 us
  transfers between devices with their start and end apart: 10, of which 5 were waited for; matrix products, arithmetic and copies ran while one was open for 7% of the time, Pallas kernels for 0%

profile of v1, /device:TPU:0, one launch (start us, length us, event | category | flops | bytes accessed | tf_op | source)
XLA Modules:
  0.0 46.1 jit_solution(13557024642948116952)
XLA Ops:
  0.0 0.0 copy-start.5
  0.0 0.7 %copy-done.5 = s32[2]{0:T(128)S(1)} copy-done((s32[2]{0:T(128)S(1)}, s32[2]{0:T(128)}, u32[]{:S(2)}) %copy-start.5) | copy-done | bytes 32
  0.7 0.0 copy-start.4
  0.7 0.6 %copy-done.4 = s32[2]{0:T(128)S(1)} copy-done((s32[2]{0:T(128)S(1)}, s32[2]{0:T(128)}, u32[]{:S(2)}) %copy-start.4) | copy-done | bytes 32
  1.3 1.5 %send_gather.1 = f32[5,128]{1,0:T(8,128)} custom-call(f32[64,128]{1,0:T(8,128)} %bitcast.32, s32[1,128]{1,0:T(1,128)} %bitcast.36, s32[4,128]{1,0:T(4,128)} %refs_3_.1), custom_call_target="tpu_custom_call" | custom-call | tf_op jit(solution)/shard_map/send_gather/pallas_call | solution.py:249
  2.8 0.0 copy-start.1
  2.8 1.3 %gather_fusion.1 = f32[2,128]{1,0:T(2,128)S(1)} fusion(f32[5,128]{1,0:T(8,128)} %send_gather.1, s32[1024]{0:T(1024)S(1)} %pad_clamp_fusion.3), kind=kCustom, calls=%fused_computation.1 | custom fusion | bytes 2056 | tf_op jit(solution)/shard_map/gather | solution.py:257
  4.2 0.0 copy-done.1
  4.2 0.6 %gather_fusion.2 = f32[2,128]{1,0:T(2,128)S(1)} fusion(f32[5,128]{1,0:T(8,128)S(1)} %copy-done.1, s32[1024]{0:T(1024)S(1)} %pad_clamp_fusion.2), kind=kCustom, calls=%fused_computation.2 | custom fusion | bytes 2056 | tf_op jit(solution)/shard_map/gather | solution.py:257
  4.7 3.1 %collective-permute-start.2 = (f32[2,128]{1,0:T(2,128)S(1)}, f32[2,128]{1,0:T(2,128)S(1)}, u32[]{:S(2)}, u32[]{:S(2)}) collective-permute-start(f32[2,128]{1,0:T(2,128)S(1)} %broadcast_select_fusion.1), channel_id=1, source_target_pairs={{0,4},{4,0},{8,12},{12,8},{16,20},{20,16},{24,28},{28,24},{1,5},{5... | collective-permute-start | bytes 3080 | tf_op jit(solution)/shard_map/ppermute | solution.py:21
  7.8 0.0 collective-permute-start
  7.8 0.0 copy-start.3
  7.9 0.6 %copy-done.3 = s32[2]{0:T(128)S(1)} copy-done((s32[2]{0:T(128)S(1)}, s32[2]{0:T(128)}, u32[]{:S(2)}) %copy-start.3) | copy-done | bytes 32
  8.5 1.1 %copy.13 = bf16[2,8,128,128]{3,2,1,0:T(8,128)(2,1)S(1)} copy(bf16[2,8,128,128]{3,1,2,0:T(8,128)(2,1)} %bitcast.30) | data formatting | bytes 1048576
  9.6 0.0 copy-start
  9.7 0.7 %slice.111.refs_4_ = bf16[9,128,128]{2,1,0:T(8,128)(2,1)} slice(bf16[16,128,128]{2,1,0:T(8,128)(2,1)S(1)} %bitcast.28), slice={[0:9], [0:128], [0:128]} | slice | bytes 589824 | tf_op jit(solution)/shard_map/reshape | solution.py:203
  10.4 0.3 copy-done
  10.7 0.7 %copy.15 = s32[1,3,128,128]{3,2,1,0:T(8,128)} copy(s32[1,3,128,128]{3,1,2,0:T(4,128)S(1)} %bitcast.31) | data formatting | bytes 393216
  12.0 0.0 collective-permute-done
  12.0 1.6 %collective-permute-start.1 = (f32[2,128]{1,0:T(2,128)S(1)}, f32[2,128]{1,0:T(2,128)S(1)}, u32[]{:S(2)}, u32[]{:S(2)}) collective-permute-start(f32[2,128]{1,0:T(2,128)S(1)} %pad_maximum_fusion.5), channel_id=1, source_target_pairs={{0,2},{1,3},{2,0},{3,1},{4,6},{5,7},{6,4},{7,5},{8,10},{9,11},{10,... | collective-permute-start | bytes 3080 | tf_op jit(solution)/shard_map/ppermute | solution.py:21
  13.6 0.0 collective-permute-done.2
  13.6 1.6 %collective-permute-start.3 = (f32[2,128]{1,0:T(2,128)S(1)}, f32[2,128]{1,0:T(2,128)S(1)}, u32[]{:S(2)}, u32[]{:S(2)}) collective-permute-start(f32[2,128]{1,0:T(2,128)S(1)} %get-tuple-element.23), channel_id=1, source_target_pairs={{0,8},{4,12},{8,16},{12,20},{16,24},{20,28},{24,0},{28,4},{1,9},{5... | collective-permute-start | bytes 3080 | tf_op jit(solution)/shard_map/ppermute | solution.py:16
  15.2 2.2 %collective-permute-start.4 = (f32[2,128]{1,0:T(2,128)S(1)}, f32[2,128]{1,0:T(2,128)S(1)}, u32[]{:S(2)}, u32[]{:S(2)}) collective-permute-start(f32[2,128]{1,0:T(2,128)S(1)} %get-tuple-element.22), channel_id=1, source_target_pairs={{0,24},{4,28},{8,0},{12,4},{16,8},{20,12},{24,16},{28,20},{1,25},{... | collective-permute-start | bytes 3080 | tf_op jit(solution)/shard_map/ppermute | solution.py:16
  17.5 0.0 collective-permute-done.1
  17.5 0.6 %gather_fusion = f32[4,128]{1,0:T(4,128)S(1)} fusion(f32[4,128]{1,0:T(4,128)S(1)} %pad_maximum_fusion, s32[1024]{0:T(1024)S(1)} %pad_clamp_fusion.4), kind=kCustom, calls=%fused_computation | custom fusion | bytes 4112 | tf_op jit(solution)/shard_map/gather | solution.py:270
  18.1 1.0 %collective-permute-done.3 = f32[2,128]{1,0:T(2,128)S(1)} collective-permute-done((f32[2,128]{1,0:T(2,128)S(1)}, f32[2,128]{1,0:T(2,128)S(1)}, u32[]{:S(2)}, u32[]{:S(2)}) %collective-permute-start.3) | collective-permute-done | bytes 1056 | tf_op jit(solution)/shard_map/ppermute | solution.py:16
  19.1 0.0 collective-permute-done.4
  19.1 0.0 copy-start.2
  19.1 0.6 %copy-done.2 = f32[1024]{0:T(1024)} copy-done((f32[1024]{0:T(1024)}, f32[1024]{0:T(1024)S(1)}, u32[]{:S(2)}) %copy-start.2) | copy-done | bytes 4120
  19.7 7.6 %faces.1 = (f32[64,128]{1,0:T(8,128)}, f32[8,128]{1,0:T(8,128)}) custom-call(s32[1]{0:T(128)S(6)} %copy.21.refs_0_, f32[64,128]{1,0:T(8,128)} %bitcast.33, f32[8,128]{1,0:T(8,128)} %bitcast.35, s32[3,128,128]{2,1,0:T(8,128)} %bitcast.29, bf16[9,128,128]{2,1,0:T(8,128)(2,1)} %slice.111.refs_4_, f32[128,128]{1,0:T(8,128)} %bitcast.34), custom_call_target="tpu_custom_call" | custom-call | tf_op jit(solution)/shard_map/faces/pallas_call | solution.py:181
  27.3 0.8 %fusion.4 = (f32[4,128]{1,0:T(4,128)S(1)}, f32[4,128]{1,0:T(4,128)S(1)}) fusion(f32[8,128]{1,0:T(8,128)} %get-tuple-element.8), kind=kLoop, calls=%fused_computation.37 | loop fusion | bytes 8192 | tf_op jit(solution)/shard_map/slice | solution.py:276
  28.1 0.8 %fusion.3 = (f32[1,128]{1,0:T(1,128)S(1)}, f32[1,128]{1,0:T(1,128)S(1)}) fusion(f32[8,128]{1,0:T(8,128)} %get-tuple-element.8), kind=kLoop, calls=%fused_computation.36 | loop fusion | bytes 2048 | tf_op jit(solution)/shard_map/slice | solution.py:281
  28.8 0.6 %gather_fusion.4 = f32[2,128]{1,0:T(2,128)S(1)} fusion(f32[4,128]{1,0:T(4,128)S(1)} %get-tuple-element.11, s32[1024]{0:T(1024)S(1)} %pad_clamp_fusion.1), kind=kCustom, calls=%fused_computation.4 | custom fusion | bytes 2056 | tf_op jit(solution)/shard_map/gather | solution.py:277
  29.4 0.6 %gather_fusion.5 = f32[2,128]{1,0:T(2,128)S(1)} fusion(f32[4,128]{1,0:T(4,128)S(1)} %get-tuple-element.11, s32[1024]{0:T(1024)S(1)} %pad_clamp_fusion), kind=kCustom, calls=%fused_computation.5 | custom fusion | bytes 2056 | tf_op jit(solution)/shard_map/gather | solution.py:277
  29.9 0.6 %gather_fusion.3 = f32[4,128]{1,0:T(4,128)S(1)} fusion(f32[4,128]{1,0:T(4,128)S(1)} %get-tuple-element.12, s32[1024]{0:T(1024)S(1)} %pad_clamp_fusion.4), kind=kCustom, calls=%fused_computation.3 | custom fusion | bytes 4112 | tf_op jit(solution)/shard_map/gather | solution.py:284
  30.5 0.6 %collective-permute-start.5 = (f32[2,128]{1,0:T(2,128)S(1)}, f32[2,128]{1,0:T(2,128)S(1)}, u32[]{:S(2)}, u32[]{:S(2)}) collective-permute-start(f32[2,128]{1,0:T(2,128)S(1)} %slice.87), channel_id=1, source_target_pairs={{0,2},{1,3},{2,0},{3,1},{4,6},{5,7},{6,4},{7,5},{8,10},{9,11},{10,... | collective-permute-start | bytes 3080 | tf_op jit(solution)/shard_map/ppermute | solution.py:21
  31.1 0.3 collective-permute-start.7
  31.4 2.7 %collective-permute-done.5 = f32[2,128]{1,0:T(2,128)S(1)} collective-permute-done((f32[2,128]{1,0:T(2,128)S(1)}, f32[2,128]{1,0:T(2,128)S(1)}, u32[]{:S(2)}, u32[]{:S(2)}) %collective-permute-start.5) | collective-permute-done | bytes 1056 | tf_op jit(solution)/shard_map/ppermute | solution.py:21
  34.2 0.0 collective-permute-start.6
  34.2 0.5 %collective-permute-done.7 = f32[2,128]{1,0:T(2,128)S(1)} collective-permute-done((f32[2,128]{1,0:T(2,128)S(1)}, f32[2,128]{1,0:T(2,128)S(1)}, u32[]{:S(2)}, u32[]{:S(2)}) %collective-permute-start.7) | collective-permute-done | bytes 1056 | tf_op jit(solution)/shard_map/ppermute | solution.py:21
  34.7 3.8 %collective-permute-start.8 = (f32[2,128]{1,0:T(2,128)S(1)}, f32[2,128]{1,0:T(2,128)S(1)}, u32[]{:S(2)}, u32[]{:S(2)}) collective-permute-start(f32[2,128]{1,0:T(2,128)S(1)} %get-tuple-element.21), channel_id=1, source_target_pairs={{0,24},{4,28},{8,0},{12,4},{16,8},{20,12},{24,16},{28,20},{1,25},{... | collective-permute-start | bytes 3080 | tf_op jit(solution)/shard_map/ppermute | solution.py:16
  38.5 0.0 collective-permute-start.9
  38.6 0.0 collective-permute-done.6
  38.6 1.3 %collective-permute-done.8 = f32[2,128]{1,0:T(2,128)S(1)} collective-permute-done((f32[2,128]{1,0:T(2,128)S(1)}, f32[2,128]{1,0:T(2,128)S(1)}, u32[]{:S(2)}, u32[]{:S(2)}) %collective-permute-start.8) | collective-permute-done | bytes 1056 | tf_op jit(solution)/shard_map/ppermute | solution.py:16
  39.8 4.1 %collective-permute-done.9 = f32[2,128]{1,0:T(2,128)S(1)} collective-permute-done((f32[2,128]{1,0:T(2,128)S(1)}, f32[2,128]{1,0:T(2,128)S(1)}, u32[]{:S(2)}, u32[]{:S(2)}) %collective-permute-start.9) | collective-permute-done | bytes 1056 | tf_op jit(solution)/shard_map/ppermute | solution.py:16
  43.9 0.6 %concatenate.32.refs_1_ = f32[5,128]{1,0:T(8,128)} concatenate(f32[1,128]{1,0:T(1,128)S(1)} %slice_add_fusion.1, f32[1,128]{1,0:T(1,128)S(1)} %get-tuple-element.18, f32[1,128]{1,0:T(1,128)S(1)} %get-tuple-element.19, f32[1,128]{1,0:T(1,128)S(1)} %get-tuple-element.17, f32[1,128]{1,0:T(1,128)S(1)} %get-tuple-element.16), dimensions={0} | concatenate | bytes 5120 | tf_op jit(solution)/shard_map/concatenate | solution.py:290
  44.5 1.6 %scatter_back.1 = f32[64,128]{1,0:T(8,128)} custom-call(f32[64,128]{1,0:T(8,128)} %get-tuple-element.7.refs_0_, f32[5,128]{1,0:T(8,128)} %concatenate.32.refs_1_, s32[1,128]{1,0:T(1,128)} %bitcast.37, s32[4,128]{1,0:T(4,128)} %refs_3_.1), custom_call_target="tpu_custom_call" | custom-call | tf_op jit(solution)/shard_map/scatter_back/pallas_call | solution.py:292
  (27 shorter events, 0.2 us)
Async XLA Ops:
  0.0 0.7 %copy-start.5 = (s32[2]{0:T(128)S(1)}, s32[2]{0:T(128)}, u32[]{:S(2)}) copy-start(s32[2]{0:T(128)} %constant.57) | copy-start | bytes 28
  0.7 0.7 %copy-start.4 = (s32[2]{0:T(128)S(1)}, s32[2]{0:T(128)}, u32[]{:S(2)}) copy-start(s32[2]{0:T(128)} %constant.58) | copy-start | bytes 28
  2.8 1.3 %copy-start.1 = (f32[5,128]{1,0:T(8,128)S(1)}, f32[5,128]{1,0:T(8,128)}, u32[]{:S(2)}) copy-start(f32[5,128]{1,0:T(8,128)} %send_gather.1) | copy-start | bytes 7684
  4.7 8.9 %collective-permute-start.2 = (f32[2,128]{1,0:T(2,128)S(1)}, f32[2,128]{1,0:T(2,128)S(1)}, u32[]{:S(2)}, u32[]{:S(2)}) collective-permute-start(f32[2,128]{1,0:T(2,128)S(1)} %broadcast_select_fusion.1), channel_id=1, source_target_pairs={{0,4},{4,0},{8,12},{12,8},{16,20},{20,16},{24,28},{28,24},{1,5},{5... | collective-permute-start | bytes 3080 | tf_op jit(solution)/shard_map/ppermute | solution.py:21
  7.8 4.2 %collective-permute-start = (f32[1,128]{1,0:T(1,128)S(1)}, f32[1,128]{1,0:T(1,128)S(1)}, u32[]{:S(2)}, u32[]{:S(2)}) collective-permute-start(f32[1,128]{1,0:T(1,128)S(1)} %get-tuple-element.15), channel_id=1, source_target_pairs={{0,1},{1,0},{2,3},{3,2},{4,5},{5,4},{6,7},{7,6},{8,9},{9,8},{10,11... | collective-permute-start | bytes 1544 | tf_op jit(solution)/shard_map/ppermute | solution.py:21
  7.8 0.7 %copy-start.3 = (s32[2]{0:T(128)S(1)}, s32[2]{0:T(128)}, u32[]{:S(2)}) copy-start(s32[2]{0:T(128)} %constant.59) | copy-start | bytes 28
  9.6 1.0 %copy-start = (s32[3,16384]{1,0:T(4,128)S(1)}, s32[3,16384]{1,0:T(4,128)}, u32[]{:S(2)}) copy-start(s32[3,16384]{1,0:T(4,128)} %param.14) | copy-start | bytes 589828
  12.0 5.5 %collective-permute-start.1 = (f32[2,128]{1,0:T(2,128)S(1)}, f32[2,128]{1,0:T(2,128)S(1)}, u32[]{:S(2)}, u32[]{:S(2)}) collective-permute-start(f32[2,128]{1,0:T(2,128)S(1)} %pad_maximum_fusion.5), channel_id=1, source_target_pairs={{0,2},{1,3},{2,0},{3,1},{4,6},{5,7},{6,4},{7,5},{8,10},{9,11},{10,... | collective-permute-start | bytes 3080 | tf_op jit(solution)/shard_map/ppermute | solution.py:21
  13.6 5.4 %collective-permute-start.3 = (f32[2,128]{1,0:T(2,128)S(1)}, f32[2,128]{1,0:T(2,128)S(1)}, u32[]{:S(2)}, u32[]{:S(2)}) collective-permute-start(f32[2,128]{1,0:T(2,128)S(1)} %get-tuple-element.23), channel_id=1, source_target_pairs={{0,8},{4,12},{8,16},{12,20},{16,24},{20,28},{24,0},{28,4},{1,9},{5... | collective-permute-start | bytes 3080 | tf_op jit(solution)/shard_map/ppermute | solution.py:16
  15.2 3.8 %collective-permute-start.4 = (f32[2,128]{1,0:T(2,128)S(1)}, f32[2,128]{1,0:T(2,128)S(1)}, u32[]{:S(2)}, u32[]{:S(2)}) collective-permute-start(f32[2,128]{1,0:T(2,128)S(1)} %get-tuple-element.22), channel_id=1, source_target_pairs={{0,24},{4,28},{8,0},{12,4},{16,8},{20,12},{24,16},{28,20},{1,25},{... | collective-permute-start | bytes 3080 | tf_op jit(solution)/shard_map/ppermute | solution.py:16
  19.1 0.6 %copy-start.2 = (f32[1024]{0:T(1024)}, f32[1024]{0:T(1024)S(1)}, u32[]{:S(2)}) copy-start(f32[1024]{0:T(1024)S(1)} %constant_dynamic-update-slice_fusion) | copy-start | bytes 12292
  30.5 3.6 %collective-permute-start.5 = (f32[2,128]{1,0:T(2,128)S(1)}, f32[2,128]{1,0:T(2,128)S(1)}, u32[]{:S(2)}, u32[]{:S(2)}) collective-permute-start(f32[2,128]{1,0:T(2,128)S(1)} %slice.87), channel_id=1, source_target_pairs={{0,2},{1,3},{2,0},{3,1},{4,6},{5,7},{6,4},{7,5},{8,10},{9,11},{10,... | collective-permute-start | bytes 3080 | tf_op jit(solution)/shard_map/ppermute | solution.py:21
  31.1 3.6 %collective-permute-start.7 = (f32[2,128]{1,0:T(2,128)S(1)}, f32[2,128]{1,0:T(2,128)S(1)}, u32[]{:S(2)}, u32[]{:S(2)}) collective-permute-start(f32[2,128]{1,0:T(2,128)S(1)} %broadcast_select_fusion), channel_id=1, source_target_pairs={{0,4},{4,0},{8,12},{12,8},{16,20},{20,16},{24,28},{28,24},{1,5},{5... | collective-permute-start | bytes 3080 | tf_op jit(solution)/shard_map/ppermute | solution.py:21
  34.2 4.4 %collective-permute-start.6 = (f32[1,128]{1,0:T(1,128)S(1)}, f32[1,128]{1,0:T(1,128)S(1)}, u32[]{:S(2)}, u32[]{:S(2)}) collective-permute-start(f32[1,128]{1,0:T(1,128)S(1)} %slice.89), channel_id=1, source_target_pairs={{0,1},{1,0},{2,3},{3,2},{4,5},{5,4},{6,7},{7,6},{8,9},{9,8},{10,11... | collective-permute-start | bytes 1544 | tf_op jit(solution)/shard_map/ppermute | solution.py:21
  34.7 5.1 %collective-permute-start.8 = (f32[2,128]{1,0:T(2,128)S(1)}, f32[2,128]{1,0:T(2,128)S(1)}, u32[]{:S(2)}, u32[]{:S(2)}) collective-permute-start(f32[2,128]{1,0:T(2,128)S(1)} %get-tuple-element.21), channel_id=1, source_target_pairs={{0,24},{4,28},{8,0},{12,4},{16,8},{20,12},{24,16},{28,20},{1,25},{... | collective-permute-start | bytes 3080 | tf_op jit(solution)/shard_map/ppermute | solution.py:16
  38.5 5.4 %collective-permute-start.9 = (f32[2,128]{1,0:T(2,128)S(1)}, f32[2,128]{1,0:T(2,128)S(1)}, u32[]{:S(2)}, u32[]{:S(2)}) collective-permute-start(f32[2,128]{1,0:T(2,128)S(1)} %get-tuple-element.20), channel_id=1, source_target_pairs={{0,8},{4,12},{8,16},{12,20},{16,24},{20,28},{24,0},{28,4},{1,9},{5... | collective-permute-start | bytes 3080 | tf_op jit(solution)/shard_map/ppermute | solution.py:16

commit v2 on v1

--- a/solution.py
+++ b/solution.py
@@ -29,12 +29,22 @@
     return jnp.take_along_axis(table, lanes, axis=1, mode="promise_in_bounds")
 
 
-def send_kernel(rows, heat_ref, sub_ref, pat_ref, out_ref):
+def read(ref, at):
+    return ref[pl.ds(at, 1), :]
+
+
+def send_kernel(rows, heat_ref, sub_ref, pat_ref, group_ref, near_ref, up_ref, down_ref):
     blocks = rows // 8
     sub_iota = iota((8, LANES), 0)
+    odd = lax.axis_index("patch") & 1
     for j in range(5):
-        index = sub_ref[0:1, :] if j == 0 else pat_ref[j - 1 : j, :]
-        index = jnp.broadcast_to(index, (8, LANES))
+        if j == 0:
+            index = sub_ref[0:1, :]
+        else:
+            index = read(pat_ref, (1, 3, 2 * odd, 2 - 2 * odd)[j - 1])
+        index = jnp.broadcast_to(index, (8, index.shape[1]))
+        if index.shape[1] < LANES:
+            index = jnp.concatenate([index] * (LANES // index.shape[1]), axis=1)
         lane = index & (LANES - 1)
         row = index >> 7
         total = jnp.zeros((8, LANES), jnp.float32)
@@ -42,28 +52,55 @@
             got = lane_gather(heat_ref[8 * a : 8 * a + 8, :], lane)
             total = jnp.where(row == sub_iota + 8 * a, got, total)
         total = jnp.where((row & 7) == sub_iota, total, 0.0)
-        out_ref[j : j + 1, :] = jnp.sum(total, axis=0, keepdims=True)
+        total = jnp.sum(total, axis=0, keepdims=True)
+        if j == 0:
+            group_ref[...] = total[:, : sub_ref.shape[1]]
+        elif j < 3:
+            (up_ref, down_ref)[j - 1][...] = total
+        else:
+            near_ref[j - 3 : j - 2, :] = total
 
 
 def faces_kernel(
     owned,
     tiles,
     blocks,
+    group,
     live_ref,
     heat_ref,
-    remote_ref,
     corner_ref,
     basis_ref,
     area_ref,
-    own_out,
-    remote_out,
-    win,
-    lane_s,
-    half_s,
-    hi_s,
-    lo_s,
-    sums_s,
+    direct_ref,
+    up_ref,
+    down_ref,
+    *refs,
 ):
+    bits = group.bit_length() - 1
+    group_refs = refs[: bits + 1]
+    own_out, group_keep, *group_outs, near_out, up_out, down_out = refs[bits + 1 : 2 * bits + 6]
+    win, lane_s, half_s, hi_s, lo_s, sums_s, remote_ref, remote_out = refs[2 * bits + 6 :]
+    group_size = group_keep.shape[1]
+    odd = lax.axis_index("patch") & 1
+    me = lax.axis_index("sub")
+    per_row = LANES // group_size
+    for q in range(group // per_row):
+        parts = []
+        for e in range(per_row):
+            from_me = me ^ (q * per_row + e)
+            part = group_refs[0][...]
+            for bit in range(bits):
+                got = read(group_refs[bit + 1], from_me & ((1 << bit) - 1))
+                part = jnp.where(from_me >> bit == 1, got, part)
+            parts.append(part)
+        remote_ref[q : q + 1, :] = parts[0] if per_row == 1 else jnp.concatenate(parts, axis=1)
+    base = group // per_row
+    is_odd = jnp.broadcast_to(odd, (1, LANES)) == 1
+    direct = direct_ref[0:1, :]
+    remote_ref[base : base + 1, :] = jnp.where(is_odd, direct, up_ref[1:2, :])
+    remote_ref[base + 1 : base + 2, :] = up_ref[0:1, :]
+    remote_ref[base + 2 : base + 3, :] = jnp.where(is_odd, down_ref[1:2, :], direct)
+    remote_ref[base + 3 : base + 4, :] = down_ref[0:1, :]
     rows = owned // LANES
     live = live_ref[0]
     lane_iota = iota((8, LANES), 1)
@@ -91,7 +128,7 @@
     nil = jnp.zeros((HALF, LANES), jnp.bfloat16)
     pad = jnp.zeros((16, LANES), jnp.bfloat16)
 
-    def group(g, remote_sums):
+    def eight_tiles(g, remote_sums):
         t0 = pl.multiple_of(8 * g, 8)
         tile = t0 + sub_iota
         near = [win[pl.ds(t0, 8), :], win[pl.ds(t0 + 2, 8), :]]
@@ -152,11 +189,27 @@
         )
 
     start = tuple(jnp.zeros((8, HALF), jnp.float32) for _ in range(blocks))
-    remote_sums = lax.fori_loop(0, tiles // 8, group, start)
+    remote_sums = lax.fori_loop(0, tiles // 8, eight_tiles, start)
     for b in range(blocks):
         for i in range(2):
             both = jnp.concatenate([remote_sums[b][4 + 2 * i : 5 + 2 * i], remote_sums[b][5 + 2 * i : 6 + 2 * i]], axis=1)
             remote_out[2 * b + i : 2 * b + i + 1, :] = both
+    up_out[...] = remote_out[base + 3 : base + 4, :]
+    down_out[...] = remote_out[base + 1 : base + 2, :]
+    near_out[0:1, :] = read(remote_out, base + 2 - 2 * odd)
+    near_out[1:2, :] = read(remote_out, base + 2 * odd)
+    for i in range(group):
+        owner = me ^ i
+        if per_row == 1:
+            row = read(remote_out, owner)
+        else:
+            row = read(remote_out, owner // per_row)
+            row = pltpu.roll(jnp.broadcast_to(row, (8, LANES)), (LANES - (owner % per_row) * group_size) % LANES, 1)[0:1, :group_size]
+        if i == 0:
+            group_keep[...] = row
+        else:
+            bit = i.bit_length() - 1
+            group_outs[bit][i - (1 << bit) : i - (1 << bit) + 1, :] = row
     sums_s[8 * tiles : 8 * tiles + 32, :] = jnp.zeros((32, LANES), jnp.float32)
     for a in range(rows // 8):
         parts = []
@@ -174,128 +227,154 @@
         own_out[8 * a : 8 * a + 8, :] = jnp.where(lane_iota < HALF, parts[0], pltpu.roll(parts[1], HALF, 1))
 
 
-def faces_call(live_faces, heat2, remote, corners, basis, area):
+def faces_call(live_faces, heat2, corners, basis, area, group, group_size, received):
     rows = heat2.shape[0]
     tiles = corners.shape[1] // LANES
-    blocks = remote.shape[0] // 2
+    bits = group.bit_length() - 1
+    blocks = (group * group_size + 4 * LANES) // (2 * LANES)
+    f32 = jnp.float32
+    group_rows = [1] + [1 << bit for bit in range(bits)]
     return pl.pallas_call(
-        lambda *refs: faces_kernel(rows * LANES, tiles, blocks, *refs),
+        lambda *refs: faces_kernel(rows * LANES, tiles, blocks, group, *refs),
         out_shape=(
-            jax.ShapeDtypeStruct((rows, LANES), jnp.float32),
-            jax.ShapeDtypeStruct((2 * blocks, LANES), jnp.float32),
+            jax.ShapeDtypeStruct((rows, LANES), f32),
+            *[jax.ShapeDtypeStruct((n, group_size), f32) for n in group_rows],
+            jax.ShapeDtypeStruct((2, LANES), f32),
+            jax.ShapeDtypeStruct((1, LANES), f32),
+            jax.ShapeDtypeStruct((1, LANES), f32),
         ),
-        in_specs=[SMEM] + [VMEM] * 5,
-        out_specs=(VMEM, VMEM),
+        in_specs=[SMEM] + [VMEM] * (4 + len(received)),
+        out_specs=(VMEM,) * (bits + 5),
         scratch_shapes=[
-            pltpu.VMEM((2 * rows + 8, LANES), jnp.float32),
-            pltpu.VMEM((3, 8, LANES), jnp.float32),
+            pltpu.VMEM((2 * rows + 8, LANES), f32),
+            pltpu.VMEM((3, 8, LANES), f32),
             pltpu.VMEM((3, 8, LANES), jnp.int32),
-            pltpu.VMEM((3, 8, LANES), jnp.float32),
-            pltpu.VMEM((3, 8, LANES), jnp.float32),
-            pltpu.VMEM((8 * tiles + 128, LANES), jnp.float32),
+            pltpu.VMEM((3, 8, LANES), f32),
+            pltpu.VMEM((3, 8, LANES), f32),
+            pltpu.VMEM((8 * tiles + 128, LANES), f32),
+            pltpu.VMEM((2 * blocks, LANES), f32),
+            pltpu.VMEM((2 * blocks, LANES), f32),
         ],
+        compiler_params=pltpu.CompilerParams(vmem_limit_bytes=6 * 2**20),
         name="faces",
     )(
         live_faces,
         heat2,
-        remote,
         corners.reshape(3, tiles, LANES),
         basis.reshape(9, tiles, LANES),
         area.reshape(tiles, LANES),
+        *received,
     )
 
 
-def scatter_kernel(rows, own_ref, back_ref, sub_ref, pat_ref, out_ref):
+def scatter_kernel(rows, bits, own_ref, sub_ref, pat_ref, direct_ref, up_ref, down_ref, *refs):
+    out_ref = refs[-1]
     row_iota = iota((rows, LANES), 0)
     lane_iota = iota((LANES, LANES), 0)
+    odd = jnp.broadcast_to(lax.axis_index("patch") & 1, (1, LANES)) == 1
+    direct = direct_ref[0:1, :]
+    group_back = refs[0][...]
+    for i in range(bits):
+        ref = refs[i + 1]
+        for at in range(0, ref.shape[0], 1 << (bits - 1 - i)):
+            group_back = group_back + ref[at : at + 1, :]
+    backs = [
+        group_back,
+        jnp.where(odd, down_ref[1:2, :], direct),
+        down_ref[0:1, :],
+        jnp.where(odd, direct, up_ref[1:2, :]),
+        up_ref[0:1, :],
+    ]
     left, right = [], []
     for j in range(5):
         index = sub_ref[0:1, :] if j == 0 else pat_ref[j - 1 : j, :]
-        value = back_ref[j : j + 1, :]
+        value = backs[j]
+        width = index.shape[1]
         hi = value.astype(jnp.bfloat16).astype(jnp.float32)
-        match = jnp.broadcast_to(index >> 7, (rows, LANES)) == row_iota
-        a_hi = jnp.where(match, jnp.broadcast_to(hi, (rows, LANES)), 0.0)
-        a_lo = jnp.where(match, jnp.broadcast_to(value - hi, (rows, LANES)), 0.0)
+        match = jnp.broadcast_to(index >> 7, (rows, width)) == row_iota[:, :width]
+        a_hi = jnp.where(match, jnp.broadcast_to(hi, (rows, width)), 0.0)
+        a_lo = jnp.where(match, jnp.broadcast_to(value - hi, (rows, width)), 0.0)
         left.append(jnp.concatenate([a_hi, a_lo], axis=0).astype(jnp.bfloat16))
-        spot = jnp.broadcast_to(index & (LANES - 1), (LANES, LANES)) == lane_iota
+        spot = jnp.broadcast_to(index & (LANES - 1), (LANES, width)) == lane_iota[:, :width]
         right.append(jnp.where(spot, 1.0, 0.0).astype(jnp.bfloat16))
-    product = lax.dot_general(
-        jnp.concatenate(left, axis=1),
-        jnp.concatenate(right, axis=1),
-        (((1,), (1,)), ((), ())),
-        preferred_element_type=jnp.float32,
-    )
+    product = 0.0
+    for part in ([0], [1, 2, 3, 4]) if left[0].shape[1] < LANES else ([0, 1, 2, 3, 4],):
+        product = product + lax.dot_general(
+            jnp.concatenate([left[j] for j in part], axis=1),
+            jnp.concatenate([right[j] for j in part], axis=1),
+            (((1,), (1,)), ((), ())),
+            preferred_element_type=jnp.float32,
+        )
     out_ref[...] = own_ref[...] + product[:rows] + product[rows:]
+
+
+def stack(parts):
+    return parts[0] if len(parts) == 1 else jnp.concatenate(parts, axis=0)
 
 
 def per_device(heat, basis, area, corners, send_sub, send_pat, live_faces):
     owned = heat.shape[0]
-    slots = corners.shape[1]
-    tiles = slots // LANES
     rows = owned // LANES
     group = lax.axis_size("sub")
     group_size = send_sub.shape[0]
     block_size = send_pat.shape[1]
     offsets = send_pat.shape[0]
     remote_len = group * group_size + offsets * block_size
-    blocks = remote_len // (2 * LANES)
-    assert offsets == 4 and block_size == LANES and group_size <= LANES
-    assert group & (group - 1) == 0 and 8 % blocks == 0 and remote_len == 2 * LANES * blocks
-    odd = lax.axis_index("patch") % 2 == 1
-    me = lax.axis_index("sub")
+    assert offsets == 4 and block_size == LANES and LANES % group_size == 0
+    assert group & (group - 1) == 0 and remote_len in (512, 1024, 2048)
+    assert lax.axis_size("patch") % 2 == 0
+    bits = group.bit_length() - 1
+    f32 = jnp.float32
     heat2 = heat.reshape(rows, LANES)
-    sub2 = jnp.pad(send_sub, (0, LANES - group_size)).reshape(1, LANES)
-
-    sent = pl.pallas_call(
+    sub2 = send_sub.reshape(1, group_size)
+
+    mine, near, up, down = pl.pallas_call(
         lambda *refs: send_kernel(rows, *refs),
-        out_shape=jax.ShapeDtypeStruct((5, LANES), jnp.float32),
+        out_shape=(
+            jax.ShapeDtypeStruct((1, group_size), f32),
+            jax.ShapeDtypeStruct((2, LANES), f32),
+            jax.ShapeDtypeStruct((1, LANES), f32),
+            jax.ShapeDtypeStruct((1, LANES), f32),
+        ),
         in_specs=[VMEM, VMEM, VMEM],
-        out_specs=VMEM,
+        out_specs=(VMEM,) * 4,
+        compiler_params=pltpu.CompilerParams(vmem_limit_bytes=2 * 2**20),
         name="send_gather",
     )(heat2, sub2, send_pat)
-
-    near_first = jnp.where(odd, sent[jnp.array([3, 1])], sent[jnp.array([1, 3])])
-    direct = swap(near_first, "patch", 1)
+    direct = swap(near, "patch", 1)
     relay = direct[1:2]
-    up = shift(jnp.concatenate([sent[2:3], relay]), "patch", 2)
-    down = shift(jnp.concatenate([sent[4:5], relay]), "patch", -2)
-    from_below = jnp.where(odd, direct[0], up[1])
-    from_above = jnp.where(odd, down[1], direct[0])
-    values = sent[0:1, :group_size]
-    bit = 1
-    while bit < group:
-        values = jnp.concatenate([values, swap(values, "sub", bit)], axis=0)
-        bit = bit * 2
-    order = me ^ jnp.arange(group)
-    group_values = values[order].reshape(-1)
-    remote = jnp.concatenate([group_values, from_below, up[0], from_above, down[0]]).reshape(2 * blocks, LANES)
-
-    own_sums, remote_sums = faces_call(live_faces, heat2, remote, corners, basis, area)
-
-    flat = remote_sums.reshape(-1)
-    patch_sums = flat[group * group_size :].reshape(4, LANES)
-    near_first = jnp.where(odd, patch_sums[jnp.array([0, 2])], patch_sums[jnp.array([2, 0])])
-    direct = swap(near_first, "patch", 1)
+    from_below = shift(jnp.concatenate([up, relay]), "patch", 2)
+    from_above = shift(jnp.concatenate([down, relay]), "patch", -2)
+    held = [mine]
+    for bit in range(bits):
+        held.append(swap(stack(held), "sub", 1 << bit))
+
+    own_sums, keep, *outs, near, up, down = faces_call(
+        live_faces, heat2, corners, basis, area, group, group_size,
+        (direct, from_below, from_above, *held),
+    )
+
+    direct = swap(near, "patch", 1)
     relay = direct[1:2]
-    down = shift(jnp.concatenate([patch_sums[1:2], relay]), "patch", -2)
-    up = shift(jnp.concatenate([patch_sums[3:4], relay]), "patch", 2)
-    back_above = jnp.where(odd, down[1], direct[0])
-    back_below = jnp.where(odd, direct[0], up[1])
-    group_sums = flat[: group * group_size].reshape(group, group_size)[order]
-    bit = group // 2
-    while bit >= 1:
-        group_sums = group_sums[:bit] + swap(group_sums[bit:], "sub", bit)
-        bit = bit // 2
-    group_back = jnp.pad(group_sums, ((0, 0), (0, LANES - group_size)))
-    back = jnp.concatenate([group_back, jnp.stack([back_above, down[0], back_below, up[0]])])
+    from_above = shift(jnp.concatenate([down, relay]), "patch", -2)
+    from_below = shift(jnp.concatenate([up, relay]), "patch", 2)
+    pieces, group_back = [], []
+    for bit in reversed(range(bits)):
+        width = 1 << bit
+        got = swap(stack([outs[bit]] + [p[width : 2 * width] for p in pieces]), "sub", width)
+        group_back.append(got)
+        pieces = [p[:width] for p in pieces] + [
+            got[at : at + width] for at in range(0, got.shape[0], width)
+        ]
 
     result = pl.pallas_call(
-        lambda *refs: scatter_kernel(rows, *refs),
-        out_shape=jax.ShapeDtypeStruct((rows, LANES), jnp.float32),
-        in_specs=[VMEM] * 4,
+        lambda *refs: scatter_kernel(rows, bits, *refs),
+        out_shape=jax.ShapeDtypeStruct((rows, LANES), f32),
+        in_specs=[VMEM] * (7 + bits),
         out_specs=VMEM,
+        compiler_params=pltpu.CompilerParams(vmem_limit_bytes=4 * 2**20),
         name="scatter_back",
-    )(own_sums, back, sub2, send_pat)
+    )(own_sums, sub2, send_pat, direct, from_below, from_above, keep, *group_back)
     return result.reshape(-1)
 
 

time: 46.6 us -> 31.3 us (0.67)
  local copies, waits for them, and re-layouts: 11.6 us -> 3.66 us
  waiting for transfers between devices: 9.6 us -> 3.52 us
  Pallas kernels: 10.8 us -> 6.96 us
  starting transfers between devices: 13.2 us -> 16.1 us
    ppermute x4, waiting for transfers between devices: 6.33 us -> 1.55 us  [shift(): return lax.ppermute(x, axis, [(i, (i + by) % n) for i in range(n)])]
    gather x6 -> x0, local copies, waits for them, and re-layouts: 4.1 us -> none  [the longest x1 1.31 us: per_device(): sent[jnp.array([3, 1])]]
    pallas_call x3, Pallas kernels: 10.8 us -> 6.96 us  [the longest x1 5.97 us: faces_call(): pl.pallas_call(lambda *refs: faces_kernel(rows * LANES, tiles, blocks, gr...]
    ppermute x6, starting transfers between devices: 5.51 us -> 8 us  [swap(): return lax.ppermute(x, axis, [(i, i ^ bit) for i in range(n)])]
    slice x5 -> x1, local copies, waits for them, and re-layouts: 1.52 us -> 0.01 us  [per_device(): p[width:2 * width]]
    ppermute x6, waiting for transfers between devices: 3.28 us -> 1.97 us  [swap(): return lax.ppermute(x, axis, [(i, i ^ bit) for i in range(n)])]
    unnamed x16 -> x14, local copies, waits for them, and re-layouts: 4.64 us -> 3.63 us
    reshape x1, local copies, waits for them, and re-layouts: 0.74 us -> 0.02 us  [faces_call(): basis.reshape(9, tiles, LANES)]
  transfers between devices with their start and end apart: 10 -> 10, of which waited for: 5 -> 3; matrix products, arithmetic and copies ran while one was open for 7% -> 4% of each run, Pallas kernels for 0% -> 0%
where the time goes in v2:
time: 31.3 us; the launch traced here: 31 us
  starting transfers between devices  16.1 us (51%)
  Pallas kernels  6.96 us (22%)
  local copies, waits for them, and re-layouts  3.66 us (12%)
  waiting for transfers between devices  3.52 us (11%)
  between operations  0.78 us (2%)
    ppermute x4, starting transfers between devices, shift(): return lax.ppermute(x, axis, [(i, (i + by) % n) for i in range(n)])  8.07 us
    ppermute x6, starting transfers between devices, swap(): return lax.ppermute(x, axis, [(i, i ^ bit) for i in range(n)])  8 us
    pallas_call x1, Pallas kernels, faces_call(): pl.pallas_call(lambda *refs: faces_kernel(rows * LANES, tiles, blocks, gr...  5.97 us
    unnamed x14, local copies, waits for them, and re-layouts  3.63 us
    ppermute x6, waiting for transfers between devices, swap(): return lax.ppermute(x, axis, [(i, i ^ bit) for i in range(n)])  1.97 us
    ppermute x4, waiting for transfers between devices, shift(): return lax.ppermute(x, axis, [(i, (i + by) % n) for i in range(n)])  1.55 us
    pallas_call x1, Pallas kernels, per_device(): pl.pallas_call(lambda *refs: scatter_kernel(rows, bits, *refs), out_shape...  0.84 us
  transfers between devices with their start and end apart: 10, of which 3 were waited for; matrix products, arithmetic and copies ran while one was open for 4% of the time, Pallas kernels for 0%

profile of v2, /device:TPU:0, one launch (start us, length us, event | category | flops | bytes accessed | tf_op | source)
XLA Modules:
  0.0 31.0 jit_solution(13661270388281640443)
XLA Ops:
  0.0 0.0 copy-start.3
  0.0 0.0 copy-start.4
  0.0 0.7 %copy-done.3 = s32[4,128]{1,0:T(4,128)S(1)} copy-done((s32[4,128]{1,0:T(4,128)S(1)}, s32[4,128]{1,0:T(4,128)}, u32[]{:S(2)}) %copy-start.3) | copy-done | bytes 2072
  0.7 0.0 copy-done.4
  0.7 0.0 copy-start
  0.7 0.8 %copy-done = f32[8192]{0:T(1024)S(1)} copy-done((f32[8192]{0:T(1024)S(1)}, f32[8192]{0:T(1024)}, u32[]{:S(2)}) %copy-start) | copy-done | bytes 32792
  1.4 0.1 send_gather.1
  1.6 0.6 %collective-permute-start.3 = (f32[1,128]{1,0:T(1,128)S(1)}, f32[1,128]{1,0:T(1,128)S(1)}, u32[]{:S(2)}, u32[]{:S(2)}) collective-permute-start(f32[1,128]{1,0:T(1,128)S(1)} %get-tuple-element.19.refs_8_), channel_id=1, source_target_pairs={{0,1},{1,0},{2,3},{3,2},{4,5},{5,4},{6,7},{7,6},{8,9},{9,8},{10,11... | collective-permute-start | bytes 1544 | tf_op jit(solution)/shard_map/ppermute | solution.py:21
  2.2 2.6 %collective-permute-start = (f32[2,128]{1,0:T(2,128)S(1)}, f32[2,128]{1,0:T(2,128)S(1)}, u32[]{:S(2)}, u32[]{:S(2)}) collective-permute-start(f32[2,128]{1,0:T(2,128)S(1)} %get-tuple-element.16), channel_id=1, source_target_pairs={{0,4},{4,0},{8,12},{12,8},{16,20},{20,16},{24,28},{28,24},{1,5},{5... | collective-permute-start | bytes 3080 | tf_op jit(solution)/shard_map/ppermute | solution.py:21
  4.7 0.0 collective-permute-done.3.refs_9_
  4.8 1.6 %collective-permute-start.4 = (f32[2,128]{1,0:T(2,128)S(1)}, f32[2,128]{1,0:T(2,128)S(1)}, u32[]{:S(2)}, u32[]{:S(2)}) collective-permute-start(f32[2,128]{1,0:T(2,128)S(1)} %pad_maximum_fusion.4), channel_id=1, source_target_pairs={{0,2},{1,3},{2,0},{3,1},{4,6},{5,7},{6,4},{7,5},{8,10},{9,11},{10,... | collective-permute-start | bytes 3080 | tf_op jit(solution)/shard_map/ppermute | solution.py:21
  6.3 0.0 collective-permute-done.refs_5_
  6.3 2.1 %collective-permute-start.1 = (f32[2,128]{1,0:T(2,128)S(1)}, f32[2,128]{1,0:T(2,128)S(1)}, u32[]{:S(2)}, u32[]{:S(2)}) collective-permute-start(f32[2,128]{1,0:T(2,128)S(1)} %get-tuple-element.30), channel_id=1, source_target_pairs={{0,8},{4,12},{8,16},{12,20},{16,24},{20,28},{24,0},{28,4},{1,9},{5... | collective-permute-start | bytes 3080 | tf_op jit(solution)/shard_map/ppermute | solution.py:16
  8.4 2.1 %collective-permute-start.2 = (f32[2,128]{1,0:T(2,128)S(1)}, f32[2,128]{1,0:T(2,128)S(1)}, u32[]{:S(2)}, u32[]{:S(2)}) collective-permute-start(f32[2,128]{1,0:T(2,128)S(1)} %get-tuple-element.29), channel_id=1, source_target_pairs={{0,24},{4,28},{8,0},{12,4},{16,8},{20,12},{24,16},{28,20},{1,25},{... | collective-permute-start | bytes 3080 | tf_op jit(solution)/shard_map/ppermute | solution.py:16
  10.5 1.1 %copy.9 = bf16[2,8,128,128]{3,2,1,0:T(8,128)(2,1)S(1)} copy(bf16[2,8,128,128]{3,1,2,0:T(8,128)(2,1)} %bitcast.18) | data formatting | bytes 1048576
  11.7 0.0 copy-start.5
  11.7 0.9 %copy-done.5 = s32[3,16384]{1,0:T(4,128)S(1)} copy-done((s32[3,16384]{1,0:T(4,128)S(1)}, s32[3,16384]{1,0:T(4,128)}, u32[]{:S(2)}) %copy-start.5) | copy-done | bytes 196632
  12.6 0.0 copy-start.1
  12.6 0.0 copy-start.2
  13.3 0.0 collective-permute-done.4.refs_10_
  13.3 0.0 collective-permute-done.1.refs_6_
  13.3 0.0 collective-permute-done.2.refs_7_
  13.4 0.0 copy-done.1
  13.4 0.1 copy-done.2
  13.5 6.0 %faces.1 = (f32[64,128]{1,0:T(8,128)S(1)}, f32[1,128]{1,0:T(1,128)S(1)}, f32[1,128]{1,0:T(1,128)S(1)}, f32[2,128]{1,0:T(2,128)S(1)}, f32[2,128]{1,0:T(2,128)S(1)...) custom-call(s32[1]{0:T(128)S(6)} %copy.12.refs_0_, f32[64,128]{1,0:T(8,128)S(1)} %bitcast.13, s32[3,128,128]{2,1,0:T(8,128)S(1)} %bitcast.11, ...), custom_call_target="tpu_custom_call" | custom-call | tf_op jit(solution)/shard_map/faces/pallas_call | solution.py:237
  19.5 1.7 %collective-permute-start.8 = (f32[2,128]{1,0:T(2,128)S(1)}, f32[2,128]{1,0:T(2,128)S(1)}, u32[]{:S(2)}, u32[]{:S(2)}) collective-permute-start(f32[2,128]{1,0:T(2,128)S(1)} %get-tuple-element.25), channel_id=1, source_target_pairs={{0,2},{1,3},{2,0},{3,1},{4,6},{5,7},{6,4},{7,5},{8,10},{9,11},{10,... | collective-permute-start | bytes 3080 | tf_op jit(solution)/shard_map/ppermute | solution.py:21
  21.2 1.5 %collective-permute-start.5 = (f32[2,128]{1,0:T(2,128)S(1)}, f32[2,128]{1,0:T(2,128)S(1)}, u32[]{:S(2)}, u32[]{:S(2)}) collective-permute-start(f32[2,128]{1,0:T(2,128)S(1)} %get-tuple-element.21), channel_id=1, source_target_pairs={{0,4},{4,0},{8,12},{12,8},{16,20},{20,16},{24,28},{28,24},{1,5},{5... | collective-permute-start | bytes 3080 | tf_op jit(solution)/shard_map/ppermute | solution.py:21
  22.7 0.4 %collective-permute-done.8.refs_7_ = f32[2,128]{1,0:T(2,128)S(1)} collective-permute-done((f32[2,128]{1,0:T(2,128)S(1)}, f32[2,128]{1,0:T(2,128)S(1)}, u32[]{:S(2)}, u32[]{:S(2)}) %collective-permute-start.8) | collective-permute-done | bytes 1056 | tf_op jit(solution)/shard_map/ppermute | solution.py:21
  23.1 0.1 collective-permute-start.9
  23.2 1.6 %collective-permute-done.5.refs_3_ = f32[2,128]{1,0:T(2,128)S(1)} collective-permute-done((f32[2,128]{1,0:T(2,128)S(1)}, f32[2,128]{1,0:T(2,128)S(1)}, u32[]{:S(2)}, u32[]{:S(2)}) %collective-permute-start.5) | collective-permute-done | bytes 1056 | tf_op jit(solution)/shard_map/ppermute | solution.py:21
  24.8 0.1 collective-permute-start.6
  24.8 3.8 %collective-permute-start.7 = (f32[2,128]{1,0:T(2,128)S(1)}, f32[2,128]{1,0:T(2,128)S(1)}, u32[]{:S(2)}, u32[]{:S(2)}) collective-permute-start(f32[2,128]{1,0:T(2,128)S(1)} %get-tuple-element.27), channel_id=1, source_target_pairs={{0,24},{4,28},{8,0},{12,4},{16,8},{20,12},{24,16},{28,20},{1,25},{... | collective-permute-start | bytes 3080 | tf_op jit(solution)/shard_map/ppermute | solution.py:16
  28.6 0.0 collective-permute-done.9.refs_8_
  28.6 1.5 %collective-permute-done.6.refs_4_ = f32[2,128]{1,0:T(2,128)S(1)} collective-permute-done((f32[2,128]{1,0:T(2,128)S(1)}, f32[2,128]{1,0:T(2,128)S(1)}, u32[]{:S(2)}, u32[]{:S(2)}) %collective-permute-start.6) | collective-permute-done | bytes 1056 | tf_op jit(solution)/shard_map/ppermute | solution.py:16
  30.2 0.0 collective-permute-done.7.refs_5_
  30.2 0.8 %scatter_back.1 = f32[64,128]{1,0:T(8,128)} custom-call(f32[64,128]{1,0:T(8,128)S(1)} %get-tuple-element.20.refs_0_, s32[1,128]{1,0:T(1,128)S(1)} %bitcast.16, s32[4,128]{1,0:T(4,128)S(1)} %copy-done.3, f32[2,128]{1,0:T(2,128)S(1)} %collective-permute-done.5.refs_3_, f32[2,128]{1,0:T(2,128)S(1)} %collective-permute-done.6.refs_4_, ...), custom_call_target="tpu_custom_call" | custom-call | tf_op jit(solution)/shard_map/scatter_back/pallas_call | solution.py:370
  (9 shorter events, 0.1 us)
Async XLA Ops:
  0.0 0.7 %copy-start.3 = (s32[4,128]{1,0:T(4,128)S(1)}, s32[4,128]{1,0:T(4,128)}, u32[]{:S(2)}) copy-start(s32[4,128]{1,0:T(4,128)} %refs_2_.3) | copy-start | bytes 6148
  0.0 0.7 %copy-start.4 = (s32[128]{0:T(128)S(1)}, s32[128]{0:T(128)}, u32[]{:S(2)}) copy-start(s32[128]{0:T(128)} %param.11) | copy-start | bytes 1540
  0.7 0.8 %copy-start = (f32[8192]{0:T(1024)S(1)}, f32[8192]{0:T(1024)}, u32[]{:S(2)}) copy-start(f32[8192]{0:T(1024)} %param.7) | copy-start | bytes 98308
  1.6 3.1 %collective-permute-start.3 = (f32[1,128]{1,0:T(1,128)S(1)}, f32[1,128]{1,0:T(1,128)S(1)}, u32[]{:S(2)}, u32[]{:S(2)}) collective-permute-start(f32[1,128]{1,0:T(1,128)S(1)} %get-tuple-element.19.refs_8_), channel_id=1, source_target_pairs={{0,1},{1,0},{2,3},{3,2},{4,5},{5,4},{6,7},{7,6},{8,9},{9,8},{10,11... | collective-permute-start | bytes 1544 | tf_op jit(solution)/shard_map/ppermute | solution.py:21
  2.2 4.2 %collective-permute-start = (f32[2,128]{1,0:T(2,128)S(1)}, f32[2,128]{1,0:T(2,128)S(1)}, u32[]{:S(2)}, u32[]{:S(2)}) collective-permute-start(f32[2,128]{1,0:T(2,128)S(1)} %get-tuple-element.16), channel_id=1, source_target_pairs={{0,4},{4,0},{8,12},{12,8},{16,20},{20,16},{24,28},{28,24},{1,5},{5... | collective-permute-start | bytes 3080 | tf_op jit(solution)/shard_map/ppermute | solution.py:21
  4.8 8.6 %collective-permute-start.4 = (f32[2,128]{1,0:T(2,128)S(1)}, f32[2,128]{1,0:T(2,128)S(1)}, u32[]{:S(2)}, u32[]{:S(2)}) collective-permute-start(f32[2,128]{1,0:T(2,128)S(1)} %pad_maximum_fusion.4), channel_id=1, source_target_pairs={{0,2},{1,3},{2,0},{3,1},{4,6},{5,7},{6,4},{7,5},{8,10},{9,11},{10,... | collective-permute-start | bytes 3080 | tf_op jit(solution)/shard_map/ppermute | solution.py:21
  6.3 7.0 %collective-permute-start.1 = (f32[2,128]{1,0:T(2,128)S(1)}, f32[2,128]{1,0:T(2,128)S(1)}, u32[]{:S(2)}, u32[]{:S(2)}) collective-permute-start(f32[2,128]{1,0:T(2,128)S(1)} %get-tuple-element.30), channel_id=1, source_target_pairs={{0,8},{4,12},{8,16},{12,20},{16,24},{20,28},{24,0},{28,4},{1,9},{5... | collective-permute-start | bytes 3080 | tf_op jit(solution)/shard_map/ppermute | solution.py:16
  8.4 4.9 %collective-permute-start.2 = (f32[2,128]{1,0:T(2,128)S(1)}, f32[2,128]{1,0:T(2,128)S(1)}, u32[]{:S(2)}, u32[]{:S(2)}) collective-permute-start(f32[2,128]{1,0:T(2,128)S(1)} %get-tuple-element.29), channel_id=1, source_target_pairs={{0,24},{4,28},{8,0},{12,4},{16,8},{20,12},{24,16},{28,20},{1,25},{... | collective-permute-start | bytes 3080 | tf_op jit(solution)/shard_map/ppermute | solution.py:16
  11.7 1.0 %copy-start.5 = (s32[3,16384]{1,0:T(4,128)S(1)}, s32[3,16384]{1,0:T(4,128)}, u32[]{:S(2)}) copy-start(s32[3,16384]{1,0:T(4,128)} %param.10) | copy-start | bytes 589828
  12.6 0.8 %copy-start.1 = (f32[8192]{0:T(1024)S(1)}, f32[8192]{0:T(1024)}, u32[]{:S(2)}) copy-start(f32[8192]{0:T(1024)} %param.7) | copy-start | bytes 98308
  12.6 0.9 %copy-start.2 = (f32[16384]{0:T(1024)S(1)}, f32[16384]{0:T(1024)}, u32[]{:S(2)}) copy-start(f32[16384]{0:T(1024)} %param.9) | copy-start | bytes 196612
  19.5 3.6 %collective-permute-start.8 = (f32[2,128]{1,0:T(2,128)S(1)}, f32[2,128]{1,0:T(2,128)S(1)}, u32[]{:S(2)}, u32[]{:S(2)}) collective-permute-start(f32[2,128]{1,0:T(2,128)S(1)} %get-tuple-element.25), channel_id=1, source_target_pairs={{0,2},{1,3},{2,0},{3,1},{4,6},{5,7},{6,4},{7,5},{8,10},{9,11},{10,... | collective-permute-start | bytes 3080 | tf_op jit(solution)/shard_map/ppermute | solution.py:21
  21.2 3.6 %collective-permute-start.5 = (f32[2,128]{1,0:T(2,128)S(1)}, f32[2,128]{1,0:T(2,128)S(1)}, u32[]{:S(2)}, u32[]{:S(2)}) collective-permute-start(f32[2,128]{1,0:T(2,128)S(1)} %get-tuple-element.21), channel_id=1, source_target_pairs={{0,4},{4,0},{8,12},{12,8},{16,20},{20,16},{24,28},{28,24},{1,5},{5... | collective-permute-start | bytes 3080 | tf_op jit(solution)/shard_map/ppermute | solution.py:21
  23.1 5.5 %collective-permute-start.9 = (f32[2,128]{1,0:T(2,128)S(1)}, f32[2,128]{1,0:T(2,128)S(1)}, u32[]{:S(2)}, u32[]{:S(2)}) collective-permute-start(f32[2,128]{1,0:T(2,128)S(1)} %pad_maximum_fusion.5), channel_id=1, source_target_pairs={{0,1},{1,0},{2,3},{3,2},{4,5},{5,4},{6,7},{7,6},{8,9},{9,8},{10,11... | collective-permute-start | bytes 3080 | tf_op jit(solution)/shard_map/ppermute | solution.py:21
  24.8 5.4 %collective-permute-start.6 = (f32[2,128]{1,0:T(2,128)S(1)}, f32[2,128]{1,0:T(2,128)S(1)}, u32[]{:S(2)}, u32[]{:S(2)}) collective-permute-start(f32[2,128]{1,0:T(2,128)S(1)} %get-tuple-element.28), channel_id=1, source_target_pairs={{0,8},{4,12},{8,16},{12,20},{16,24},{20,28},{24,0},{28,4},{1,9},{5... | collective-permute-start | bytes 3080 | tf_op jit(solution)/shard_map/ppermute | solution.py:16
  24.8 5.4 %collective-permute-start.7 = (f32[2,128]{1,0:T(2,128)S(1)}, f32[2,128]{1,0:T(2,128)S(1)}, u32[]{:S(2)}, u32[]{:S(2)}) collective-permute-start(f32[2,128]{1,0:T(2,128)S(1)} %get-tuple-element.27), channel_id=1, source_target_pairs={{0,24},{4,28},{8,0},{12,4},{16,8},{20,12},{24,16},{28,20},{1,25},{... | collective-permute-start | bytes 3080 | tf_op jit(solution)/shard_map/ppermute | solution.py:16

commit v3 on v2

--- a/solution.py
+++ b/solution.py
@@ -5,9 +5,13 @@
 from jax.experimental.pallas import tpu as pltpu
 from jax.sharding import PartitionSpec as P
 
+
 LANES = 128
 HALF = 64
+UNROLL = (8, 4, 4)
+COST = (1 << 24, 1 << 24)
 VMEM = pl.BlockSpec(memory_space=pltpu.VMEM)
+HBM = pl.BlockSpec(memory_space=pltpu.HBM)
 SMEM = pl.BlockSpec(memory_space=pltpu.SMEM)
 
 
@@ -33,7 +37,17 @@
     return ref[pl.ds(at, 1), :]
 
 
-def send_kernel(rows, heat_ref, sub_ref, pat_ref, group_ref, near_ref, up_ref, down_ref):
+def send_kernel(
+    rows, heat_hbm, sub_hbm, pat_hbm, group_ref, near_ref, up_ref, down_ref, sub_ref, pat_ref, heat_ref, sems
+):
+    copies = [
+        pltpu.make_async_copy(source, target, sems.at[i])
+        for i, (source, target) in enumerate(((heat_hbm, heat_ref), (sub_hbm, sub_ref), (pat_hbm, pat_ref)))
+    ]
+    for copy in copies:
+        copy.start()
+    for copy in copies:
+        copy.wait()
     blocks = rows // 8
     sub_iota = iota((8, LANES), 0)
     odd = lax.axis_index("patch") & 1
@@ -61,28 +75,145 @@
             near_ref[j - 3 : j - 2, :] = total
 
 
-def faces_kernel(
+def prepare_kernel(
     owned,
     tiles,
     blocks,
-    group,
     live_ref,
+    heat_hbm,
+    corner_hbm,
+    basis_hbm,
+    area_hbm,
+    near_out,
+    off_out,
+    half_out,
+    lane_out,
+    basis_out,
+    last_out,
+    weight_out,
     heat_ref,
     corner_ref,
     basis_ref,
-    area_ref,
-    direct_ref,
-    up_ref,
-    down_ref,
-    *refs,
+    win,
+    corner_s,
+    sems,
 ):
+    copies = [
+        pltpu.make_async_copy(source, target, sems.at[i])
+        for i, (source, target) in enumerate(
+            ((corner_hbm, corner_ref), (heat_hbm, heat_ref), (basis_hbm, basis_ref), (area_hbm, weight_out))
+        )
+    ]
+    for copy in copies:
+        copy.start()
+    rows = owned // LANES
+    lane_iota = iota((8, LANES), 1)
+    sub_iota = iota((8, LANES), 0)
+    copies[1].wait()
+    zero = jnp.zeros((8, LANES), jnp.float32)
+    win[0:8, :] = zero
+    win[2 * rows : 2 * rows + 8, :] = zero
+    for a in range(rows // 8):
+        here = heat_ref[8 * a : 8 * a + 8, :]
+        if a + 1 < rows // 8:
+            after = heat_ref[8 * a + 1 : 8 * a + 9, :]
+        else:
+            after = jnp.concatenate([heat_ref[8 * a + 1 : 8 * a + 8, :], zero[0:1]], axis=0)
+        both = jnp.where(lane_iota < HALF, after, here)
+        win[pl.ds(16 * a + 2, 8, stride=2), :] = here
+        win[pl.ds(16 * a + 3, 8, stride=2), :] = pltpu.roll(both, HALF, 1)
+    first = pltpu.roll(jnp.broadcast_to(heat_ref[0:1, :], (8, LANES)), HALF, 1)
+    win[1:2, :] = jnp.where(lane_iota < HALF, 0.0, first)[0:1]
+    copies[0].wait()
+
+    def spread_corners(t, carry):
+        at = pl.ds(pl.multiple_of(LANES * t, LANES), LANES)
+        corner_s[pl.ds(pl.multiple_of(4 * t, 4), 3), :] = corner_ref[:, at]
+        return carry
+
+    lax.fori_loop(0, tiles, spread_corners, 0, unroll=UNROLL[0])
+
+    def near_values(g, carry):
+        t0 = pl.multiple_of(8 * g, 8)
+        tile = t0 + sub_iota
+        near = [win[pl.ds(t0, 8), :], win[pl.ds(t0 + 2, 8), :]]
+        near_start = HALF * tile - LANES
+        far_start = owned + 2 * LANES * (sub_iota % blocks) - 2 * LANES
+        at = pl.ds(t0, 8)
+        for k in range(3):
+            pos = corner_s[pl.ds(4 * t0 + k, 8, stride=4), :]
+            off = pos - jnp.where(pos >= owned, far_start, near_start)
+            lane = off & (LANES - 1)
+            near_out[k, at, :] = jnp.where(
+                off >= LANES, lane_gather(near[1], lane), lane_gather(near[0], lane)
+            )
+            off_out[k, at, :] = off
+            half_out[k, at, :] = off >> 6
+            lane_out[k, at, :] = (off & (HALF - 1)).astype(jnp.float32)
+        return carry
+
+    lax.fori_loop(0, tiles // 8, near_values, 0, unroll=UNROLL[1])
+    copies[2].wait()
+
+    def spread_basis(t, carry):
+        at = pl.ds(pl.multiple_of(LANES * t, LANES), LANES)
+        nine = basis_ref[:, at].astype(jnp.float32)
+        basis_out[pl.ds(pl.multiple_of(8 * t, 8), 8), :] = nine[0:8]
+        last_out[pl.ds(t, 1), :] = nine[8:9]
+        return carry
+
+    lax.fori_loop(0, tiles, spread_basis, 0, unroll=UNROLL[0])
+    copies[3].wait()
+    live = live_ref[0]
+    for t0 in range(0, tiles, 8):
+        slot = (t0 + sub_iota) * LANES + lane_iota
+        weight_out[t0 : t0 + 8, :] = jnp.where(slot < live, -weight_out[t0 : t0 + 8, :], 0.0)
+
+
+def prepare_call(live_faces, heat2, corners, basis, area, blocks):
+    rows = heat2.shape[0]
+    tiles = corners.shape[1] // LANES
+    f32 = jnp.float32
+    per_corner = (3, tiles, LANES)
+    return pl.pallas_call(
+        lambda *refs: prepare_kernel(rows * LANES, tiles, blocks, *refs),
+        out_shape=(
+            jax.ShapeDtypeStruct(per_corner, f32),
+            jax.ShapeDtypeStruct(per_corner, jnp.int32),
+            jax.ShapeDtypeStruct(per_corner, jnp.int32),
+            jax.ShapeDtypeStruct(per_corner, f32),
+            jax.ShapeDtypeStruct((8 * tiles, LANES), f32),
+            jax.ShapeDtypeStruct((tiles, LANES), f32),
+            jax.ShapeDtypeStruct((tiles, LANES), f32),
+        ),
+        in_specs=[SMEM] + [HBM] * 4,
+        out_specs=(VMEM,) * 7,
+        scratch_shapes=[
+            pltpu.VMEM(heat2.shape, f32),
+            pltpu.VMEM(corners.shape, jnp.int32),
+            pltpu.VMEM(basis.shape, basis.dtype),
+            pltpu.VMEM((2 * rows + 8, LANES), f32),
+            pltpu.VMEM((4 * tiles, LANES), jnp.int32),
+            pltpu.SemaphoreType.DMA((4,)),
+        ],
+        cost_estimate=pl.CostEstimate(flops=COST[0], bytes_accessed=1 << 20, transcendentals=0),
+        compiler_params=pltpu.CompilerParams(vmem_limit_bytes=6 * 2**20),
+        name="prepare",
+    )(live_faces, *in_hbm(heat2, corners, basis, area.reshape(tiles, LANES)))
+
+
+def faces_kernel(tiles, blocks, group, *refs):
+    near_ref, off_ref, half_s, lane_s, basis_s, last_s, weight_ref, direct_ref, up_ref, down_ref, *refs = refs
     bits = group.bit_length() - 1
     group_refs = refs[: bits + 1]
     own_out, group_keep, *group_outs, near_out, up_out, down_out = refs[bits + 1 : 2 * bits + 6]
-    win, lane_s, half_s, hi_s, lo_s, sums_s, remote_ref, remote_out = refs[2 * bits + 6 :]
+    hi_s, lo_s, sums_s, remote_ref, remote_out = refs[2 * bits + 6 :]
     group_size = group_keep.shape[1]
     odd = lax.axis_index("patch") & 1
     me = lax.axis_index("sub")
+    rows = own_out.shape[0]
+    lane_iota = iota((8, LANES), 1)
+    sub_iota = iota((8, LANES), 0)
     per_row = LANES // group_size
     for q in range(group // per_row):
         parts = []
@@ -101,24 +232,6 @@
     remote_ref[base + 1 : base + 2, :] = up_ref[0:1, :]
     remote_ref[base + 2 : base + 3, :] = jnp.where(is_odd, down_ref[1:2, :], direct)
     remote_ref[base + 3 : base + 4, :] = down_ref[0:1, :]
-    rows = owned // LANES
-    live = live_ref[0]
-    lane_iota = iota((8, LANES), 1)
-    sub_iota = iota((8, LANES), 0)
-    zero = jnp.zeros((8, LANES), jnp.float32)
-    win[0:8, :] = zero
-    win[2 * rows : 2 * rows + 8, :] = zero
-    for a in range(rows // 8):
-        here = heat_ref[8 * a : 8 * a + 8, :]
-        if a + 1 < rows // 8:
-            after = heat_ref[8 * a + 1 : 8 * a + 9, :]
-        else:
-            after = jnp.concatenate([heat_ref[8 * a + 1 : 8 * a + 8, :], zero[0:1]], axis=0)
-        both = jnp.where(lane_iota < HALF, after, here)
-        win[pl.ds(16 * a + 2, 8, stride=2), :] = here
-        win[pl.ds(16 * a + 3, 8, stride=2), :] = pltpu.roll(both, HALF, 1)
-    first = pltpu.roll(jnp.broadcast_to(heat_ref[0:1, :], (8, LANES)), HALF, 1)
-    win[1:2, :] = jnp.where(lane_iota < HALF, 0.0, first)[0:1]
     remote_rows = [
         jnp.concatenate([remote_ref[2 * (t % blocks) + i : 2 * (t % blocks) + i + 1, :] for t in range(8)], axis=0)
         for i in range(2)
@@ -128,43 +241,39 @@
     nil = jnp.zeros((HALF, LANES), jnp.bfloat16)
     pad = jnp.zeros((16, LANES), jnp.bfloat16)
 
-    def eight_tiles(g, remote_sums):
+    def face_values(g, carry):
         t0 = pl.multiple_of(8 * g, 8)
-        tile = t0 + sub_iota
-        near = [win[pl.ds(t0, 8), :], win[pl.ds(t0 + 2, 8), :]]
-        slot = tile * LANES + lane_iota
-        near_start = HALF * tile - LANES
-        far_start = owned + 2 * LANES * (sub_iota % blocks)
-        values, offs = [], []
+        at = pl.ds(t0, 8)
+        values = []
         for k in range(3):
-            pos = corner_ref[k, pl.ds(t0, 8), :]
-            far = pos >= owned
-            off = pos - jnp.where(far, far_start, near_start)
+            off = off_ref[k, at, :]
             lane = off & (LANES - 1)
-            upper = off >= LANES
-            got_near = jnp.where(upper, lane_gather(near[1], lane), lane_gather(near[0], lane))
-            got_far = jnp.where(upper, lane_gather(remote_rows[1], lane), lane_gather(remote_rows[0], lane))
-            values.append(jnp.where(far, got_far, got_near))
-            offs.append(jnp.where(far, off + 2 * LANES, off))
-        basis = [basis_ref[i, pl.ds(t0, 8), :].astype(jnp.float32) for i in range(9)]
+            far = jnp.where(
+                off >= 3 * LANES, lane_gather(remote_rows[1], lane), lane_gather(remote_rows[0], lane)
+            )
+            values.append(jnp.where(off >= 2 * LANES, far, near_ref[k, at, :]))
+        basis = [basis_s[pl.ds(8 * t0 + i, 8, stride=8), :] for i in range(8)] + [last_s[at, :]]
         grad = [sum(basis[3 * k + c] * values[k] for k in range(3)) for c in range(3)]
         square = grad[0] * grad[0] + grad[1] * grad[1] + grad[2] * grad[2]
-        scale = -area_ref[pl.ds(t0, 8), :] / jnp.maximum(jnp.sqrt(square), 1.0)
-        scale = jnp.where(slot < live, scale, 0.0)
+        scale = weight_ref[at, :] / jnp.maximum(jnp.sqrt(square), 1.0)
         field = [grad[c] * scale for c in range(3)]
         for k in range(3):
             term = sum(basis[3 * k + c] * field[c] for c in range(3))
             hi = term.astype(jnp.bfloat16).astype(jnp.float32)
-            hi_s[k] = hi
-            lo_s[k] = term - hi
-            half_s[k] = offs[k] >> 6
-            lane_s[k] = (offs[k] & (HALF - 1)).astype(jnp.float32)
+            hi_s[k, at, :] = hi
+            lo_s[k, at, :] = term - hi
+        return carry
+
+    lax.fori_loop(0, tiles // 8, face_values, 0, unroll=UNROLL[1])
+
+    def eight_tiles(g, remote_sums):
+        t0 = pl.multiple_of(8 * g, 8)
         out = []
         for pair in range(4):
             left, right = [], []
             for t in range(2):
                 for k in range(3):
-                    at = pl.ds(2 * pair + t, 1)
+                    at = pl.ds(t0 + 2 * pair + t, 1)
                     half = jnp.broadcast_to(half_s[k, at, :], (8, LANES))
                     match = half == sub_iota
                     a_hi = jnp.where(match, jnp.broadcast_to(hi_s[k, at, :], (8, LANES)), 0.0)
@@ -189,7 +298,7 @@
         )
 
     start = tuple(jnp.zeros((8, HALF), jnp.float32) for _ in range(blocks))
-    remote_sums = lax.fori_loop(0, tiles // 8, eight_tiles, start)
+    remote_sums = lax.fori_loop(0, tiles // 8, eight_tiles, start, unroll=UNROLL[2])
     for b in range(blocks):
         for i in range(2):
             both = jnp.concatenate([remote_sums[b][4 + 2 * i : 5 + 2 * i], remote_sums[b][5 + 2 * i : 6 + 2 * i]], axis=1)
@@ -227,15 +336,14 @@
         own_out[8 * a : 8 * a + 8, :] = jnp.where(lane_iota < HALF, parts[0], pltpu.roll(parts[1], HALF, 1))
 
 
-def faces_call(live_faces, heat2, corners, basis, area, group, group_size, received):
-    rows = heat2.shape[0]
-    tiles = corners.shape[1] // LANES
+def faces_call(prepared, rows, group, group_size, received):
+    tiles = prepared[0].shape[1]
     bits = group.bit_length() - 1
     blocks = (group * group_size + 4 * LANES) // (2 * LANES)
     f32 = jnp.float32
     group_rows = [1] + [1 << bit for bit in range(bits)]
     return pl.pallas_call(
-        lambda *refs: faces_kernel(rows * LANES, tiles, blocks, group, *refs),
+        lambda *refs: faces_kernel(tiles, blocks, group, *refs),
         out_shape=(
             jax.ShapeDtypeStruct((rows, LANES), f32),
             *[jax.ShapeDtypeStruct((n, group_size), f32) for n in group_rows],
@@ -243,28 +351,19 @@
             jax.ShapeDtypeStruct((1, LANES), f32),
             jax.ShapeDtypeStruct((1, LANES), f32),
         ),
-        in_specs=[SMEM] + [VMEM] * (4 + len(received)),
+        in_specs=[VMEM] * (len(prepared) + len(received)),
         out_specs=(VMEM,) * (bits + 5),
         scratch_shapes=[
-            pltpu.VMEM((2 * rows + 8, LANES), f32),
-            pltpu.VMEM((3, 8, LANES), f32),
-            pltpu.VMEM((3, 8, LANES), jnp.int32),
-            pltpu.VMEM((3, 8, LANES), f32),
-            pltpu.VMEM((3, 8, LANES), f32),
+            pltpu.VMEM((3, tiles, LANES), f32),
+            pltpu.VMEM((3, tiles, LANES), f32),
             pltpu.VMEM((8 * tiles + 128, LANES), f32),
             pltpu.VMEM((2 * blocks, LANES), f32),
             pltpu.VMEM((2 * blocks, LANES), f32),
         ],
+        cost_estimate=pl.CostEstimate(flops=COST[1], bytes_accessed=1 << 20, transcendentals=0),
         compiler_params=pltpu.CompilerParams(vmem_limit_bytes=6 * 2**20),
         name="faces",
-    )(
-        live_faces,
-        heat2,
-        corners.reshape(3, tiles, LANES),
-        basis.reshape(9, tiles, LANES),
-        area.reshape(tiles, LANES),
-        *received,
-    )
+    )(*prepared, *received)
 
 
 def scatter_kernel(rows, bits, own_ref, sub_ref, pat_ref, direct_ref, up_ref, down_ref, *refs):
@@ -308,6 +407,10 @@
     out_ref[...] = own_ref[...] + product[:rows] + product[rows:]
 
 
+def in_hbm(*arrays):
+    return [pltpu.with_memory_space_constraint(array, pltpu.HBM) for array in arrays]
+
+
 def stack(parts):
     return parts[0] if len(parts) == 1 else jnp.concatenate(parts, axis=0)
 
@@ -328,19 +431,26 @@
     heat2 = heat.reshape(rows, LANES)
     sub2 = send_sub.reshape(1, group_size)
 
-    mine, near, up, down = pl.pallas_call(
+    mine, near, up, down, sub_index, pat_index = pl.pallas_call(
         lambda *refs: send_kernel(rows, *refs),
         out_shape=(
             jax.ShapeDtypeStruct((1, group_size), f32),
             jax.ShapeDtypeStruct((2, LANES), f32),
             jax.ShapeDtypeStruct((1, LANES), f32),
             jax.ShapeDtypeStruct((1, LANES), f32),
+            jax.ShapeDtypeStruct(sub2.shape, jnp.int32),
+            jax.ShapeDtypeStruct(send_pat.shape, jnp.int32),
         ),
-        in_specs=[VMEM, VMEM, VMEM],
-        out_specs=(VMEM,) * 4,
+        in_specs=[HBM] * 3,
+        out_specs=(VMEM,) * 6,
+        scratch_shapes=[
+            pltpu.VMEM(heat2.shape, f32),
+            pltpu.SemaphoreType.DMA((3,)),
+        ],
         compiler_params=pltpu.CompilerParams(vmem_limit_bytes=2 * 2**20),
         name="send_gather",
-    )(heat2, sub2, send_pat)
+    )(*in_hbm(heat2, sub2, send_pat))
+    prepared = prepare_call(live_faces, heat2, corners, basis, area, remote_len // (2 * LANES))
     direct = swap(near, "patch", 1)
     relay = direct[1:2]
     from_below = shift(jnp.concatenate([up, relay]), "patch", 2)
@@ -350,8 +460,7 @@
         held.append(swap(stack(held), "sub", 1 << bit))
 
     own_sums, keep, *outs, near, up, down = faces_call(
-        live_faces, heat2, corners, basis, area, group, group_size,
-        (direct, from_below, from_above, *held),
+        prepared, rows, group, group_size, (direct, from_below, from_above, *held)
     )
 
     direct = swap(near, "patch", 1)
@@ -374,7 +483,7 @@
         out_specs=VMEM,
         compiler_params=pltpu.CompilerParams(vmem_limit_bytes=4 * 2**20),
         name="scatter_back",
-    )(own_sums, sub2, send_pat, direct, from_below, from_above, keep, *group_back)
+    )(own_sums, sub_index, pat_index, direct, from_below, from_above, keep, *group_back)
     return result.reshape(-1)
 
 
@@ -388,6 +497,5 @@
         P(None, ("patch", "sub")),
         P(("patch", "sub")),
     )
-    return jax.shard_map(
-        per_device, mesh=mesh, in_specs=placed, out_specs=P(("patch", "sub")), check_vma=False
-    )
+
+    return jax.shard_map(per_device, mesh=mesh, in_specs=placed, out_specs=P(("patch", "sub")), check_vma=False)

time: 31.3 us -> 28.9 us (0.923)
  waiting for transfers between devices: 3.52 us -> 7.85 us
  local copies, waits for them, and re-layouts: 3.66 us -> 0.01 us
  starting transfers between devices: 16.1 us -> 13.4 us
    ppermute x4, waiting for transfers between devices: 1.55 us -> 7.09 us  [shift(): return lax.ppermute(x, axis, [(i, (i + by) % n) for i in range(n)])]
    unnamed x14 -> x0, local copies, waits for them, and re-layouts: 3.63 us -> none
    ppermute x4, starting transfers between devices: 8.07 us -> 5.73 us  [shift(): return lax.ppermute(x, axis, [(i, (i + by) % n) for i in range(n)])]
    ppermute x6, waiting for transfers between devices: 1.97 us -> 0.76 us  [swap(): return lax.ppermute(x, axis, [(i, i ^ bit) for i in range(n)])]
    pallas_call x1 -> x2, Pallas kernels: 5.97 us -> 4.93 us  [the longest x1 2.98 us: faces_call(): pl.pallas_call(lambda *refs: faces_kernel(tiles, blocks, group, *refs), o...]
    pallas_call x1, Pallas kernels: 0.15 us -> 0.94 us  [per_device(): pl.pallas_call(lambda *refs: send_kernel(rows, *refs), out_shape=(jax.Sha...]
    ppermute x6, starting transfers between devices: 8 us -> 7.65 us  [swap(): return lax.ppermute(x, axis, [(i, i ^ bit) for i in range(n)])]
  transfers between devices with their start and end apart: 10 -> 10, of which waited for: 3 -> 4; matrix products, arithmetic and copies ran while one was open for 4% -> 0% of each run, Pallas kernels for 0% -> 7%
where the time goes in v3:
time: 28.9 us; the launch traced here: 28.7 us
  starting transfers between devices  13.4 us (46%)
  waiting for transfers between devices  7.85 us (27%)
  Pallas kernels  6.71 us (23%)
  between operations  0.72 us (2%)
    ppermute x6, starting transfers between devices, swap(): return lax.ppermute(x, axis, [(i, i ^ bit) for i in range(n)])  7.65 us
    ppermute x4, waiting for transfers between devices, shift(): return lax.ppermute(x, axis, [(i, (i + by) % n) for i in range(n)])  7.09 us
    ppermute x4, starting transfers between devices, shift(): return lax.ppermute(x, axis, [(i, (i + by) % n) for i in range(n)])  5.73 us
    pallas_call x1, Pallas kernels, faces_call(): pl.pallas_call(lambda *refs: faces_kernel(tiles, blocks, group, *refs), o...  2.98 us
    pallas_call x1, Pallas kernels, prepare_call(): pl.pallas_call(lambda *refs: prepare_kernel(rows * LANES, tiles, blocks,...  1.95 us
    pallas_call x1, Pallas kernels, per_device(): pl.pallas_call(lambda *refs: send_kernel(rows, *refs), out_shape=(jax.Sha...  0.94 us
    pallas_call x1, Pallas kernels, per_device(): pl.pallas_call(lambda *refs: scatter_kernel(rows, bits, *refs), out_shape...  0.84 us
    ppermute x6, waiting for transfers between devices, swap(): return lax.ppermute(x, axis, [(i, i ^ bit) for i in range(n)])  0.76 us
  transfers between devices with their start and end apart: 10, of which 4 were waited for; matrix products, arithmetic and copies ran while one was open for 0% of the time, Pallas kernels for 7%

profile of v3, /device:TPU:0, one launch (start us, length us, event | category | flops | bytes accessed | tf_op | source)
XLA Modules:
  0.0 28.7 jit_solution(4178512249808822964)
XLA Ops:
  0.0 0.9 %send_gather.1 = (f32[1,128]{1,0:T(1,128)S(1)}, f32[2,128]{1,0:T(2,128)S(1)}, f32[1,128]{1,0:T(1,128)S(1)}, f32[1,128]{1,0:T(1,128)S(1)}, s32[1,128]{1,0:T(1,128)S(1)}, /*index=5*/s32[4,128]{1,0:T(4,128)S(1)}) custom-call(f32[64,128]{1,0:T(8,128)} %bitcast.4, s32[1,128]{1,0:T(1,128)} %bitcast.7, s32[4,128]{1,0:T(4,128)} %refs_2_.3), custom_call_target="tpu_custom_call" | custom-call | tf_op jit(solution)/shard_map/send_gather/pallas_call | solution.py:434
  0.9 0.6 %collective-permute-start.3 = (f32[1,128]{1,0:T(1,128)S(1)}, f32[1,128]{1,0:T(1,128)S(1)}, u32[]{:S(2)}, u32[]{:S(2)}) collective-permute-start(f32[1,128]{1,0:T(1,128)S(1)} %get-tuple-element.35.refs_10_), channel_id=1, source_target_pairs={{0,1},{1,0},{2,3},{3,2},{4,5},{5,4},{6,7},{7,6},{8,9},{9,8},{10,11... | collective-permute-start | bytes 1544 | tf_op jit(solution)/shard_map/ppermute | solution.py:25
  1.5 2.6 %collective-permute-start = (f32[2,128]{1,0:T(2,128)S(1)}, f32[2,128]{1,0:T(2,128)S(1)}, u32[]{:S(2)}, u32[]{:S(2)}) collective-permute-start(f32[2,128]{1,0:T(2,128)S(1)} %get-tuple-element.32), channel_id=1, source_target_pairs={{0,4},{4,0},{8,12},{12,8},{16,20},{20,16},{24,28},{28,24},{1,5},{5... | collective-permute-start | bytes 3080 | tf_op jit(solution)/shard_map/ppermute | solution.py:25
  4.7 0.0 collective-permute-done.3.refs_11_
  4.8 1.6 %collective-permute-start.4 = (f32[2,128]{1,0:T(2,128)S(1)}, f32[2,128]{1,0:T(2,128)S(1)}, u32[]{:S(2)}, u32[]{:S(2)}) collective-permute-start(f32[2,128]{1,0:T(2,128)S(1)} %pad_maximum_fusion.4), channel_id=1, source_target_pairs={{0,2},{1,3},{2,0},{3,1},{4,6},{5,7},{6,4},{7,5},{8,10},{9,11},{10,... | collective-permute-start | bytes 3080 | tf_op jit(solution)/shard_map/ppermute | solution.py:25
  6.3 0.0 collective-permute-done.refs_7_
  6.3 3.7 %collective-permute-start.2 = (f32[2,128]{1,0:T(2,128)S(1)}, f32[2,128]{1,0:T(2,128)S(1)}, u32[]{:S(2)}, u32[]{:S(2)}) collective-permute-start(f32[2,128]{1,0:T(2,128)S(1)} %get-tuple-element.47), channel_id=1, source_target_pairs={{0,24},{4,28},{8,0},{12,4},{16,8},{20,12},{24,16},{28,20},{1,25},{... | collective-permute-start | bytes 3080 | tf_op jit(solution)/shard_map/ppermute | solution.py:20
  10.0 0.0 collective-permute-start.1
  10.0 1.9 %prepare.1 = (f32[3,128,128]{2,1,0:T(8,128)S(1)}, s32[3,128,128]{2,1,0:T(8,128)S(1)}, s32[3,128,128]{2,1,0:T(8,128)S(1)}, f32[3,128,128]{2,1,0:T(8,128)S(1)}, f3...) custom-call(s32[1]{0:T(128)S(6)} %copy.8.refs_0_, f32[64,128]{1,0:T(8,128)} %bitcast.5, ...), custom_call_target="tpu_custom_call" | custom-call | flops 16777216 | bytes 1048576 | tf_op jit(solution)/shard_map/prepare/pallas_call | solution.py:178
  12.0 0.0 collective-permute-done.4.refs_12_
  12.0 0.0 collective-permute-done.2.refs_9_
  12.0 3.4 %collective-permute-done.1.refs_8_ = f32[2,128]{1,0:T(2,128)S(1)} collective-permute-done((f32[2,128]{1,0:T(2,128)S(1)}, f32[2,128]{1,0:T(2,128)S(1)}, u32[]{:S(2)}, u32[]{:S(2)}) %collective-permute-start.1) | collective-permute-done | bytes 1056 | tf_op jit(solution)/shard_map/ppermute | solution.py:20
  15.4 3.0 %faces.1 = (f32[64,128]{1,0:T(8,128)S(1)}, f32[1,128]{1,0:T(1,128)S(1)}, f32[1,128]{1,0:T(1,128)S(1)}, f32[2,128]{1,0:T(2,128)S(1)}, f32[2,128]{1,0:T(2,128)S(1)...) custom-call(f32[3,128,128]{2,1,0:T(8,128)S(1)} %get-tuple-element.25.refs_0_, ...), custom_call_target="tpu_custom_call" | custom-call | flops 16777216 | bytes 1048576 | tf_op jit(solution)/shard_map/faces/pallas_call | solution.py:345
  18.3 1.4 %collective-permute-start.5 = (f32[2,128]{1,0:T(2,128)S(1)}, f32[2,128]{1,0:T(2,128)S(1)}, u32[]{:S(2)}, u32[]{:S(2)}) collective-permute-start(f32[2,128]{1,0:T(2,128)S(1)} %get-tuple-element.39), channel_id=1, source_target_pairs={{0,4},{4,0},{8,12},{12,8},{16,20},{20,16},{24,28},{28,24},{1,5},{5... | collective-permute-start | bytes 3080 | tf_op jit(solution)/shard_map/ppermute | solution.py:25
  19.7 1.5 %collective-permute-start.8 = (f32[2,128]{1,0:T(2,128)S(1)}, f32[2,128]{1,0:T(2,128)S(1)}, u32[]{:S(2)}, u32[]{:S(2)}) collective-permute-start(f32[2,128]{1,0:T(2,128)S(1)} %get-tuple-element.43), channel_id=1, source_target_pairs={{0,2},{1,3},{2,0},{3,1},{4,6},{5,7},{6,4},{7,5},{8,10},{9,11},{10,... | collective-permute-start | bytes 3080 | tf_op jit(solution)/shard_map/ppermute | solution.py:25
  21.2 0.7 %collective-permute-done.5.refs_3_ = f32[2,128]{1,0:T(2,128)S(1)} collective-permute-done((f32[2,128]{1,0:T(2,128)S(1)}, f32[2,128]{1,0:T(2,128)S(1)}, u32[]{:S(2)}, u32[]{:S(2)}) %collective-permute-start.5) | collective-permute-done | bytes 1056 | tf_op jit(solution)/shard_map/ppermute | solution.py:25
  22.0 0.5 %collective-permute-start.7 = (f32[2,128]{1,0:T(2,128)S(1)}, f32[2,128]{1,0:T(2,128)S(1)}, u32[]{:S(2)}, u32[]{:S(2)}) collective-permute-start(f32[2,128]{1,0:T(2,128)S(1)} %get-tuple-element.45), channel_id=1, source_target_pairs={{0,24},{4,28},{8,0},{12,4},{16,8},{20,12},{24,16},{28,20},{1,25},{... | collective-permute-start | bytes 3080 | tf_op jit(solution)/shard_map/ppermute | solution.py:20
  22.5 1.6 %collective-permute-start.6 = (f32[2,128]{1,0:T(2,128)S(1)}, f32[2,128]{1,0:T(2,128)S(1)}, u32[]{:S(2)}, u32[]{:S(2)}) collective-permute-start(f32[2,128]{1,0:T(2,128)S(1)} %get-tuple-element.46), channel_id=1, source_target_pairs={{0,8},{4,12},{8,16},{12,20},{16,24},{20,28},{24,0},{28,4},{1,9},{5... | collective-permute-start | bytes 3080 | tf_op jit(solution)/shard_map/ppermute | solution.py:20
  24.1 0.0 collective-permute-done.8.refs_7_
  24.1 0.1 collective-permute-start.9
  24.2 1.5 %collective-permute-done.7.refs_5_ = f32[2,128]{1,0:T(2,128)S(1)} collective-permute-done((f32[2,128]{1,0:T(2,128)S(1)}, f32[2,128]{1,0:T(2,128)S(1)}, u32[]{:S(2)}, u32[]{:S(2)}) %collective-permute-start.7) | collective-permute-done | bytes 1056 | tf_op jit(solution)/shard_map/ppermute | solution.py:20
  25.6 2.2 %collective-permute-done.6.refs_4_ = f32[2,128]{1,0:T(2,128)S(1)} collective-permute-done((f32[2,128]{1,0:T(2,128)S(1)}, f32[2,128]{1,0:T(2,128)S(1)}, u32[]{:S(2)}, u32[]{:S(2)}) %collective-permute-start.6) | collective-permute-done | bytes 1056 | tf_op jit(solution)/shard_map/ppermute | solution.py:20
  27.9 0.0 collective-permute-done.9.refs_8_
  27.9 0.8 %scatter_back.1 = f32[64,128]{1,0:T(8,128)} custom-call(f32[64,128]{1,0:T(8,128)S(1)} %get-tuple-element.36.refs_0_, s32[1,128]{1,0:T(1,128)S(1)} %get-tuple-element.37.refs_1_, s32[4,128]{1,0:T(4,128)S(1)} %get-tuple-element.38.refs_2_, f32[2,128]{1,0:T(2,128)S(1)} %collective-permute-done.5.refs_3_, f32[2,128]{1,0:T(2,128)S(1)} %collective-permute-done.6.refs_4_, ...), custom_call_target="tpu_custom_call" | custom-call | tf_op jit(solution)/shard_map/scatter_back/pallas_call | solution.py:479
  (7 shorter events, 0.1 us)
Async XLA Ops:
  0.9 3.8 %collective-permute-start.3 = (f32[1,128]{1,0:T(1,128)S(1)}, f32[1,128]{1,0:T(1,128)S(1)}, u32[]{:S(2)}, u32[]{:S(2)}) collective-permute-start(f32[1,128]{1,0:T(1,128)S(1)} %get-tuple-element.35.refs_10_), channel_id=1, source_target_pairs={{0,1},{1,0},{2,3},{3,2},{4,5},{5,4},{6,7},{7,6},{8,9},{9,8},{10,11... | collective-permute-start | bytes 1544 | tf_op jit(solution)/shard_map/ppermute | solution.py:25
  1.5 4.8 %collective-permute-start = (f32[2,128]{1,0:T(2,128)S(1)}, f32[2,128]{1,0:T(2,128)S(1)}, u32[]{:S(2)}, u32[]{:S(2)}) collective-permute-start(f32[2,128]{1,0:T(2,128)S(1)} %get-tuple-element.32), channel_id=1, source_target_pairs={{0,4},{4,0},{8,12},{12,8},{16,20},{20,16},{24,28},{28,24},{1,5},{5... | collective-permute-start | bytes 3080 | tf_op jit(solution)/shard_map/ppermute | solution.py:25
  4.8 7.2 %collective-permute-start.4 = (f32[2,128]{1,0:T(2,128)S(1)}, f32[2,128]{1,0:T(2,128)S(1)}, u32[]{:S(2)}, u32[]{:S(2)}) collective-permute-start(f32[2,128]{1,0:T(2,128)S(1)} %pad_maximum_fusion.4), channel_id=1, source_target_pairs={{0,2},{1,3},{2,0},{3,1},{4,6},{5,7},{6,4},{7,5},{8,10},{9,11},{10,... | collective-permute-start | bytes 3080 | tf_op jit(solution)/shard_map/ppermute | solution.py:25
  6.3 5.6 %collective-permute-start.2 = (f32[2,128]{1,0:T(2,128)S(1)}, f32[2,128]{1,0:T(2,128)S(1)}, u32[]{:S(2)}, u32[]{:S(2)}) collective-permute-start(f32[2,128]{1,0:T(2,128)S(1)} %get-tuple-element.47), channel_id=1, source_target_pairs={{0,24},{4,28},{8,0},{12,4},{16,8},{20,12},{24,16},{28,20},{1,25},{... | collective-permute-start | bytes 3080 | tf_op jit(solution)/shard_map/ppermute | solution.py:20
  10.0 5.4 %collective-permute-start.1 = (f32[2,128]{1,0:T(2,128)S(1)}, f32[2,128]{1,0:T(2,128)S(1)}, u32[]{:S(2)}, u32[]{:S(2)}) collective-permute-start(f32[2,128]{1,0:T(2,128)S(1)} %get-tuple-element.48), channel_id=1, source_target_pairs={{0,8},{4,12},{8,16},{12,20},{16,24},{20,28},{24,0},{28,4},{1,9},{5... | collective-permute-start | bytes 3080 | tf_op jit(solution)/shard_map/ppermute | solution.py:20
  18.3 3.6 %collective-permute-start.5 = (f32[2,128]{1,0:T(2,128)S(1)}, f32[2,128]{1,0:T(2,128)S(1)}, u32[]{:S(2)}, u32[]{:S(2)}) collective-permute-start(f32[2,128]{1,0:T(2,128)S(1)} %get-tuple-element.39), channel_id=1, source_target_pairs={{0,4},{4,0},{8,12},{12,8},{16,20},{20,16},{24,28},{28,24},{1,5},{5... | collective-permute-start | bytes 3080 | tf_op jit(solution)/shard_map/ppermute | solution.py:25
  19.7 4.3 %collective-permute-start.8 = (f32[2,128]{1,0:T(2,128)S(1)}, f32[2,128]{1,0:T(2,128)S(1)}, u32[]{:S(2)}, u32[]{:S(2)}) collective-permute-start(f32[2,128]{1,0:T(2,128)S(1)} %get-tuple-element.43), channel_id=1, source_target_pairs={{0,2},{1,3},{2,0},{3,1},{4,6},{5,7},{6,4},{7,5},{8,10},{9,11},{10,... | collective-permute-start | bytes 3080 | tf_op jit(solution)/shard_map/ppermute | solution.py:25
  22.0 3.6 %collective-permute-start.7 = (f32[2,128]{1,0:T(2,128)S(1)}, f32[2,128]{1,0:T(2,128)S(1)}, u32[]{:S(2)}, u32[]{:S(2)}) collective-permute-start(f32[2,128]{1,0:T(2,128)S(1)} %get-tuple-element.45), channel_id=1, source_target_pairs={{0,24},{4,28},{8,0},{12,4},{16,8},{20,12},{24,16},{28,20},{1,25},{... | collective-permute-start | bytes 3080 | tf_op jit(solution)/shard_map/ppermute | solution.py:20
  22.5 5.4 %collective-permute-start.6 = (f32[2,128]{1,0:T(2,128)S(1)}, f32[2,128]{1,0:T(2,128)S(1)}, u32[]{:S(2)}, u32[]{:S(2)}) collective-permute-start(f32[2,128]{1,0:T(2,128)S(1)} %get-tuple-element.46), channel_id=1, source_target_pairs={{0,8},{4,12},{8,16},{12,20},{16,24},{20,28},{24,0},{28,4},{1,9},{5... | collective-permute-start | bytes 3080 | tf_op jit(solution)/shard_map/ppermute | solution.py:20
  24.1 3.8 %collective-permute-start.9 = (f32[2,128]{1,0:T(2,128)S(1)}, f32[2,128]{1,0:T(2,128)S(1)}, u32[]{:S(2)}, u32[]{:S(2)}) collective-permute-start(f32[2,128]{1,0:T(2,128)S(1)} %pad_maximum_fusion.5), channel_id=1, source_target_pairs={{0,1},{1,0},{2,3},{3,2},{4,5},{5,4},{6,7},{7,6},{8,9},{9,8},{10,11... | collective-permute-start | bytes 3080 | tf_op jit(solution)/shard_map/ppermute | solution.py:25

commit v4 on v3

--- a/solution.py
+++ b/solution.py
@@ -8,16 +8,18 @@
 
 LANES = 128
 HALF = 64
-UNROLL = (8, 4, 4)
+QUARTER = 32
+UNROLL = (16, 16, 16)
 COST = (1 << 24, 1 << 24)
 VMEM = pl.BlockSpec(memory_space=pltpu.VMEM)
 HBM = pl.BlockSpec(memory_space=pltpu.HBM)
 SMEM = pl.BlockSpec(memory_space=pltpu.SMEM)
 
 
-def shift(x, axis, by):
+def swap_far(x, axis, outer):
     n = lax.axis_size(axis)
-    return lax.ppermute(x, axis, [(i, (i + by) % n) for i in range(n)])
+    low = [i for i in range(n) if (i % 4 >= 2) == outer]
+    return lax.ppermute(x, axis, [(i, (i + 2) % n) for i in low] + [((i + 2) % n, i) for i in low])
 
 
 def swap(x, axis, bit):
@@ -38,7 +40,7 @@
 
 
 def send_kernel(
-    rows, heat_hbm, sub_hbm, pat_hbm, group_ref, near_ref, up_ref, down_ref, sub_ref, pat_ref, heat_ref, sems
+    rows, heat_hbm, sub_hbm, pat_hbm, group_ref, near_ref, outer_ref, inner_ref, sub_ref, pat_ref, heat_ref, sems
 ):
     copies = [
         pltpu.make_async_copy(source, target, sems.at[i])
@@ -51,11 +53,12 @@
     blocks = rows // 8
     sub_iota = iota((8, LANES), 0)
     odd = lax.axis_index("patch") & 1
+    high = (lax.axis_index("patch") >> 1) & 1
     for j in range(5):
         if j == 0:
             index = sub_ref[0:1, :]
         else:
-            index = read(pat_ref, (1, 3, 2 * odd, 2 - 2 * odd)[j - 1])
+            index = read(pat_ref, (3 - 2 * high, 1 + 2 * high, 2 * odd, 2 - 2 * odd)[j - 1])
         index = jnp.broadcast_to(index, (8, index.shape[1]))
         if index.shape[1] < LANES:
             index = jnp.concatenate([index] * (LANES // index.shape[1]), axis=1)
@@ -70,9 +73,15 @@
         if j == 0:
             group_ref[...] = total[:, : sub_ref.shape[1]]
         elif j < 3:
-            (up_ref, down_ref)[j - 1][...] = total
+            (outer_ref, inner_ref)[j - 1][...] = total
         else:
             near_ref[j - 3 : j - 2, :] = total
+
+
+def by_side(high, outer_ref, inner_ref):
+    is_high = jnp.broadcast_to(high, outer_ref.shape) == 1
+    outer, inner = outer_ref[...], inner_ref[...]
+    return jnp.where(is_high, inner, outer), jnp.where(is_high, outer, inner)
 
 
 def prepare_kernel(
@@ -86,7 +95,7 @@
     area_hbm,
     near_out,
     off_out,
-    half_out,
+    part_out,
     lane_out,
     basis_out,
     last_out,
@@ -148,8 +157,8 @@
                 off >= LANES, lane_gather(near[1], lane), lane_gather(near[0], lane)
             )
             off_out[k, at, :] = off
-            half_out[k, at, :] = off >> 6
-            lane_out[k, at, :] = (off & (HALF - 1)).astype(jnp.float32)
+            part_out[k, at, :] = (off >> 5).astype(jnp.float32)
+            lane_out[k, at, :] = (off & (QUARTER - 1)).astype(jnp.float32)
         return carry
 
     lax.fori_loop(0, tiles // 8, near_values, 0, unroll=UNROLL[1])
@@ -180,7 +189,7 @@
         out_shape=(
             jax.ShapeDtypeStruct(per_corner, f32),
             jax.ShapeDtypeStruct(per_corner, jnp.int32),
-            jax.ShapeDtypeStruct(per_corner, jnp.int32),
+            jax.ShapeDtypeStruct(per_corner, f32),
             jax.ShapeDtypeStruct(per_corner, f32),
             jax.ShapeDtypeStruct((8 * tiles, LANES), f32),
             jax.ShapeDtypeStruct((tiles, LANES), f32),
@@ -203,10 +212,10 @@
 
 
 def faces_kernel(tiles, blocks, group, *refs):
-    near_ref, off_ref, half_s, lane_s, basis_s, last_s, weight_ref, direct_ref, up_ref, down_ref, *refs = refs
+    near_ref, off_ref, part_s, lane_s, basis_s, last_s, weight_ref, direct_ref, outer_ref, inner_ref, *refs = refs
     bits = group.bit_length() - 1
     group_refs = refs[: bits + 1]
-    own_out, group_keep, *group_outs, near_out, up_out, down_out = refs[bits + 1 : 2 * bits + 6]
+    own_out, group_keep, *group_outs, near_out, outer_out, inner_out = refs[bits + 1 : 2 * bits + 6]
     hi_s, lo_s, sums_s, remote_ref, remote_out = refs[2 * bits + 6 :]
     group_size = group_keep.shape[1]
     odd = lax.axis_index("patch") & 1
@@ -228,18 +237,20 @@
     base = group // per_row
     is_odd = jnp.broadcast_to(odd, (1, LANES)) == 1
     direct = direct_ref[0:1, :]
-    remote_ref[base : base + 1, :] = jnp.where(is_odd, direct, up_ref[1:2, :])
-    remote_ref[base + 1 : base + 2, :] = up_ref[0:1, :]
-    remote_ref[base + 2 : base + 3, :] = jnp.where(is_odd, down_ref[1:2, :], direct)
-    remote_ref[base + 3 : base + 4, :] = down_ref[0:1, :]
+    high = (lax.axis_index("patch") >> 1) & 1
+    below, above = by_side(high, outer_ref, inner_ref)
+    remote_ref[base : base + 1, :] = jnp.where(is_odd, direct, below[1:2])
+    remote_ref[base + 1 : base + 2, :] = below[0:1]
+    remote_ref[base + 2 : base + 3, :] = jnp.where(is_odd, above[1:2], direct)
+    remote_ref[base + 3 : base + 4, :] = above[0:1]
     remote_rows = [
         jnp.concatenate([remote_ref[2 * (t % blocks) + i : 2 * (t % blocks) + i + 1, :] for t in range(8)], axis=0)
         for i in range(2)
     ]
-    half_iota = iota((HALF, LANES), 0, jnp.float32).astype(jnp.bfloat16)
-    one = jnp.ones((HALF, LANES), jnp.bfloat16)
-    nil = jnp.zeros((HALF, LANES), jnp.bfloat16)
-    pad = jnp.zeros((16, LANES), jnp.bfloat16)
+    lane_row = iota((QUARTER, LANES), 0, jnp.float32).astype(jnp.bfloat16)
+    part_row = iota((16, LANES), 0, jnp.float32).astype(jnp.bfloat16)
+    one = jnp.ones((QUARTER, LANES), jnp.bfloat16)
+    nil = jnp.zeros((QUARTER, LANES), jnp.bfloat16)
 
     def face_values(g, carry):
         t0 = pl.multiple_of(8 * g, 8)
@@ -266,45 +277,42 @@
 
     lax.fori_loop(0, tiles // 8, face_values, 0, unroll=UNROLL[1])
 
+    def spread_row(ref, k, t, rows):
+        return jnp.broadcast_to(ref[k, pl.ds(t, 1), :], (rows, LANES)).astype(jnp.bfloat16)
+
+    def tile_sums(t):
+        left, right = [], []
+        for k in range(3):
+            match = spread_row(part_s, k, t, 16) == part_row
+            a_hi = jnp.where(match, spread_row(hi_s, k, t, 16), nil[:16])
+            a_lo = jnp.where(match, spread_row(lo_s, k, t, 16), nil[:16])
+            left.append(jnp.concatenate([a_hi, a_lo], axis=0))
+            right.append(jnp.where(spread_row(lane_s, k, t, QUARTER) == lane_row, one, nil))
+        product = lax.dot_general(
+            jnp.concatenate(left, axis=1),
+            jnp.concatenate(right, axis=1),
+            (((1,), (1,)), ((), ())),
+            preferred_element_type=jnp.float32,
+        )
+        return product[:16] + product[16:]
+
     def eight_tiles(g, remote_sums):
-        t0 = pl.multiple_of(8 * g, 8)
-        out = []
-        for pair in range(4):
-            left, right = [], []
-            for t in range(2):
-                for k in range(3):
-                    at = pl.ds(t0 + 2 * pair + t, 1)
-                    half = jnp.broadcast_to(half_s[k, at, :], (8, LANES))
-                    match = half == sub_iota
-                    a_hi = jnp.where(match, jnp.broadcast_to(hi_s[k, at, :], (8, LANES)), 0.0)
-                    a_lo = jnp.where(match, jnp.broadcast_to(lo_s[k, at, :], (8, LANES)), 0.0)
-                    a = jnp.concatenate([a_hi, a_lo], axis=0).astype(jnp.bfloat16)
-                    left.append(jnp.concatenate([a, pad] if t == 0 else [pad, a], axis=0))
-                    lane = jnp.broadcast_to(lane_s[k, at, :], (HALF, LANES)).astype(jnp.bfloat16)
-                    right.append(jnp.where(lane == half_iota, one, nil))
-            product = lax.dot_general(
-                jnp.concatenate(left, axis=1),
-                jnp.concatenate(right, axis=1),
-                (((1,), (1,)), ((), ())),
-                preferred_element_type=jnp.float32,
-            )
-            for t in range(2):
-                total = product[16 * t : 16 * t + 8] + product[16 * t + 8 : 16 * t + 16]
-                sums_s[pl.ds(pl.multiple_of(8 * (t0 + 2 * pair + t), 8), 8), 0:HALF] = total
-                out.append(total)
-        return tuple(
-            acc + sum(out[t] for t in range(8) if t % blocks == b)
-            for b, acc in enumerate(remote_sums)
-        )
-
-    start = tuple(jnp.zeros((8, HALF), jnp.float32) for _ in range(blocks))
+        remote_sums = list(remote_sums)
+        for i in range(8):
+            t = 8 * g + i
+            total = tile_sums(t)
+            sums_s[pl.ds(pl.multiple_of(8 * t + 8, 8), 8), 0:QUARTER] = total[:8]
+            remote_sums[i % blocks] = remote_sums[i % blocks] + total[8:]
+        return tuple(remote_sums)
+
+    start = tuple(jnp.zeros((8, QUARTER), jnp.float32) for _ in range(blocks))
     remote_sums = lax.fori_loop(0, tiles // 8, eight_tiles, start, unroll=UNROLL[2])
     for b in range(blocks):
         for i in range(2):
-            both = jnp.concatenate([remote_sums[b][4 + 2 * i : 5 + 2 * i], remote_sums[b][5 + 2 * i : 6 + 2 * i]], axis=1)
-            remote_out[2 * b + i : 2 * b + i + 1, :] = both
-    up_out[...] = remote_out[base + 3 : base + 4, :]
-    down_out[...] = remote_out[base + 1 : base + 2, :]
+            row = [remote_sums[b][4 * i + e : 4 * i + e + 1] for e in range(4)]
+            remote_out[2 * b + i : 2 * b + i + 1, :] = jnp.concatenate(row, axis=1)
+    outer_out[...] = read(remote_out, base + 1 + 2 * high)
+    inner_out[...] = read(remote_out, base + 3 - 2 * high)
     near_out[0:1, :] = read(remote_out, base + 2 - 2 * odd)
     near_out[1:2, :] = read(remote_out, base + 2 * odd)
     for i in range(group):
@@ -319,21 +327,21 @@
         else:
             bit = i.bit_length() - 1
             group_outs[bit][i - (1 << bit) : i - (1 << bit) + 1, :] = row
-    sums_s[8 * tiles : 8 * tiles + 32, :] = jnp.zeros((32, LANES), jnp.float32)
+    sums_s[0:8, :] = jnp.zeros((8, LANES), jnp.float32)
+    sums_s[8 * tiles + 8 : 8 * tiles + 32, :] = jnp.zeros((24, LANES), jnp.float32)
     for a in range(rows // 8):
-        parts = []
-        for odd in range(2):
-            total = jnp.zeros((8, LANES), jnp.float32)
-            for i in range(4):
-                lowest = 16 * a + odd + 2 - i
-                if lowest >= 0:
-                    got = sums_s[pl.ds(8 * lowest + i, 8, stride=16), :]
-                else:
-                    got = sums_s[pl.ds(8 * (lowest + 2) + i, 8, stride=16), :]
-                    got = jnp.where(sub_iota == 0, 0.0, pltpu.roll(got, 1, 0))
-                total = total + got
-            parts.append(total)
-        own_out[8 * a : 8 * a + 8, :] = jnp.where(lane_iota < HALF, parts[0], pltpu.roll(parts[1], HALF, 1))
+        whole = None
+        for e in range(4):
+            total = None
+            for h in range(e & 1, 8, 2):
+                tile = 16 * a + (e + 4 - h) // 2
+                got = sums_s[pl.ds(8 * (tile + 1) + h, 8, stride=16), :]
+                total = got if total is None else total + got
+            if e == 0:
+                whole = total
+            else:
+                whole = jnp.where(lane_iota >= QUARTER * e, pltpu.roll(total, QUARTER * e, 1), whole)
+        own_out[8 * a : 8 * a + 8, :] = whole
 
 
 def faces_call(prepared, rows, group, group_size, received):
@@ -366,12 +374,13 @@
     )(*prepared, *received)
 
 
-def scatter_kernel(rows, bits, own_ref, sub_ref, pat_ref, direct_ref, up_ref, down_ref, *refs):
+def scatter_kernel(rows, bits, own_ref, sub_ref, pat_ref, direct_ref, outer_ref, inner_ref, *refs):
     out_ref = refs[-1]
     row_iota = iota((rows, LANES), 0)
     lane_iota = iota((LANES, LANES), 0)
     odd = jnp.broadcast_to(lax.axis_index("patch") & 1, (1, LANES)) == 1
     direct = direct_ref[0:1, :]
+    below, above = by_side((lax.axis_index("patch") >> 1) & 1, outer_ref, inner_ref)
     group_back = refs[0][...]
     for i in range(bits):
         ref = refs[i + 1]
@@ -379,10 +388,10 @@
             group_back = group_back + ref[at : at + 1, :]
     backs = [
         group_back,
-        jnp.where(odd, down_ref[1:2, :], direct),
-        down_ref[0:1, :],
-        jnp.where(odd, direct, up_ref[1:2, :]),
-        up_ref[0:1, :],
+        jnp.where(odd, above[1:2], direct),
+        above[0:1],
+        jnp.where(odd, direct, below[1:2]),
+        below[0:1],
     ]
     left, right = [], []
     for j in range(5):
@@ -425,13 +434,13 @@
     remote_len = group * group_size + offsets * block_size
     assert offsets == 4 and block_size == LANES and LANES % group_size == 0
     assert group & (group - 1) == 0 and remote_len in (512, 1024, 2048)
-    assert lax.axis_size("patch") % 2 == 0
+    assert lax.axis_size("patch") % 4 == 0
     bits = group.bit_length() - 1
     f32 = jnp.float32
     heat2 = heat.reshape(rows, LANES)
     sub2 = send_sub.reshape(1, group_size)
 
-    mine, near, up, down, sub_index, pat_index = pl.pallas_call(
+    mine, near, outer, inner, sub_index, pat_index = pl.pallas_call(
         lambda *refs: send_kernel(rows, *refs),
         out_shape=(
             jax.ShapeDtypeStruct((1, group_size), f32),
@@ -453,20 +462,20 @@
     prepared = prepare_call(live_faces, heat2, corners, basis, area, remote_len // (2 * LANES))
     direct = swap(near, "patch", 1)
     relay = direct[1:2]
-    from_below = shift(jnp.concatenate([up, relay]), "patch", 2)
-    from_above = shift(jnp.concatenate([down, relay]), "patch", -2)
+    outer = swap_far(jnp.concatenate([outer, relay]), "patch", True)
+    inner = swap_far(jnp.concatenate([inner, relay]), "patch", False)
     held = [mine]
     for bit in range(bits):
         held.append(swap(stack(held), "sub", 1 << bit))
 
-    own_sums, keep, *outs, near, up, down = faces_call(
-        prepared, rows, group, group_size, (direct, from_below, from_above, *held)
+    own_sums, keep, *outs, near, outer, inner = faces_call(
+        prepared, rows, group, group_size, (direct, outer, inner, *held)
     )
 
     direct = swap(near, "patch", 1)
     relay = direct[1:2]
-    from_above = shift(jnp.concatenate([down, relay]), "patch", -2)
-    from_below = shift(jnp.concatenate([up, relay]), "patch", 2)
+    outer = swap_far(jnp.concatenate([outer, relay]), "patch", True)
+    inner = swap_far(jnp.concatenate([inner, relay]), "patch", False)
     pieces, group_back = [], []
     for bit in reversed(range(bits)):
         width = 1 << bit
@@ -483,7 +492,7 @@
         out_specs=VMEM,
         compiler_params=pltpu.CompilerParams(vmem_limit_bytes=4 * 2**20),
         name="scatter_back",
-    )(own_sums, sub_index, pat_index, direct, from_below, from_above, keep, *group_back)
+    )(own_sums, sub_index, pat_index, direct, outer, inner, keep, *group_back)
     return result.reshape(-1)
 
 

time: 28.9 us -> 25.1 us (0.87)
  waiting for transfers between devices: 7.85 us -> 4.78 us
  Pallas kernels: 6.71 us -> 4.98 us
  starting transfers between devices: 13.4 us -> 14.4 us
    ppermute x4, waiting for transfers between devices: 7.09 us -> 4.02 us  [swap_far(): lax.ppermute(x, axis, [(i, (i + 2) % n) for i in low] + [((i + 2) % n, i)...]
    pallas_call x1, Pallas kernels: 2.98 us -> 1.54 us  [faces_call(): pl.pallas_call(lambda *refs: faces_kernel(tiles, blocks, group, *refs), o...]
    ppermute x4, starting transfers between devices: 5.73 us -> 6.72 us  [swap_far(): lax.ppermute(x, axis, [(i, (i + 2) % n) for i in low] + [((i + 2) % n, i)...]
    pallas_call x1, Pallas kernels: 1.95 us -> 1.65 us  [prepare_call(): pl.pallas_call(lambda *refs: prepare_kernel(rows * LANES, tiles, blocks,...]
where the time goes in v4:
time: 25.1 us; the launch traced here: 24.9 us
  starting transfers between devices  14.4 us (57%)
  Pallas kernels  4.98 us (20%)
  waiting for transfers between devices  4.78 us (19%)
  between operations  0.73 us (3%)
    ppermute x6, starting transfers between devices, swap(): return lax.ppermute(x, axis, [(i, i ^ bit) for i in range(n)])  7.66 us
    ppermute x4, starting transfers between devices, swap_far(): lax.ppermute(x, axis, [(i, (i + 2) % n) for i in low] + [((i + 2) % n, i)...  6.72 us
    ppermute x4, waiting for transfers between devices, swap_far(): lax.ppermute(x, axis, [(i, (i + 2) % n) for i in low] + [((i + 2) % n, i)...  4.02 us
    pallas_call x1, Pallas kernels, prepare_call(): pl.pallas_call(lambda *refs: prepare_kernel(rows * LANES, tiles, blocks,...  1.65 us
    pallas_call x1, Pallas kernels, faces_call(): pl.pallas_call(lambda *refs: faces_kernel(tiles, blocks, group, *refs), o...  1.54 us
    pallas_call x1, Pallas kernels, per_device(): pl.pallas_call(lambda *refs: send_kernel(rows, *refs), out_shape=(jax.Sha...  0.94 us
    pallas_call x1, Pallas kernels, per_device(): pl.pallas_call(lambda *refs: scatter_kernel(rows, bits, *refs), out_shape...  0.84 us
    ppermute x6, waiting for transfers between devices, swap(): return lax.ppermute(x, axis, [(i, i ^ bit) for i in range(n)])  0.76 us
  transfers between devices with their start and end apart: 10, of which 4 were waited for; matrix products, arithmetic and copies ran while one was open for 0% of the time, Pallas kernels for 7%

profile of v4, /device:TPU:0, one launch (start us, length us, event | category | flops | bytes accessed | tf_op | source)
XLA Modules:
  0.0 24.9 jit_solution(8791257536193423291)
XLA Ops:
  0.0 0.9 %send_gather.1 = (f32[1,128]{1,0:T(1,128)S(1)}, f32[2,128]{1,0:T(2,128)S(1)}, f32[1,128]{1,0:T(1,128)S(1)}, f32[1,128]{1,0:T(1,128)S(1)}, s32[1,128]{1,0:T(1,128)S(1)}, /*index=5*/s32[4,128]{1,0:T(4,128)S(1)}) custom-call(f32[64,128]{1,0:T(8,128)} %bitcast.4, s32[1,128]{1,0:T(1,128)} %bitcast.7, s32[4,128]{1,0:T(4,128)} %refs_2_.3), custom_call_target="tpu_custom_call" | custom-call | tf_op jit(solution)/shard_map/send_gather/pallas_call | solution.py:443
  1.0 0.6 %collective-permute-start.3 = (f32[1,128]{1,0:T(1,128)S(1)}, f32[1,128]{1,0:T(1,128)S(1)}, u32[]{:S(2)}, u32[]{:S(2)}) collective-permute-start(f32[1,128]{1,0:T(1,128)S(1)} %get-tuple-element.35.refs_10_), channel_id=1, source_target_pairs={{0,1},{1,0},{2,3},{3,2},{4,5},{5,4},{6,7},{7,6},{8,9},{9,8},{10,11... | collective-permute-start | bytes 1544 | tf_op jit(solution)/shard_map/ppermute | solution.py:27
  1.5 2.6 %collective-permute-start = (f32[2,128]{1,0:T(2,128)S(1)}, f32[2,128]{1,0:T(2,128)S(1)}, u32[]{:S(2)}, u32[]{:S(2)}) collective-permute-start(f32[2,128]{1,0:T(2,128)S(1)} %get-tuple-element.32), channel_id=1, source_target_pairs={{0,4},{4,0},{8,12},{12,8},{16,20},{20,16},{24,28},{28,24},{1,5},{5... | collective-permute-start | bytes 3080 | tf_op jit(solution)/shard_map/ppermute | solution.py:27
  4.7 0.0 collective-permute-done.3.refs_11_
  4.8 1.6 %collective-permute-start.4 = (f32[2,128]{1,0:T(2,128)S(1)}, f32[2,128]{1,0:T(2,128)S(1)}, u32[]{:S(2)}, u32[]{:S(2)}) collective-permute-start(f32[2,128]{1,0:T(2,128)S(1)} %pad_maximum_fusion.4), channel_id=1, source_target_pairs={{0,2},{1,3},{2,0},{3,1},{4,6},{5,7},{6,4},{7,5},{8,10},{9,11},{10,... | collective-permute-start | bytes 3080 | tf_op jit(solution)/shard_map/ppermute | solution.py:27
  6.3 0.0 collective-permute-done.refs_7_
  6.3 1.6 %collective-permute-start.2 = (f32[2,128]{1,0:T(2,128)S(1)}, f32[2,128]{1,0:T(2,128)S(1)}, u32[]{:S(2)}, u32[]{:S(2)}) collective-permute-start(f32[2,128]{1,0:T(2,128)S(1)} %get-tuple-element.47), channel_id=1, source_target_pairs={{0,8},{4,12},{16,24},{20,28},{8,0},{12,4},{24,16},{28,20},{1,9},{5... | collective-permute-start | bytes 3080 | tf_op jit(solution)/shard_map/ppermute | solution.py:22
  8.0 2.5 %collective-permute-start.1 = (f32[2,128]{1,0:T(2,128)S(1)}, f32[2,128]{1,0:T(2,128)S(1)}, u32[]{:S(2)}, u32[]{:S(2)}) collective-permute-start(f32[2,128]{1,0:T(2,128)S(1)} %get-tuple-element.48), channel_id=1, source_target_pairs={{8,16},{12,20},{24,0},{28,4},{16,8},{20,12},{0,24},{4,28},{9,17},{... | collective-permute-start | bytes 3080 | tf_op jit(solution)/shard_map/ppermute | solution.py:22
  10.5 1.6 %prepare.1 = (f32[3,128,128]{2,1,0:T(8,128)S(1)}, s32[3,128,128]{2,1,0:T(8,128)S(1)}, f32[3,128,128]{2,1,0:T(8,128)S(1)}, f32[3,128,128]{2,1,0:T(8,128)S(1)}, f3...) custom-call(s32[1]{0:T(128)S(6)} %copy.8.refs_0_, f32[64,128]{1,0:T(8,128)} %bitcast.5, ...), custom_call_target="tpu_custom_call" | custom-call | flops 16777216 | bytes 1048576 | tf_op jit(solution)/shard_map/prepare/pallas_call | solution.py:187
  12.1 0.0 collective-permute-done.4.refs_12_
  12.1 0.0 collective-permute-done.2.refs_9_
  12.1 1.2 %collective-permute-done.1.refs_8_ = f32[2,128]{1,0:T(2,128)S(1)} collective-permute-done((f32[2,128]{1,0:T(2,128)S(1)}, f32[2,128]{1,0:T(2,128)S(1)}, u32[]{:S(2)}, u32[]{:S(2)}) %collective-permute-start.1) | collective-permute-done | bytes 1056 | tf_op jit(solution)/shard_map/ppermute | solution.py:22
  13.4 1.5 %faces.1 = (f32[64,128]{1,0:T(8,128)S(1)}, f32[1,128]{1,0:T(1,128)S(1)}, f32[1,128]{1,0:T(1,128)S(1)}, f32[2,128]{1,0:T(2,128)S(1)}, f32[2,128]{1,0:T(2,128)S(1)...) custom-call(f32[3,128,128]{2,1,0:T(8,128)S(1)} %get-tuple-element.25.refs_0_, ...), custom_call_target="tpu_custom_call" | custom-call | flops 16777216 | bytes 1048576 | tf_op jit(solution)/shard_map/faces/pallas_call | solution.py:353
  14.9 1.4 %collective-permute-start.5 = (f32[2,128]{1,0:T(2,128)S(1)}, f32[2,128]{1,0:T(2,128)S(1)}, u32[]{:S(2)}, u32[]{:S(2)}) collective-permute-start(f32[2,128]{1,0:T(2,128)S(1)} %get-tuple-element.39), channel_id=1, source_target_pairs={{0,4},{4,0},{8,12},{12,8},{16,20},{20,16},{24,28},{28,24},{1,5},{5... | collective-permute-start | bytes 3080 | tf_op jit(solution)/shard_map/ppermute | solution.py:27
  16.3 1.5 %collective-permute-start.8 = (f32[2,128]{1,0:T(2,128)S(1)}, f32[2,128]{1,0:T(2,128)S(1)}, u32[]{:S(2)}, u32[]{:S(2)}) collective-permute-start(f32[2,128]{1,0:T(2,128)S(1)} %get-tuple-element.43), channel_id=1, source_target_pairs={{0,2},{1,3},{2,0},{3,1},{4,6},{5,7},{6,4},{7,5},{8,10},{9,11},{10,... | collective-permute-start | bytes 3080 | tf_op jit(solution)/shard_map/ppermute | solution.py:27
  17.8 0.7 %collective-permute-done.5.refs_3_ = f32[2,128]{1,0:T(2,128)S(1)} collective-permute-done((f32[2,128]{1,0:T(2,128)S(1)}, f32[2,128]{1,0:T(2,128)S(1)}, u32[]{:S(2)}, u32[]{:S(2)}) %collective-permute-start.5) | collective-permute-done | bytes 1056 | tf_op jit(solution)/shard_map/ppermute | solution.py:27
  18.6 0.1 collective-permute-start.7
  18.6 2.5 %collective-permute-start.6 = (f32[2,128]{1,0:T(2,128)S(1)}, f32[2,128]{1,0:T(2,128)S(1)}, u32[]{:S(2)}, u32[]{:S(2)}) collective-permute-start(f32[2,128]{1,0:T(2,128)S(1)} %get-tuple-element.46), channel_id=1, source_target_pairs={{8,16},{12,20},{24,0},{28,4},{16,8},{20,12},{0,24},{4,28},{9,17},{... | collective-permute-start | bytes 3080 | tf_op jit(solution)/shard_map/ppermute | solution.py:22
  21.2 0.0 collective-permute-done.8.refs_7_
  21.2 0.1 collective-permute-start.9
  21.3 0.9 %collective-permute-done.7.refs_5_ = f32[2,128]{1,0:T(2,128)S(1)} collective-permute-done((f32[2,128]{1,0:T(2,128)S(1)}, f32[2,128]{1,0:T(2,128)S(1)}, u32[]{:S(2)}, u32[]{:S(2)}) %collective-permute-start.7) | collective-permute-done | bytes 1056 | tf_op jit(solution)/shard_map/ppermute | solution.py:22
  22.2 1.9 %collective-permute-done.6.refs_4_ = f32[2,128]{1,0:T(2,128)S(1)} collective-permute-done((f32[2,128]{1,0:T(2,128)S(1)}, f32[2,128]{1,0:T(2,128)S(1)}, u32[]{:S(2)}, u32[]{:S(2)}) %collective-permute-start.6) | collective-permute-done | bytes 1056 | tf_op jit(solution)/shard_map/ppermute | solution.py:22
  24.1 0.0 collective-permute-done.9.refs_8_
  24.1 0.8 %scatter_back.1 = f32[64,128]{1,0:T(8,128)} custom-call(f32[64,128]{1,0:T(8,128)S(1)} %get-tuple-element.36.refs_0_, s32[1,128]{1,0:T(1,128)S(1)} %get-tuple-element.37.refs_1_, s32[4,128]{1,0:T(4,128)S(1)} %get-tuple-element.38.refs_2_, f32[2,128]{1,0:T(2,128)S(1)} %collective-permute-done.5.refs_3_, f32[2,128]{1,0:T(2,128)S(1)} %collective-permute-done.6.refs_4_, ...), custom_call_target="tpu_custom_call" | custom-call | tf_op jit(solution)/shard_map/scatter_back/pallas_call | solution.py:488
  (7 shorter events, 0.1 us)
Async XLA Ops:
  1.0 3.8 %collective-permute-start.3 = (f32[1,128]{1,0:T(1,128)S(1)}, f32[1,128]{1,0:T(1,128)S(1)}, u32[]{:S(2)}, u32[]{:S(2)}) collective-permute-start(f32[1,128]{1,0:T(1,128)S(1)} %get-tuple-element.35.refs_10_), channel_id=1, source_target_pairs={{0,1},{1,0},{2,3},{3,2},{4,5},{5,4},{6,7},{7,6},{8,9},{9,8},{10,11... | collective-permute-start | bytes 1544 | tf_op jit(solution)/shard_map/ppermute | solution.py:27
  1.5 4.8 %collective-permute-start = (f32[2,128]{1,0:T(2,128)S(1)}, f32[2,128]{1,0:T(2,128)S(1)}, u32[]{:S(2)}, u32[]{:S(2)}) collective-permute-start(f32[2,128]{1,0:T(2,128)S(1)} %get-tuple-element.32), channel_id=1, source_target_pairs={{0,4},{4,0},{8,12},{12,8},{16,20},{20,16},{24,28},{28,24},{1,5},{5... | collective-permute-start | bytes 3080 | tf_op jit(solution)/shard_map/ppermute | solution.py:27
  4.8 7.4 %collective-permute-start.4 = (f32[2,128]{1,0:T(2,128)S(1)}, f32[2,128]{1,0:T(2,128)S(1)}, u32[]{:S(2)}, u32[]{:S(2)}) collective-permute-start(f32[2,128]{1,0:T(2,128)S(1)} %pad_maximum_fusion.4), channel_id=1, source_target_pairs={{0,2},{1,3},{2,0},{3,1},{4,6},{5,7},{6,4},{7,5},{8,10},{9,11},{10,... | collective-permute-start | bytes 3080 | tf_op jit(solution)/shard_map/ppermute | solution.py:27
  6.3 5.8 %collective-permute-start.2 = (f32[2,128]{1,0:T(2,128)S(1)}, f32[2,128]{1,0:T(2,128)S(1)}, u32[]{:S(2)}, u32[]{:S(2)}) collective-permute-start(f32[2,128]{1,0:T(2,128)S(1)} %get-tuple-element.47), channel_id=1, source_target_pairs={{0,8},{4,12},{16,24},{20,28},{8,0},{12,4},{24,16},{28,20},{1,9},{5... | collective-permute-start | bytes 3080 | tf_op jit(solution)/shard_map/ppermute | solution.py:22
  8.0 5.4 %collective-permute-start.1 = (f32[2,128]{1,0:T(2,128)S(1)}, f32[2,128]{1,0:T(2,128)S(1)}, u32[]{:S(2)}, u32[]{:S(2)}) collective-permute-start(f32[2,128]{1,0:T(2,128)S(1)} %get-tuple-element.48), channel_id=1, source_target_pairs={{8,16},{12,20},{24,0},{28,4},{16,8},{20,12},{0,24},{4,28},{9,17},{... | collective-permute-start | bytes 3080 | tf_op jit(solution)/shard_map/ppermute | solution.py:22
  14.9 3.6 %collective-permute-start.5 = (f32[2,128]{1,0:T(2,128)S(1)}, f32[2,128]{1,0:T(2,128)S(1)}, u32[]{:S(2)}, u32[]{:S(2)}) collective-permute-start(f32[2,128]{1,0:T(2,128)S(1)} %get-tuple-element.39), channel_id=1, source_target_pairs={{0,4},{4,0},{8,12},{12,8},{16,20},{20,16},{24,28},{28,24},{1,5},{5... | collective-permute-start | bytes 3080 | tf_op jit(solution)/shard_map/ppermute | solution.py:27
  16.3 4.9 %collective-permute-start.8 = (f32[2,128]{1,0:T(2,128)S(1)}, f32[2,128]{1,0:T(2,128)S(1)}, u32[]{:S(2)}, u32[]{:S(2)}) collective-permute-start(f32[2,128]{1,0:T(2,128)S(1)} %get-tuple-element.43), channel_id=1, source_target_pairs={{0,2},{1,3},{2,0},{3,1},{4,6},{5,7},{6,4},{7,5},{8,10},{9,11},{10,... | collective-permute-start | bytes 3080 | tf_op jit(solution)/shard_map/ppermute | solution.py:27
  18.6 3.6 %collective-permute-start.7 = (f32[2,128]{1,0:T(2,128)S(1)}, f32[2,128]{1,0:T(2,128)S(1)}, u32[]{:S(2)}, u32[]{:S(2)}) collective-permute-start(f32[2,128]{1,0:T(2,128)S(1)} %get-tuple-element.45), channel_id=1, source_target_pairs={{0,8},{4,12},{16,24},{20,28},{8,0},{12,4},{24,16},{28,20},{1,9},{5... | collective-permute-start | bytes 3080 | tf_op jit(solution)/shard_map/ppermute | solution.py:22
  18.6 5.4 %collective-permute-start.6 = (f32[2,128]{1,0:T(2,128)S(1)}, f32[2,128]{1,0:T(2,128)S(1)}, u32[]{:S(2)}, u32[]{:S(2)}) collective-permute-start(f32[2,128]{1,0:T(2,128)S(1)} %get-tuple-element.46), channel_id=1, source_target_pairs={{8,16},{12,20},{24,0},{28,4},{16,8},{20,12},{0,24},{4,28},{9,17},{... | collective-permute-start | bytes 3080 | tf_op jit(solution)/shard_map/ppermute | solution.py:22
  21.2 2.9 %collective-permute-start.9 = (f32[2,128]{1,0:T(2,128)S(1)}, f32[2,128]{1,0:T(2,128)S(1)}, u32[]{:S(2)}, u32[]{:S(2)}) collective-permute-start(f32[2,128]{1,0:T(2,128)S(1)} %pad_maximum_fusion.5), channel_id=1, source_target_pairs={{0,1},{1,0},{2,3},{3,2},{4,5},{5,4},{6,7},{7,6},{8,9},{9,8},{10,11... | collective-permute-start | bytes 3080 | tf_op jit(solution)/shard_map/ppermute | solution.py:27

commit v5 on v4

v5 whole, which is shorter than its diff:
```python
import jax
import jax.numpy as jnp
from jax import lax
from jax.experimental import pallas as pl
from jax.experimental.pallas import tpu as pltpu
from jax.sharding import PartitionSpec as P


LANES = 128
HALF = 64
QUARTER = 32
COST = (1 << 24, 1 << 24)
VMEM = pl.BlockSpec(memory_space=pltpu.VMEM)
HBM = pl.BlockSpec(memory_space=pltpu.HBM)
SMEM = pl.BlockSpec(memory_space=pltpu.SMEM)


def swap_far(x, axis, outer):
    n = lax.axis_size(axis)
    low = [i for i in range(n) if (i % 4 >= 2) == outer]
    return lax.ppermute(x, axis, [(i, (i + 2) % n) for i in low] + [((i + 2) % n, i) for i in low])


def swap(x, axis, bit):
    n = lax.axis_size(axis)
    return lax.ppermute(x, axis, [(i, i ^ bit) for i in range(n)])


def iota(shape, dim, dtype=jnp.int32):
    return lax.broadcasted_iota(jnp.int32, shape, dim).astype(dtype)


def lane_gather(table, lanes):
    return jnp.take_along_axis(table, lanes, axis=1, mode="promise_in_bounds")


def read(ref, at):
    return ref[pl.ds(at, 1), :]


def send_kernel(
    rows, heat_hbm, sub_hbm, pat_hbm, group_ref, near_ref, outer_ref, inner_ref, sub_ref, pat_ref, heat_ref, sems
):
    copies = [
        pltpu.make_async_copy(source, target, sems.at[i])
        for i, (source, target) in enumerate(((heat_hbm, heat_ref), (sub_hbm, sub_ref), (pat_hbm, pat_ref)))
    ]
    for copy in copies:
        copy.start()
    for copy in copies:
        copy.wait()
    blocks = rows // 8
    sub_iota = iota((8, LANES), 0)
    odd = lax.axis_index("patch") & 1
    high = (lax.axis_index("patch") >> 1) & 1
    for j in range(5):
        if j == 0:
            index = sub_ref[0:1, :]
        else:
            index = read(pat_ref, (3 - 2 * high, 1 + 2 * high, 2 * odd, 2 - 2 * odd)[j - 1])
        index = jnp.broadcast_to(index, (8, index.shape[1]))
        if index.shape[1] < LANES:
            index = jnp.concatenate([index] * (LANES // index.shape[1]), axis=1)
        lane = index & (LANES - 1)
        row = index >> 7
        total = jnp.zeros((8, LANES), jnp.float32)
        for a in range(blocks):
            got = lane_gather(heat_ref[8 * a : 8 * a + 8, :], lane)
            total = jnp.where(row == sub_iota + 8 * a, got, total)
        total = jnp.where((row & 7) == sub_iota, total, 0.0)
        total = jnp.sum(total, axis=0, keepdims=True)
        if j == 0:
            group_ref[...] = total[:, : sub_ref.shape[1]]
        elif j < 3:
            (outer_ref, inner_ref)[j - 1][0:1, :] = total
        elif j == 3:
            near_ref[...] = total
        else:
            outer_ref[1:2, :] = total
            inner_ref[1:2, :] = total


def by_side(high, outer_ref, inner_ref):
    is_high = jnp.broadcast_to(high, outer_ref.shape) == 1
    outer, inner = outer_ref[...], inner_ref[...]
    return jnp.where(is_high, inner, outer), jnp.where(is_high, outer, inner)


def prepare_kernel(
    owned,
    tiles,
    blocks,
    live_ref,
    heat_hbm,
    corner_hbm,
    basis_hbm,
    area_hbm,
    near_out,
    off_out,
    part_out,
    lane_out,
    basis_out,
    last_out,
    weight_out,
    heat_ref,
    corner_ref,
    basis_ref,
    area_ref,
    win,
    corner_s,
    sems,
):
    copies = [
        pltpu.make_async_copy(source, target, sems.at[i])
        for i, (source, target) in enumerate(
            ((corner_hbm, corner_ref), (heat_hbm, heat_ref), (basis_hbm, basis_ref), (area_hbm, area_ref))
        )
    ]
    for copy in copies:
        copy.start()
    rows = owned // LANES
    lane_iota = iota((8, LANES), 1)
    sub_iota = iota((8, LANES), 0)
    copies[1].wait()
    zero = jnp.zeros((8, LANES), jnp.float32)
    win[0:8, :] = zero
    win[2 * rows : 2 * rows + 8, :] = zero
    for a in range(rows // 8):
        here = heat_ref[8 * a : 8 * a + 8, :]
        if a + 1 < rows // 8:
            after = heat_ref[8 * a + 1 : 8 * a + 9, :]
        else:
            after = jnp.concatenate([heat_ref[8 * a + 1 : 8 * a + 8, :], zero[0:1]], axis=0)
        both = jnp.where(lane_iota < HALF, after, here)
        win[pl.ds(16 * a + 2, 8, stride=2), :] = here
        win[pl.ds(16 * a + 3, 8, stride=2), :] = pltpu.roll(both, HALF, 1)
    first = pltpu.roll(jnp.broadcast_to(heat_ref[0:1, :], (8, LANES)), HALF, 1)
    win[1:2, :] = jnp.where(lane_iota < HALF, 0.0, first)[0:1]
    copies[0].wait()

    per_class = tiles // blocks
    place = [t % blocks * per_class + t // blocks for t in range(tiles)]
    for t in range(tiles):
        corner_s[4 * place[t] : 4 * place[t] + 3, :] = corner_ref[:, LANES * t : LANES * (t + 1)]
    for r in range(blocks):
        for g in range(per_class // 8):
            t0 = 8 * blocks * g + r
            tile = t0 + blocks * sub_iota
            near = [win[pl.ds(t0 + 2 * i, 8, stride=blocks), :] for i in range(2)]
            near_start = HALF * tile - LANES
            far_start = owned + 2 * LANES * r - 2 * LANES
            at = slice(per_class * r + 8 * g, per_class * r + 8 * g + 8)
            for k in range(3):
                pos = corner_s[pl.ds(4 * (per_class * r + 8 * g) + k, 8, stride=4), :]
                off = pos - jnp.where(pos >= owned, far_start, near_start)
                lane = off & (LANES - 1)
                near_out[k, at, :] = jnp.where(
                    off >= LANES, lane_gather(near[1], lane), lane_gather(near[0], lane)
                )
                off_out[k, at, :] = off
                part_out[k, at, :] = (off >> 5).astype(jnp.float32)
                lane_out[k, at, :] = (off & (QUARTER - 1)).astype(jnp.float32)
    copies[2].wait()

    for t in range(tiles):
        nine = basis_ref[:, LANES * t : LANES * (t + 1)].astype(jnp.float32)
        basis_out[8 * place[t] : 8 * place[t] + 8, :] = nine[0:8]
        last_out[place[t] : place[t] + 1, :] = nine[8:9]
    copies[3].wait()
    live = live_ref[0]
    for r in range(blocks):
        for g in range(per_class // 8):
            t0 = 8 * blocks * g + r
            slot = (t0 + blocks * sub_iota) * LANES + lane_iota
            at = slice(per_class * r + 8 * g, per_class * r + 8 * g + 8)
            weight_out[at, :] = jnp.where(slot < live, -area_ref[pl.ds(t0, 8, stride=blocks), :], 0.0)


def prepare_call(live_faces, heat2, corners, basis, area, blocks):
    rows = heat2.shape[0]
    tiles = corners.shape[1] // LANES
    f32 = jnp.float32
    per_corner = (3, tiles, LANES)
    return pl.pallas_call(
        lambda *refs: prepare_kernel(rows * LANES, tiles, blocks, *refs),
        out_shape=(
            jax.ShapeDtypeStruct(per_corner, f32),
            jax.ShapeDtypeStruct(per_corner, jnp.int32),
            jax.ShapeDtypeStruct(per_corner, f32),
            jax.ShapeDtypeStruct(per_corner, f32),
            jax.ShapeDtypeStruct((8 * tiles, LANES), f32),
            jax.ShapeDtypeStruct((tiles, LANES), f32),
            jax.ShapeDtypeStruct((tiles, LANES), f32),
        ),
        in_specs=[SMEM] + [HBM] * 4,
        out_specs=(VMEM,) * 7,
        scratch_shapes=[
            pltpu.VMEM(heat2.shape, f32),
            pltpu.VMEM(corners.shape, jnp.int32),
            pltpu.VMEM(basis.shape, basis.dtype),
            pltpu.VMEM((tiles, LANES), f32),
            pltpu.VMEM((2 * rows + 8, LANES), f32),
            pltpu.VMEM((4 * tiles, LANES), jnp.int32),
            pltpu.SemaphoreType.DMA((4,)),
        ],
        cost_estimate=pl.CostEstimate(flops=COST[0], bytes_accessed=1 << 20, transcendentals=0),
        compiler_params=pltpu.CompilerParams(vmem_limit_bytes=6 * 2**20),
        name="prepare",
    )(live_faces, *in_hbm(heat2, corners, basis, area.reshape(tiles, LANES)))


def class_sums(classes, blocks, prepared, remote_ref, hi_s, lo_s, sums_ref):
    near_ref, off_ref, part_s, lane_s, basis_s, last_s, weight_ref = prepared
    per_class = near_ref.shape[1] // blocks
    lane_row = iota((QUARTER, LANES), 0, jnp.float32).astype(jnp.bfloat16)
    part_row = iota((16, LANES), 0, jnp.float32).astype(jnp.bfloat16)
    one = jnp.ones((QUARTER, LANES), jnp.bfloat16)
    nil = jnp.zeros((QUARTER, LANES), jnp.bfloat16)

    def spread_row(ref, k, row, height):
        return jnp.broadcast_to(ref[k, row : row + 1, :], (height, LANES)).astype(jnp.bfloat16)

    def tile_sums(row):
        left, right = [], []
        for k in range(3):
            match = spread_row(part_s, k, row, 16) == part_row
            a_hi = jnp.where(match, spread_row(hi_s, k, row - per_class * classes[0], 16), nil[:16])
            a_lo = jnp.where(match, spread_row(lo_s, k, row - per_class * classes[0], 16), nil[:16])
            left.append(jnp.concatenate([a_hi, a_lo], axis=0))
            right.append(jnp.where(spread_row(lane_s, k, row, QUARTER) == lane_row, one, nil))
        product = lax.dot_general(
            jnp.concatenate(left, axis=1),
            jnp.concatenate(right, axis=1),
            (((1,), (1,)), ((), ())),
            preferred_element_type=jnp.float32,
        )
        return product[:16] + product[16:]

    for r in classes:
        far_rows = [
            jnp.broadcast_to(remote_ref[2 * (r - classes[0]) + i : 2 * (r - classes[0]) + i + 1, :], (8, LANES))
            for i in range(2)
        ]
        for g in range(per_class // 8):
            row = per_class * r + 8 * g
            at = slice(row, row + 8)
            values = []
            for k in range(3):
                off = off_ref[k, at, :]
                lane = off & (LANES - 1)
                far = jnp.where(
                    off >= 3 * LANES, lane_gather(far_rows[1], lane), lane_gather(far_rows[0], lane)
                )
                values.append(jnp.where(off >= 2 * LANES, far, near_ref[k, at, :]))
            basis = [basis_s[pl.ds(8 * row + i, 8, stride=8), :] for i in range(8)] + [last_s[at, :]]
            grad = [sum(basis[3 * k + c] * values[k] for k in range(3)) for c in range(3)]
            square = grad[0] * grad[0] + grad[1] * grad[1] + grad[2] * grad[2]
            scale = weight_ref[at, :] / jnp.maximum(jnp.sqrt(square), 1.0)
            field = [grad[c] * scale for c in range(3)]
            kept = slice(row - per_class * classes[0], row - per_class * classes[0] + 8)
            for k in range(3):
                term = sum(basis[3 * k + c] * field[c] for c in range(3))
                hi = term.astype(jnp.bfloat16).astype(jnp.float32)
                hi_s[k, kept, :] = hi
                lo_s[k, kept, :] = term - hi
    remote_sums = []
    for r in classes:
        remote_sum = jnp.zeros((8, QUARTER), jnp.float32)
        for i in range(per_class):
            total = tile_sums(per_class * r + i)
            spot = 8 * (blocks * i + r) + 8
            sums_ref[spot : spot + 8, 0:QUARTER] = total[:8]
            remote_sum = remote_sum + total[8:]
        remote_sums.append(remote_sum)
    return remote_sums


def full_rows(quarters):
    return [
        jnp.concatenate([sums[4 * i + e : 4 * i + e + 1] for e in range(4)], axis=1)
        for sums in quarters
        for i in range(2)
    ]


def patch_faces_kernel(classes, blocks, *refs):
    prepared, refs = refs[:7], refs[7:]
    direct_ref, outer_ref, inner_ref, sums_out, near_out, outer_out, inner_out = refs[:7]
    hi_s, lo_s, remote_ref = refs[7:]
    odd = lax.axis_index("patch") & 1
    high = (lax.axis_index("patch") >> 1) & 1
    is_odd = jnp.broadcast_to(odd, (1, LANES)) == 1
    is_high = jnp.broadcast_to(high, (1, LANES)) == 1
    direct = direct_ref[0:1, :]
    below, above = by_side(high, outer_ref, inner_ref)
    relayed = direct_ref[1:2, :]
    remote_ref[0:1, :] = jnp.where(is_odd, direct, relayed)
    remote_ref[1:2, :] = below[0:1]
    remote_ref[2:3, :] = jnp.where(is_odd, relayed, direct)
    remote_ref[3:4, :] = above[0:1]
    rows = full_rows(class_sums(classes, blocks, prepared, remote_ref, hi_s, lo_s, sums_out))
    outer_out[0:1, :] = jnp.where(is_high, rows[3], rows[1])
    inner_out[0:1, :] = jnp.where(is_high, rows[1], rows[3])
    near_out[...] = jnp.where(is_odd, rows[0], rows[2])
    relay = jnp.where(is_odd, rows[2], rows[0])
    outer_out[1:2, :] = relay
    inner_out[1:2, :] = relay


def group_faces_kernel(classes, blocks, group, *refs):
    prepared, sums_ref, refs = refs[:7], refs[7], refs[8:]
    tiles = prepared[0].shape[1]
    bits = group.bit_length() - 1
    group_refs = refs[: bits + 1]
    own_out, group_keep, *group_outs = refs[bits + 1 : 2 * bits + 3]
    hi_s, lo_s, sums_s, remote_ref, remote_out = refs[2 * bits + 3 :]
    group_size = group_keep.shape[1]
    me = lax.axis_index("sub")
    rows = own_out.shape[0]
    lane_iota = iota((8, LANES), 1)
    per_row = LANES // group_size
    for q in range(group // per_row):
        parts = []
        for e in range(per_row):
            from_me = me ^ (q * per_row + e)
            part = group_refs[0][...]
            for bit in range(bits):
                got = read(group_refs[bit + 1], from_me & ((1 << bit) - 1))
                part = jnp.where(from_me >> bit == 1, got, part)
            parts.append(part)
        remote_ref[q : q + 1, :] = parts[0] if per_row == 1 else jnp.concatenate(parts, axis=1)
    for t in range(tiles):
        if t % blocks not in classes:
            sums_s[8 * t + 8 : 8 * t + 16, :] = sums_ref[8 * t + 8 : 8 * t + 16, :]
    sums_s[0:8, :] = jnp.zeros((8, LANES), jnp.float32)
    sums_s[8 * tiles + 8 : 8 * tiles + 32, :] = jnp.zeros((24, LANES), jnp.float32)
    for i, row in enumerate(full_rows(class_sums(classes, blocks, prepared, remote_ref, hi_s, lo_s, sums_s))):
        remote_out[i : i + 1, :] = row
    for i in range(group):
        owner = me ^ i
        row = read(remote_out, owner // per_row)
        if per_row > 1:
            turn = (LANES - (owner % per_row) * group_size) % LANES
            row = pltpu.roll(jnp.broadcast_to(row, (8, LANES)), turn, 1)[0:1, :group_size]
        if i == 0:
            group_keep[...] = row
        else:
            bit = i.bit_length() - 1
            group_outs[bit][i - (1 << bit) : i - (1 << bit) + 1, :] = row
    for a in range(rows // 8):
        whole = None
        for e in range(4):
            total = None
            for h in range(e & 1, 8, 2):
                tile = 16 * a + (e + 4 - h) // 2
                got = sums_s[pl.ds(8 * (tile + 1) + h, 8, stride=16), :]
                total = got if total is None else total + got
            if e == 0:
                whole = total
            else:
                whole = jnp.where(lane_iota >= QUARTER * e, pltpu.roll(total, QUARTER * e, 1), whole)
        own_out[8 * a : 8 * a + 8, :] = whole


def patch_faces_call(prepared, blocks, received):
    tiles = prepared[0].shape[1]
    f32 = jnp.float32
    classes = tuple(range(blocks - 2, blocks))
    kept = (3, 2 * tiles // blocks, LANES)
    return pl.pallas_call(
        lambda *refs: patch_faces_kernel(classes, blocks, *refs),
        out_shape=(
            jax.ShapeDtypeStruct((8 * tiles + 32, LANES), f32),
            jax.ShapeDtypeStruct((1, LANES), f32),
            jax.ShapeDtypeStruct((2, LANES), f32),
            jax.ShapeDtypeStruct((2, LANES), f32),
        ),
        in_specs=[VMEM] * (len(prepared) + len(received)),
        out_specs=(VMEM,) * 4,
        scratch_shapes=[pltpu.VMEM(kept, f32), pltpu.VMEM(kept, f32), pltpu.VMEM((4, LANES), f32)],
        cost_estimate=pl.CostEstimate(flops=COST[1], bytes_accessed=1 << 20, transcendentals=0),
        compiler_params=pltpu.CompilerParams(vmem_limit_bytes=6 * 2**20),
        name="patch_faces",
    )(*prepared, *received)


def group_faces_call(prepared, blocks, sums, rows, group, group_size, held):
    tiles = prepared[0].shape[1]
    bits = group.bit_length() - 1
    f32 = jnp.float32
    classes = tuple(range(blocks - 2))
    kept = (3, len(classes) * tiles // blocks, LANES)
    group_rows = [1] + [1 << bit for bit in range(bits)]
    return pl.pallas_call(
        lambda *refs: group_faces_kernel(classes, blocks, group, *refs),
        out_shape=(
            jax.ShapeDtypeStruct((rows, LANES), f32),
            *[jax.ShapeDtypeStruct((n, group_size), f32) for n in group_rows],
        ),
        in_specs=[VMEM] * (len(prepared) + 1 + len(held)),
        out_specs=(VMEM,) * (bits + 2),
        scratch_shapes=[
            pltpu.VMEM(kept, f32),
            pltpu.VMEM(kept, f32),
            pltpu.VMEM((8 * tiles + 32, LANES), f32),
            pltpu.VMEM((2 * len(classes), LANES), f32),
            pltpu.VMEM((2 * len(classes), LANES), f32),
        ],
        cost_estimate=pl.CostEstimate(flops=COST[1], bytes_accessed=1 << 20, transcendentals=0),
        compiler_params=pltpu.CompilerParams(vmem_limit_bytes=6 * 2**20),
        name="group_faces",
    )(*prepared, sums, *held)


def scatter_kernel(rows, bits, own_ref, sub_ref, pat_ref, direct_ref, outer_ref, inner_ref, *refs):
    out_ref = refs[-1]
    row_iota = iota((rows, LANES), 0)
    lane_iota = iota((LANES, LANES), 0)
    odd = jnp.broadcast_to(lax.axis_index("patch") & 1, (1, LANES)) == 1
    direct = direct_ref[0:1, :]
    below, above = by_side((lax.axis_index("patch") >> 1) & 1, outer_ref, inner_ref)
    group_back = refs[0][...]
    for i in range(bits):
        ref = refs[i + 1]
        for at in range(0, ref.shape[0], 1 << (bits - 1 - i)):
            group_back = group_back + ref[at : at + 1, :]
    backs = [
        group_back,
        jnp.where(odd, direct_ref[1:2, :], direct),
        above[0:1],
        jnp.where(odd, direct, direct_ref[1:2, :]),
        below[0:1],
    ]
    left, right = [], []
    for j in range(5):
        index = sub_ref[0:1, :] if j == 0 else pat_ref[j - 1 : j, :]
        value = backs[j]
        width = index.shape[1]
        hi = value.astype(jnp.bfloat16).astype(jnp.float32)
        match = jnp.broadcast_to(index >> 7, (rows, width)) == row_iota[:, :width]
        a_hi = jnp.where(match, jnp.broadcast_to(hi, (rows, width)), 0.0)
        a_lo = jnp.where(match, jnp.broadcast_to(value - hi, (rows, width)), 0.0)
        left.append(jnp.concatenate([a_hi, a_lo], axis=0).astype(jnp.bfloat16))
        spot = jnp.broadcast_to(index & (LANES - 1), (LANES, width)) == lane_iota[:, :width]
        right.append(jnp.where(spot, 1.0, 0.0).astype(jnp.bfloat16))
    product = 0.0
    for part in ([0], [1, 2, 3, 4]) if left[0].shape[1] < LANES else ([0, 1, 2, 3, 4],):
        product = product + lax.dot_general(
            jnp.concatenate([left[j] for j in part], axis=1),
            jnp.concatenate([right[j] for j in part], axis=1),
            (((1,), (1,)), ((), ())),
            preferred_element_type=jnp.float32,
        )
    out_ref[...] = own_ref[...] + product[:rows] + product[rows:]


def in_hbm(*arrays):
    return [pltpu.with_memory_space_constraint(array, pltpu.HBM) for array in arrays]


def stack(parts):
    return parts[0] if len(parts) == 1 else jnp.concatenate(parts, axis=0)


def per_device(heat, basis, area, corners, send_sub, send_pat, live_faces):
    owned = heat.shape[0]
    rows = owned // LANES
    group = lax.axis_size("sub")
    group_size = send_sub.shape[0]
    block_size = send_pat.shape[1]
    offsets = send_pat.shape[0]
    remote_len = group * group_size + offsets * block_size
    assert offsets == 4 and block_size == LANES and LANES % group_size == 0
    assert group & (group - 1) == 0 and group * group_size % (2 * LANES) == 0
    assert lax.axis_size("patch") % 4 == 0
    bits = group.bit_length() - 1
    f32 = jnp.float32
    heat2 = heat.reshape(rows, LANES)
    sub2 = send_sub.reshape(1, group_size)

    mine, near, outer, inner, sub_index, pat_index = pl.pallas_call(
        lambda *refs: send_kernel(rows, *refs),
        out_shape=(
            jax.ShapeDtypeStruct((1, group_size), f32),
            jax.ShapeDtypeStruct((1, LANES), f32),
            jax.ShapeDtypeStruct((2, LANES), f32),
            jax.ShapeDtypeStruct((2, LANES), f32),
            jax.ShapeDtypeStruct(sub2.shape, jnp.int32),
            jax.ShapeDtypeStruct(send_pat.shape, jnp.int32),
        ),
        in_specs=[HBM] * 3,
        out_specs=(VMEM,) * 6,
        scratch_shapes=[
            pltpu.VMEM(heat2.shape, f32),
            pltpu.SemaphoreType.DMA((3,)),
        ],
        compiler_params=pltpu.CompilerParams(vmem_limit_bytes=2 * 2**20),
        name="send_gather",
    )(*in_hbm(heat2, sub2, send_pat))
    blocks = remote_len // (2 * LANES)
    prepared = prepare_call(live_faces, heat2, corners, basis, area, blocks)
    place = lax.axis_index("patch")
    take_inner = ((place >> 1) & 1) == (place & 1)
    outer = swap_far(outer, "patch", True)
    inner = swap_far(inner, "patch", False)
    relay = jnp.where(take_inner, inner[1:2], outer[1:2])
    direct = swap(jnp.concatenate([near, relay]), "patch", 1)
    held = [mine]
    for bit in range(bits):
        held.append(swap(stack(held), "sub", 1 << bit))

    sums, near, outer, inner = patch_faces_call(prepared, blocks, (direct, outer, inner))
    own_sums, keep, *outs = group_faces_call(prepared, blocks, sums, rows, group, group_size, held)

    outer = swap_far(outer, "patch", True)
    inner = swap_far(inner, "patch", False)
    relay = jnp.where(take_inner, inner[1:2], outer[1:2])
    direct = swap(jnp.concatenate([near, relay]), "patch", 1)
    pieces, group_back = [], []
    for bit in reversed(range(bits)):
        width = 1 << bit
        got = swap(stack([outs[bit]] + [p[width : 2 * width] for p in pieces]), "sub", width)
        group_back.append(got)
        pieces = [p[:width] for p in pieces] + [
            got[at : at + width] for at in range(0, got.shape[0], width)
        ]

    result = pl.pallas_call(
        lambda *refs: scatter_kernel(rows, bits, *refs),
        out_shape=jax.ShapeDtypeStruct((rows, LANES), f32),
        in_specs=[VMEM] * (7 + bits),
        out_specs=VMEM,
        compiler_params=pltpu.CompilerParams(vmem_limit_bytes=4 * 2**20),
        name="scatter_back",
    )(own_sums, sub_index, pat_index, direct, outer, inner, keep, *group_back)
    return result.reshape(-1)


def solution(mesh):
    placed = (
        P(("patch", "sub")),
        P(None, ("patch", "sub")),
        P(("patch", "sub")),
        P(None, ("patch", "sub")),
        P(("patch", "sub")),
        P(None, ("patch", "sub")),
        P(("patch", "sub")),
    )

    return jax.shard_map(per_device, mesh=mesh, in_specs=placed, out_specs=P(("patch", "sub")), check_vma=False)
```

time: 25.1 us -> 27.3 us (1.088)
  waiting for transfers between devices: 4.78 us -> 7.61 us
  starting transfers between devices: 14.4 us -> 13.8 us
    ppermute x6, waiting for transfers between devices: 0.76 us -> 3.99 us  [swap(): return lax.ppermute(x, axis, [(i, i ^ bit) for i in range(n)])]
    ppermute x6, starting transfers between devices: 7.66 us -> 6.19 us  [swap(): return lax.ppermute(x, axis, [(i, i ^ bit) for i in range(n)])]
    ppermute x4, starting transfers between devices: 6.72 us -> 7.59 us  [swap_far(): lax.ppermute(x, axis, [(i, (i + 2) % n) for i in low] + [((i + 2) % n, i)...]
    ppermute x4, waiting for transfers between devices: 4.02 us -> 3.62 us  [swap_far(): lax.ppermute(x, axis, [(i, (i + 2) % n) for i in low] + [((i + 2) % n, i)...]
    pallas_call x1 -> x2, Pallas kernels: 1.54 us -> 1.78 us  [the longest x1 0.91 us: group_faces_call(): pl.pallas_call(lambda *refs: group_faces_kernel(classes, blocks, group, *...]
  transfers between devices with their start and end apart: 10 -> 10, of which waited for: 4 -> 6; matrix products, arithmetic and copies ran while one was open for 0% -> 0% of each run, Pallas kernels for 7% -> 8%
where the time goes in v5:
time: 27.3 us; the launch traced here: 27.1 us
  starting transfers between devices  13.8 us (51%)
  waiting for transfers between devices  7.61 us (28%)
  Pallas kernels  4.97 us (18%)
  between operations  0.7 us (3%)
    ppermute x4, starting transfers between devices, swap_far(): lax.ppermute(x, axis, [(i, (i + 2) % n) for i in low] + [((i + 2) % n, i)...  7.59 us
    ppermute x6, starting transfers between devices, swap(): return lax.ppermute(x, axis, [(i, i ^ bit) for i in range(n)])  6.19 us
    ppermute x6, waiting for transfers between devices, swap(): return lax.ppermute(x, axis, [(i, i ^ bit) for i in range(n)])  3.99 us
    ppermute x4, waiting for transfers between devices, swap_far(): lax.ppermute(x, axis, [(i, (i + 2) % n) for i in low] + [((i + 2) % n, i)...  3.62 us
    pallas_call x1, Pallas kernels, prepare_call(): pl.pallas_call(lambda *refs: prepare_kernel(rows * LANES, tiles, blocks,...  1.41 us
    pallas_call x1, Pallas kernels, per_device(): pl.pallas_call(lambda *refs: send_kernel(rows, *refs), out_shape=(jax.Sha...  0.94 us
    pallas_call x1, Pallas kernels, group_faces_call(): pl.pallas_call(lambda *refs: group_faces_kernel(classes, blocks, group, *...  0.91 us
    pallas_call x1, Pallas kernels, patch_faces_call(): pl.pallas_call(lambda *refs: patch_faces_kernel(classes, blocks, *refs),...  0.87 us
  transfers between devices with their start and end apart: 10, of which 6 were waited for; matrix products, arithmetic and copies ran while one was open for 0% of the time, Pallas kernels for 8%

profile of v5, /device:TPU:0, one launch (start us, length us, event | category | flops | bytes accessed | tf_op | source)
XLA Modules:
  0.0 27.1 jit_solution(8827068652323021300)
XLA Ops:
  0.0 0.9 %send_gather.1 = (f32[1,128]{1,0:T(1,128)S(1)}, f32[1,128]{1,0:T(1,128)S(1)}, f32[2,128]{1,0:T(2,128)S(1)}, f32[2,128]{1,0:T(2,128)S(1)}, s32[1,128]{1,0:T(1,128)S(1)}, /*index=5*/s32[4,128]{1,0:T(4,128)S(1)}) custom-call(f32[64,128]{1,0:T(8,128)} %bitcast.4, s32[1,128]{1,0:T(1,128)} %bitcast.7, s32[4,128]{1,0:T(4,128)} %refs_2_.3), custom_call_target="tpu_custom_call" | custom-call | tf_op jit(solution)/shard_map/send_gather/pallas_call | solution.py:481
  1.0 0.6 %collective-permute-start.3 = (f32[1,128]{1,0:T(1,128)S(1)}, f32[1,128]{1,0:T(1,128)S(1)}, u32[]{:S(2)}, u32[]{:S(2)}) collective-permute-start(f32[1,128]{1,0:T(1,128)S(1)} %get-tuple-element.37.refs_8_), channel_id=1, source_target_pairs={{0,1},{1,0},{2,3},{3,2},{4,5},{5,4},{6,7},{7,6},{8,9},{9,8},{10,11... | collective-permute-start | bytes 1544 | tf_op jit(solution)/shard_map/ppermute | solution.py:26
  1.5 2.6 %collective-permute-start = (f32[2,128]{1,0:T(2,128)S(1)}, f32[2,128]{1,0:T(2,128)S(1)}, u32[]{:S(2)}, u32[]{:S(2)}) collective-permute-start(f32[2,128]{1,0:T(2,128)S(1)} %get-tuple-element.34), channel_id=1, source_target_pairs={{0,8},{4,12},{16,24},{20,28},{8,0},{12,4},{24,16},{28,20},{1,9},{5... | collective-permute-start | bytes 3080 | tf_op jit(solution)/shard_map/ppermute | solution.py:21
  4.1 2.5 %collective-permute-start.1 = (f32[2,128]{1,0:T(2,128)S(1)}, f32[2,128]{1,0:T(2,128)S(1)}, u32[]{:S(2)}, u32[]{:S(2)}) collective-permute-start(f32[2,128]{1,0:T(2,128)S(1)} %get-tuple-element.35), channel_id=1, source_target_pairs={{8,16},{12,20},{24,0},{28,4},{16,8},{20,12},{0,24},{4,28},{9,17},{... | collective-permute-start | bytes 3080 | tf_op jit(solution)/shard_map/ppermute | solution.py:21
  7.3 1.4 %prepare.1 = (f32[3,128,128]{2,1,0:T(8,128)S(1)}, s32[3,128,128]{2,1,0:T(8,128)S(1)}, f32[3,128,128]{2,1,0:T(8,128)S(1)}, f32[3,128,128]{2,1,0:T(8,128)S(1)}, f3...) custom-call(s32[1]{0:T(128)S(6)} %copy.8.refs_0_, f32[64,128]{1,0:T(8,128)} %bitcast.5, ...), custom_call_target="tpu_custom_call" | custom-call | flops 16777216 | bytes 1048576 | tf_op jit(solution)/shard_map/prepare/pallas_call | solution.py:184
  8.7 0.0 collective-permute-done.refs_9_
  8.7 0.8 %collective-permute-done.1.refs_8_ = f32[2,128]{1,0:T(2,128)S(1)} collective-permute-done((f32[2,128]{1,0:T(2,128)S(1)}, f32[2,128]{1,0:T(2,128)S(1)}, u32[]{:S(2)}, u32[]{:S(2)}) %collective-permute-start.1) | collective-permute-done | bytes 1056 | tf_op jit(solution)/shard_map/ppermute | solution.py:21
  9.5 1.6 %collective-permute-start.2 = (f32[2,128]{1,0:T(2,128)S(1)}, f32[2,128]{1,0:T(2,128)S(1)}, u32[]{:S(2)}, u32[]{:S(2)}) collective-permute-start(f32[2,128]{1,0:T(2,128)S(1)} %pad_maximum_fusion), channel_id=1, source_target_pairs={{0,4},{4,0},{8,12},{12,8},{16,20},{20,16},{24,28},{28,24},{1,5},{5... | collective-permute-start | bytes 3080 | tf_op jit(solution)/shard_map/ppermute | solution.py:26
  11.1 0.0 collective-permute-done.3.refs_9_
  11.1 1.6 %collective-permute-start.4 = (f32[2,128]{1,0:T(2,128)S(1)}, f32[2,128]{1,0:T(2,128)S(1)}, u32[]{:S(2)}, u32[]{:S(2)}) collective-permute-start(f32[2,128]{1,0:T(2,128)S(1)} %pad_maximum_fusion.1), channel_id=1, source_target_pairs={{0,2},{1,3},{2,0},{3,1},{4,6},{5,7},{6,4},{7,5},{8,10},{9,11},{10,... | collective-permute-start | bytes 3080 | tf_op jit(solution)/shard_map/ppermute | solution.py:26
  12.7 0.5 %collective-permute-done.2.refs_7_ = f32[2,128]{1,0:T(2,128)S(1)} collective-permute-done((f32[2,128]{1,0:T(2,128)S(1)}, f32[2,128]{1,0:T(2,128)S(1)}, u32[]{:S(2)}, u32[]{:S(2)}) %collective-permute-start.2) | collective-permute-done | bytes 1056 | tf_op jit(solution)/shard_map/ppermute | solution.py:26
  13.2 0.9 %patch_faces.1 = (f32[1056,128]{1,0:T(8,128)S(1)}, f32[1,128]{1,0:T(1,128)S(1)}, f32[2,128]{1,0:T(2,128)S(1)}, f32[2,128]{1,0:T(2,128)S(1)}) custom-call(f32[3,128,128]{2,1,0:T(8,128)S(1)} %get-tuple-element.26.refs_0_, s32[3,128,128]{2,1,0:T(8,128)S(1)} %get-tuple-element.27.refs_1_, f32[3,128,128]{2,1,0:T(8,128)S(1)} %get-tuple-element.28.refs_2_, ...), custom_call_target="tpu_custom_call" | custom-call | flops 16777216 | bytes 1048576 | tf_op jit(solution)/shard_map/patch_faces/pallas_call | solution.py:370
  14.0 0.7 %collective-permute-done.4.refs_10_ = f32[2,128]{1,0:T(2,128)S(1)} collective-permute-done((f32[2,128]{1,0:T(2,128)S(1)}, f32[2,128]{1,0:T(2,128)S(1)}, u32[]{:S(2)}, u32[]{:S(2)}) %collective-permute-start.4) | collective-permute-done | bytes 1056 | tf_op jit(solution)/shard_map/ppermute | solution.py:26
  14.8 0.9 %group_faces.1 = (f32[64,128]{1,0:T(8,128)S(1)}, f32[1,128]{1,0:T(1,128)S(1)}, f32[1,128]{1,0:T(1,128)S(1)}, f32[2,128]{1,0:T(2,128)S(1)}) custom-call(f32[3,128,128]{2,1,0:T(8,128)S(1)} %get-tuple-element.26.refs_0_, s32[3,128,128]{2,1,0:T(8,128)S(1)} %get-tuple-element.27.refs_1_, f32[3,128,128]{2,1,0:T(8,128)S(1)} %get-tuple-element.28.refs_2_, ...), custom_call_target="tpu_custom_call" | custom-call | flops 16777216 | bytes 1048576 | tf_op jit(solution)/shard_map/group_faces/pallas_call | solution.py:394
  15.7 1.6 %collective-permute-start.8 = (f32[2,128]{1,0:T(2,128)S(1)}, f32[2,128]{1,0:T(2,128)S(1)}, u32[]{:S(2)}, u32[]{:S(2)}) collective-permute-start(f32[2,128]{1,0:T(2,128)S(1)} %get-tuple-element.45), channel_id=1, source_target_pairs={{0,2},{1,3},{2,0},{3,1},{4,6},{5,7},{6,4},{7,5},{8,10},{9,11},{10,... | collective-permute-start | bytes 3080 | tf_op jit(solution)/shard_map/ppermute | solution.py:26
  17.2 0.0 collective-permute-start.5
  17.2 2.5 %collective-permute-start.6 = (f32[2,128]{1,0:T(2,128)S(1)}, f32[2,128]{1,0:T(2,128)S(1)}, u32[]{:S(2)}, u32[]{:S(2)}) collective-permute-start(f32[2,128]{1,0:T(2,128)S(1)} %get-tuple-element.43), channel_id=1, source_target_pairs={{8,16},{12,20},{24,0},{28,4},{16,8},{20,12},{0,24},{4,28},{9,17},{... | collective-permute-start | bytes 3080 | tf_op jit(solution)/shard_map/ppermute | solution.py:21
  19.7 0.0 collective-permute-done.8.refs_7_
  19.7 0.1 collective-permute-start.9
  19.8 1.0 %collective-permute-done.5.refs_5_ = f32[2,128]{1,0:T(2,128)S(1)} collective-permute-done((f32[2,128]{1,0:T(2,128)S(1)}, f32[2,128]{1,0:T(2,128)S(1)}, u32[]{:S(2)}, u32[]{:S(2)}) %collective-permute-start.5) | collective-permute-done | bytes 1056 | tf_op jit(solution)/shard_map/ppermute | solution.py:21
  20.8 1.8 %collective-permute-done.6.refs_4_ = f32[2,128]{1,0:T(2,128)S(1)} collective-permute-done((f32[2,128]{1,0:T(2,128)S(1)}, f32[2,128]{1,0:T(2,128)S(1)}, u32[]{:S(2)}, u32[]{:S(2)}) %collective-permute-start.6) | collective-permute-done | bytes 1056 | tf_op jit(solution)/shard_map/ppermute | solution.py:21
  22.6 0.9 %collective-permute-start.7 = (f32[2,128]{1,0:T(2,128)S(1)}, f32[2,128]{1,0:T(2,128)S(1)}, u32[]{:S(2)}, u32[]{:S(2)}) collective-permute-start(f32[2,128]{1,0:T(2,128)S(1)} %pad_maximum_fusion.2), channel_id=1, source_target_pairs={{0,4},{4,0},{8,12},{12,8},{16,20},{20,16},{24,28},{28,24},{1,5},{5... | collective-permute-start | bytes 3080 | tf_op jit(solution)/shard_map/ppermute | solution.py:26
  23.5 0.0 collective-permute-done.9.refs_8_
  23.5 2.8 %collective-permute-done.7.refs_3_ = f32[2,128]{1,0:T(2,128)S(1)} collective-permute-done((f32[2,128]{1,0:T(2,128)S(1)}, f32[2,128]{1,0:T(2,128)S(1)}, u32[]{:S(2)}, u32[]{:S(2)}) %collective-permute-start.7) | collective-permute-done | bytes 1056 | tf_op jit(solution)/shard_map/ppermute | solution.py:26
  26.3 0.8 %scatter_back.1 = f32[64,128]{1,0:T(8,128)} custom-call(f32[64,128]{1,0:T(8,128)S(1)} %get-tuple-element.38.refs_0_, s32[1,128]{1,0:T(1,128)S(1)} %get-tuple-element.39.refs_1_, s32[4,128]{1,0:T(4,128)S(1)} %get-tuple-element.40.refs_2_, f32[2,128]{1,0:T(2,128)S(1)} %collective-permute-done.7.refs_3_, f32[2,128]{1,0:T(2,128)S(1)} %collective-permute-done.6.refs_4_, ...), custom_call_target="tpu_custom_call" | custom-call | tf_op jit(solution)/shard_map/scatter_back/pallas_call | solution.py:528
  (7 shorter events, 0.1 us)
Async XLA Ops:
  1.0 10.2 %collective-permute-start.3 = (f32[1,128]{1,0:T(1,128)S(1)}, f32[1,128]{1,0:T(1,128)S(1)}, u32[]{:S(2)}, u32[]{:S(2)}) collective-permute-start(f32[1,128]{1,0:T(1,128)S(1)} %get-tuple-element.37.refs_8_), channel_id=1, source_target_pairs={{0,1},{1,0},{2,3},{3,2},{4,5},{5,4},{6,7},{7,6},{8,9},{9,8},{10,11... | collective-permute-start | bytes 1544 | tf_op jit(solution)/shard_map/ppermute | solution.py:26
  1.5 7.2 %collective-permute-start = (f32[2,128]{1,0:T(2,128)S(1)}, f32[2,128]{1,0:T(2,128)S(1)}, u32[]{:S(2)}, u32[]{:S(2)}) collective-permute-start(f32[2,128]{1,0:T(2,128)S(1)} %get-tuple-element.34), channel_id=1, source_target_pairs={{0,8},{4,12},{16,24},{20,28},{8,0},{12,4},{24,16},{28,20},{1,9},{5... | collective-permute-start | bytes 3080 | tf_op jit(solution)/shard_map/ppermute | solution.py:21
  4.1 5.4 %collective-permute-start.1 = (f32[2,128]{1,0:T(2,128)S(1)}, f32[2,128]{1,0:T(2,128)S(1)}, u32[]{:S(2)}, u32[]{:S(2)}) collective-permute-start(f32[2,128]{1,0:T(2,128)S(1)} %get-tuple-element.35), channel_id=1, source_target_pairs={{8,16},{12,20},{24,0},{28,4},{16,8},{20,12},{0,24},{4,28},{9,17},{... | collective-permute-start | bytes 3080 | tf_op jit(solution)/shard_map/ppermute | solution.py:21
  9.5 3.6 %collective-permute-start.2 = (f32[2,128]{1,0:T(2,128)S(1)}, f32[2,128]{1,0:T(2,128)S(1)}, u32[]{:S(2)}, u32[]{:S(2)}) collective-permute-start(f32[2,128]{1,0:T(2,128)S(1)} %pad_maximum_fusion), channel_id=1, source_target_pairs={{0,4},{4,0},{8,12},{12,8},{16,20},{20,16},{24,28},{28,24},{1,5},{5... | collective-permute-start | bytes 3080 | tf_op jit(solution)/shard_map/ppermute | solution.py:26
  11.1 3.6 %collective-permute-start.4 = (f32[2,128]{1,0:T(2,128)S(1)}, f32[2,128]{1,0:T(2,128)S(1)}, u32[]{:S(2)}, u32[]{:S(2)}) collective-permute-start(f32[2,128]{1,0:T(2,128)S(1)} %pad_maximum_fusion.1), channel_id=1, source_target_pairs={{0,2},{1,3},{2,0},{3,1},{4,6},{5,7},{6,4},{7,5},{8,10},{9,11},{10,... | collective-permute-start | bytes 3080 | tf_op jit(solution)/shard_map/ppermute | solution.py:26
  15.7 4.0 %collective-permute-start.8 = (f32[2,128]{1,0:T(2,128)S(1)}, f32[2,128]{1,0:T(2,128)S(1)}, u32[]{:S(2)}, u32[]{:S(2)}) collective-permute-start(f32[2,128]{1,0:T(2,128)S(1)} %get-tuple-element.45), channel_id=1, source_target_pairs={{0,2},{1,3},{2,0},{3,1},{4,6},{5,7},{6,4},{7,5},{8,10},{9,11},{10,... | collective-permute-start | bytes 3080 | tf_op jit(solution)/shard_map/ppermute | solution.py:26
  17.2 3.6 %collective-permute-start.5 = (f32[2,128]{1,0:T(2,128)S(1)}, f32[2,128]{1,0:T(2,128)S(1)}, u32[]{:S(2)}, u32[]{:S(2)}) collective-permute-start(f32[2,128]{1,0:T(2,128)S(1)} %get-tuple-element.42), channel_id=1, source_target_pairs={{0,8},{4,12},{16,24},{20,28},{8,0},{12,4},{24,16},{28,20},{1,9},{5... | collective-permute-start | bytes 3080 | tf_op jit(solution)/shard_map/ppermute | solution.py:21
  17.2 5.4 %collective-permute-start.6 = (f32[2,128]{1,0:T(2,128)S(1)}, f32[2,128]{1,0:T(2,128)S(1)}, u32[]{:S(2)}, u32[]{:S(2)}) collective-permute-start(f32[2,128]{1,0:T(2,128)S(1)} %get-tuple-element.43), channel_id=1, source_target_pairs={{8,16},{12,20},{24,0},{28,4},{16,8},{20,12},{0,24},{4,28},{9,17},{... | collective-permute-start | bytes 3080 | tf_op jit(solution)/shard_map/ppermute | solution.py:21
  19.7 3.8 %collective-permute-start.9 = (f32[2,128]{1,0:T(2,128)S(1)}, f32[2,128]{1,0:T(2,128)S(1)}, u32[]{:S(2)}, u32[]{:S(2)}) collective-permute-start(f32[2,128]{1,0:T(2,128)S(1)} %pad_maximum_fusion.3), channel_id=1, source_target_pairs={{0,1},{1,0},{2,3},{3,2},{4,5},{5,4},{6,7},{7,6},{8,9},{9,8},{10,11... | collective-permute-start | bytes 3080 | tf_op jit(solution)/shard_map/ppermute | solution.py:26
  22.6 3.6 %collective-permute-start.7 = (f32[2,128]{1,0:T(2,128)S(1)}, f32[2,128]{1,0:T(2,128)S(1)}, u32[]{:S(2)}, u32[]{:S(2)}) collective-permute-start(f32[2,128]{1,0:T(2,128)S(1)} %pad_maximum_fusion.2), channel_id=1, source_target_pairs={{0,4},{4,0},{8,12},{12,8},{16,20},{20,16},{24,28},{28,24},{1,5},{5... | collective-permute-start | bytes 3080 | tf_op jit(solution)/shard_map/ppermute | solution.py:26

commit v6 on v5

--- a/solution.py
+++ b/solution.py
@@ -209,33 +209,35 @@
     )(live_faces, *in_hbm(heat2, corners, basis, area.reshape(tiles, LANES)))
 
 
-def class_sums(classes, blocks, prepared, remote_ref, hi_s, lo_s, sums_ref):
-    near_ref, off_ref, part_s, lane_s, basis_s, last_s, weight_ref = prepared
+def spread_row(ref, k, row, height):
+    return jnp.broadcast_to(ref[k, row : row + 1, :], (height, LANES)).astype(jnp.bfloat16)
+
+
+def lane_match(lane_ref, k, row):
+    match = spread_row(lane_ref, k, row, QUARTER) == iota((QUARTER, LANES), 0, jnp.float32).astype(jnp.bfloat16)
+    return jnp.where(match, jnp.ones(match.shape, jnp.bfloat16), jnp.zeros(match.shape, jnp.bfloat16))
+
+
+def contract(left, right):
+    return lax.dot_general(
+        jnp.concatenate(left, axis=1),
+        jnp.concatenate(right, axis=1),
+        (((1,), (1,)), ((), ())),
+        preferred_element_type=jnp.float32,
+    )
+
+
+def window_part(first, part_ref, hi_ref, lo_ref, k, row, kept):
+    want = (first + (iota((16, LANES), 0) & 7)).astype(jnp.float32).astype(jnp.bfloat16)
+    value = jnp.concatenate(
+        [jnp.broadcast_to(ref[k, kept : kept + 1, :], (8, LANES)) for ref in (hi_ref, lo_ref)], axis=0
+    ).astype(jnp.bfloat16)
+    return jnp.where(spread_row(part_ref, k, row, 16) == want, value, jnp.zeros((16, LANES), jnp.bfloat16))
+
+
+def class_terms(classes, blocks, prepared, remote_ref, hi_s, lo_s):
+    near_ref, off_ref, _, _, basis_s, last_s, weight_ref = prepared
     per_class = near_ref.shape[1] // blocks
-    lane_row = iota((QUARTER, LANES), 0, jnp.float32).astype(jnp.bfloat16)
-    part_row = iota((16, LANES), 0, jnp.float32).astype(jnp.bfloat16)
-    one = jnp.ones((QUARTER, LANES), jnp.bfloat16)
-    nil = jnp.zeros((QUARTER, LANES), jnp.bfloat16)
-
-    def spread_row(ref, k, row, height):
-        return jnp.broadcast_to(ref[k, row : row + 1, :], (height, LANES)).astype(jnp.bfloat16)
-
-    def tile_sums(row):
-        left, right = [], []
-        for k in range(3):
-            match = spread_row(part_s, k, row, 16) == part_row
-            a_hi = jnp.where(match, spread_row(hi_s, k, row - per_class * classes[0], 16), nil[:16])
-            a_lo = jnp.where(match, spread_row(lo_s, k, row - per_class * classes[0], 16), nil[:16])
-            left.append(jnp.concatenate([a_hi, a_lo], axis=0))
-            right.append(jnp.where(spread_row(lane_s, k, row, QUARTER) == lane_row, one, nil))
-        product = lax.dot_general(
-            jnp.concatenate(left, axis=1),
-            jnp.concatenate(right, axis=1),
-            (((1,), (1,)), ((), ())),
-            preferred_element_type=jnp.float32,
-        )
-        return product[:16] + product[16:]
-
     for r in classes:
         far_rows = [
             jnp.broadcast_to(remote_ref[2 * (r - classes[0]) + i : 2 * (r - classes[0]) + i + 1, :], (8, LANES))
@@ -263,16 +265,52 @@
                 hi = term.astype(jnp.bfloat16).astype(jnp.float32)
                 hi_s[k, kept, :] = hi
                 lo_s[k, kept, :] = term - hi
-    remote_sums = []
+
+
+def remote_sums(classes, per_class, part_ref, lane_ref, hi_s, lo_s):
+    found = []
+    for r in classes:
+        total = jnp.zeros((16, QUARTER), jnp.float32)
+        for i in range(0, per_class, 2):
+            rows = [(k, per_class * r + i + t) for t in range(2) for k in range(3)]
+            left = [window_part(8, part_ref, hi_s, lo_s, k, row, row - per_class * classes[0]) for k, row in rows]
+            total = total + contract(left, [lane_match(lane_ref, k, row) for k, row in rows])
+        found.append(total[:8] + total[8:])
+    return found
+
+
+def owned_sums(classes, blocks, per_class, part_ref, lane_ref, hi_ref, lo_ref, sums_s):
+    for r in classes:
+        for i in range(per_class):
+            row = per_class * r + i
+            kept = row - per_class * classes[0]
+            left = [window_part(0, part_ref, hi_ref, lo_ref, k, row, kept) for k in range(3)]
+            total = contract(left, [lane_match(lane_ref, k, row) for k in range(3)])
+            spot = 8 * (blocks * i + r) + 8
+            sums_s[spot : spot + 8, 0:QUARTER] = total[:8] + total[8:]
+
+
+def both_sums(classes, blocks, per_class, part_ref, lane_ref, hi_s, lo_s, sums_s):
+    part_row = iota((16, LANES), 0, jnp.float32).astype(jnp.bfloat16)
+    nil = jnp.zeros((16, LANES), jnp.bfloat16)
+    found = []
     for r in classes:
         remote_sum = jnp.zeros((8, QUARTER), jnp.float32)
         for i in range(per_class):
-            total = tile_sums(per_class * r + i)
+            row = per_class * r + i
+            kept = row - per_class * classes[0]
+            left = []
+            for k in range(3):
+                match = spread_row(part_ref, k, row, 16) == part_row
+                parts = [jnp.where(match, spread_row(ref, k, kept, 16), nil) for ref in (hi_s, lo_s)]
+                left.append(jnp.concatenate(parts, axis=0))
+            product = contract(left, [lane_match(lane_ref, k, row) for k in range(3)])
+            total = product[:16] + product[16:]
             spot = 8 * (blocks * i + r) + 8
-            sums_ref[spot : spot + 8, 0:QUARTER] = total[:8]
+            sums_s[spot : spot + 8, 0:QUARTER] = total[:8]
             remote_sum = remote_sum + total[8:]
-        remote_sums.append(remote_sum)
-    return remote_sums
+        found.append(remote_sum)
+    return found
 
 
 def full_rows(quarters):
@@ -285,8 +323,8 @@
 
 def patch_faces_kernel(classes, blocks, *refs):
     prepared, refs = refs[:7], refs[7:]
-    direct_ref, outer_ref, inner_ref, sums_out, near_out, outer_out, inner_out = refs[:7]
-    hi_s, lo_s, remote_ref = refs[7:]
+    direct_ref, outer_ref, inner_ref, hi_out, lo_out, near_out, outer_out, inner_out, remote_ref = refs
+    per_class = prepared[0].shape[1] // blocks
     odd = lax.axis_index("patch") & 1
     high = (lax.axis_index("patch") >> 1) & 1
     is_odd = jnp.broadcast_to(odd, (1, LANES)) == 1
@@ -298,7 +336,8 @@
     remote_ref[1:2, :] = below[0:1]
     remote_ref[2:3, :] = jnp.where(is_odd, relayed, direct)
     remote_ref[3:4, :] = above[0:1]
-    rows = full_rows(class_sums(classes, blocks, prepared, remote_ref, hi_s, lo_s, sums_out))
+    class_terms(classes, blocks, prepared, remote_ref, hi_out, lo_out)
+    rows = full_rows(remote_sums(classes, per_class, prepared[2], prepared[3], hi_out, lo_out))
     outer_out[0:1, :] = jnp.where(is_high, rows[3], rows[1])
     inner_out[0:1, :] = jnp.where(is_high, rows[1], rows[3])
     near_out[...] = jnp.where(is_odd, rows[0], rows[2])
@@ -308,7 +347,8 @@
 
 
 def group_faces_kernel(classes, blocks, group, *refs):
-    prepared, sums_ref, refs = refs[:7], refs[7], refs[8:]
+    prepared, patch_hi, patch_lo, refs = refs[:7], refs[7], refs[8], refs[9:]
+    per_class = prepared[0].shape[1] // blocks
     tiles = prepared[0].shape[1]
     bits = group.bit_length() - 1
     group_refs = refs[: bits + 1]
@@ -329,13 +369,15 @@
                 part = jnp.where(from_me >> bit == 1, got, part)
             parts.append(part)
         remote_ref[q : q + 1, :] = parts[0] if per_row == 1 else jnp.concatenate(parts, axis=1)
-    for t in range(tiles):
-        if t % blocks not in classes:
-            sums_s[8 * t + 8 : 8 * t + 16, :] = sums_ref[8 * t + 8 : 8 * t + 16, :]
     sums_s[0:8, :] = jnp.zeros((8, LANES), jnp.float32)
     sums_s[8 * tiles + 8 : 8 * tiles + 32, :] = jnp.zeros((24, LANES), jnp.float32)
-    for i, row in enumerate(full_rows(class_sums(classes, blocks, prepared, remote_ref, hi_s, lo_s, sums_s))):
+    class_terms(classes, blocks, prepared, remote_ref, hi_s, lo_s)
+    part_ref, lane_ref = prepared[2:4]
+    found = both_sums(classes, blocks, per_class, part_ref, lane_ref, hi_s, lo_s, sums_s)
+    for i, row in enumerate(full_rows(found)):
         remote_out[i : i + 1, :] = row
+    others = tuple(r for r in range(blocks) if r not in classes)
+    owned_sums(others, blocks, per_class, part_ref, lane_ref, patch_hi, patch_lo, sums_s)
     for i in range(group):
         owner = me ^ i
         row = read(remote_out, owner // per_row)
@@ -370,21 +412,22 @@
     return pl.pallas_call(
         lambda *refs: patch_faces_kernel(classes, blocks, *refs),
         out_shape=(
-            jax.ShapeDtypeStruct((8 * tiles + 32, LANES), f32),
+            jax.ShapeDtypeStruct(kept, f32),
+            jax.ShapeDtypeStruct(kept, f32),
             jax.ShapeDtypeStruct((1, LANES), f32),
             jax.ShapeDtypeStruct((2, LANES), f32),
             jax.ShapeDtypeStruct((2, LANES), f32),
         ),
         in_specs=[VMEM] * (len(prepared) + len(received)),
-        out_specs=(VMEM,) * 4,
-        scratch_shapes=[pltpu.VMEM(kept, f32), pltpu.VMEM(kept, f32), pltpu.VMEM((4, LANES), f32)],
+        out_specs=(VMEM,) * 5,
+        scratch_shapes=[pltpu.VMEM((4, LANES), f32)],
         cost_estimate=pl.CostEstimate(flops=COST[1], bytes_accessed=1 << 20, transcendentals=0),
         compiler_params=pltpu.CompilerParams(vmem_limit_bytes=6 * 2**20),
         name="patch_faces",
     )(*prepared, *received)
 
 
-def group_faces_call(prepared, blocks, sums, rows, group, group_size, held):
+def group_faces_call(prepared, blocks, patch_terms, rows, group, group_size, held):
     tiles = prepared[0].shape[1]
     bits = group.bit_length() - 1
     f32 = jnp.float32
@@ -397,7 +440,7 @@
             jax.ShapeDtypeStruct((rows, LANES), f32),
             *[jax.ShapeDtypeStruct((n, group_size), f32) for n in group_rows],
         ),
-        in_specs=[VMEM] * (len(prepared) + 1 + len(held)),
+        in_specs=[VMEM] * (len(prepared) + 2 + len(held)),
         out_specs=(VMEM,) * (bits + 2),
         scratch_shapes=[
             pltpu.VMEM(kept, f32),
@@ -409,7 +452,7 @@
         cost_estimate=pl.CostEstimate(flops=COST[1], bytes_accessed=1 << 20, transcendentals=0),
         compiler_params=pltpu.CompilerParams(vmem_limit_bytes=6 * 2**20),
         name="group_faces",
-    )(*prepared, sums, *held)
+    )(*prepared, *patch_terms, *held)
 
 
 def scatter_kernel(rows, bits, own_ref, sub_ref, pat_ref, direct_ref, outer_ref, inner_ref, *refs):
@@ -509,8 +552,8 @@
     for bit in range(bits):
         held.append(swap(stack(held), "sub", 1 << bit))
 
-    sums, near, outer, inner = patch_faces_call(prepared, blocks, (direct, outer, inner))
-    own_sums, keep, *outs = group_faces_call(prepared, blocks, sums, rows, group, group_size, held)
+    *patch_terms, near, outer, inner = patch_faces_call(prepared, blocks, (direct, outer, inner))
+    own_sums, keep, *outs = group_faces_call(prepared, blocks, patch_terms, rows, group, group_size, held)
 
     outer = swap_far(outer, "patch", True)
     inner = swap_far(inner, "patch", False)

time: 27.3 us -> 27.8 us (1.018)
  Pallas kernels: 4.97 us -> 5.35 us
    pallas_call x1, Pallas kernels: 0.91 us -> 1.43 us  [group_faces_call(): pl.pallas_call(lambda *refs: group_faces_kernel(classes, blocks, group, *...]
where the time goes in v6:
time: 27.8 us; the launch traced here: 27.6 us
  starting transfers between devices  13.6 us (49%)
  waiting for transfers between devices  7.88 us (28%)
  Pallas kernels  5.35 us (19%)
  between operations  0.7 us (3%)
    ppermute x4, starting transfers between devices, swap_far(): lax.ppermute(x, axis, [(i, (i + 2) % n) for i in low] + [((i + 2) % n, i)...  7.59 us
    ppermute x6, starting transfers between devices, swap(): return lax.ppermute(x, axis, [(i, i ^ bit) for i in range(n)])  6.02 us
    ppermute x6, waiting for transfers between devices, swap(): return lax.ppermute(x, axis, [(i, i ^ bit) for i in range(n)])  4.26 us
    ppermute x4, waiting for transfers between devices, swap_far(): lax.ppermute(x, axis, [(i, (i + 2) % n) for i in low] + [((i + 2) % n, i)...  3.62 us
    pallas_call x1, Pallas kernels, group_faces_call(): pl.pallas_call(lambda *refs: group_faces_kernel(classes, blocks, group, *...  1.43 us
    pallas_call x1, Pallas kernels, prepare_call(): pl.pallas_call(lambda *refs: prepare_kernel(rows * LANES, tiles, blocks,...  1.41 us
    pallas_call x1, Pallas kernels, per_device(): pl.pallas_call(lambda *refs: send_kernel(rows, *refs), out_shape=(jax.Sha...  0.94 us
    pallas_call x1, Pallas kernels, per_device(): pl.pallas_call(lambda *refs: scatter_kernel(rows, bits, *refs), out_shape...  0.84 us
  transfers between devices with their start and end apart: 10, of which 6 were waited for; matrix products, arithmetic and copies ran while one was open for 0% of the time, Pallas kernels for 8%

profile of v6, /device:TPU:0, one launch (start us, length us, event | category | flops | bytes accessed | tf_op | source)
XLA Modules:
  0.0 27.6 jit_solution(4886698610915119790)
XLA Ops:
  0.0 0.9 %send_gather.1 = (f32[1,128]{1,0:T(1,128)S(1)}, f32[1,128]{1,0:T(1,128)S(1)}, f32[2,128]{1,0:T(2,128)S(1)}, f32[2,128]{1,0:T(2,128)S(1)}, s32[1,128]{1,0:T(1,128)S(1)}, /*index=5*/s32[4,128]{1,0:T(4,128)S(1)}) custom-call(f32[64,128]{1,0:T(8,128)} %bitcast.4, s32[1,128]{1,0:T(1,128)} %bitcast.7, s32[4,128]{1,0:T(4,128)} %refs_2_.3), custom_call_target="tpu_custom_call" | custom-call | tf_op jit(solution)/shard_map/send_gather/pallas_call | solution.py:524
  1.0 0.6 %collective-permute-start.3 = (f32[1,128]{1,0:T(1,128)S(1)}, f32[1,128]{1,0:T(1,128)S(1)}, u32[]{:S(2)}, u32[]{:S(2)}) collective-permute-start(f32[1,128]{1,0:T(1,128)S(1)} %get-tuple-element.39.refs_9_), channel_id=1, source_target_pairs={{0,1},{1,0},{2,3},{3,2},{4,5},{5,4},{6,7},{7,6},{8,9},{9,8},{10,11... | collective-permute-start | bytes 1544 | tf_op jit(solution)/shard_map/ppermute | solution.py:26
  1.5 2.6 %collective-permute-start = (f32[2,128]{1,0:T(2,128)S(1)}, f32[2,128]{1,0:T(2,128)S(1)}, u32[]{:S(2)}, u32[]{:S(2)}) collective-permute-start(f32[2,128]{1,0:T(2,128)S(1)} %get-tuple-element.35), channel_id=1, source_target_pairs={{0,8},{4,12},{16,24},{20,28},{8,0},{12,4},{24,16},{28,20},{1,9},{5... | collective-permute-start | bytes 3080 | tf_op jit(solution)/shard_map/ppermute | solution.py:21
  4.1 2.5 %collective-permute-start.1 = (f32[2,128]{1,0:T(2,128)S(1)}, f32[2,128]{1,0:T(2,128)S(1)}, u32[]{:S(2)}, u32[]{:S(2)}) collective-permute-start(f32[2,128]{1,0:T(2,128)S(1)} %get-tuple-element.36), channel_id=1, source_target_pairs={{8,16},{12,20},{24,0},{28,4},{16,8},{20,12},{0,24},{4,28},{9,17},{... | collective-permute-start | bytes 3080 | tf_op jit(solution)/shard_map/ppermute | solution.py:21
  7.3 1.4 %prepare.1 = (f32[3,128,128]{2,1,0:T(8,128)S(1)}, s32[3,128,128]{2,1,0:T(8,128)S(1)}, f32[3,128,128]{2,1,0:T(8,128)S(1)}, f32[3,128,128]{2,1,0:T(8,128)S(1)}, f3...) custom-call(s32[1]{0:T(128)S(6)} %copy.8.refs_0_, f32[64,128]{1,0:T(8,128)} %bitcast.5, ...), custom_call_target="tpu_custom_call" | custom-call | flops 16777216 | bytes 1048576 | tf_op jit(solution)/shard_map/prepare/pallas_call | solution.py:184
  8.7 0.0 collective-permute-done.refs_9_
  8.7 0.8 %collective-permute-done.1.refs_8_ = f32[2,128]{1,0:T(2,128)S(1)} collective-permute-done((f32[2,128]{1,0:T(2,128)S(1)}, f32[2,128]{1,0:T(2,128)S(1)}, u32[]{:S(2)}, u32[]{:S(2)}) %collective-permute-start.1) | collective-permute-done | bytes 1056 | tf_op jit(solution)/shard_map/ppermute | solution.py:21
  9.5 1.6 %collective-permute-start.2 = (f32[2,128]{1,0:T(2,128)S(1)}, f32[2,128]{1,0:T(2,128)S(1)}, u32[]{:S(2)}, u32[]{:S(2)}) collective-permute-start(f32[2,128]{1,0:T(2,128)S(1)} %pad_maximum_fusion), channel_id=1, source_target_pairs={{0,4},{4,0},{8,12},{12,8},{16,20},{20,16},{24,28},{28,24},{1,5},{5... | collective-permute-start | bytes 3080 | tf_op jit(solution)/shard_map/ppermute | solution.py:26
  11.1 0.0 collective-permute-done.3.refs_10_
  11.1 1.6 %collective-permute-start.4 = (f32[2,128]{1,0:T(2,128)S(1)}, f32[2,128]{1,0:T(2,128)S(1)}, u32[]{:S(2)}, u32[]{:S(2)}) collective-permute-start(f32[2,128]{1,0:T(2,128)S(1)} %pad_maximum_fusion.1), channel_id=1, source_target_pairs={{0,2},{1,3},{2,0},{3,1},{4,6},{5,7},{6,4},{7,5},{8,10},{9,11},{10,... | collective-permute-start | bytes 3080 | tf_op jit(solution)/shard_map/ppermute | solution.py:26
  12.7 0.5 %collective-permute-done.2.refs_7_ = f32[2,128]{1,0:T(2,128)S(1)} collective-permute-done((f32[2,128]{1,0:T(2,128)S(1)}, f32[2,128]{1,0:T(2,128)S(1)}, u32[]{:S(2)}, u32[]{:S(2)}) %collective-permute-start.2) | collective-permute-done | bytes 1056 | tf_op jit(solution)/shard_map/ppermute | solution.py:26
  13.2 0.7 %patch_faces.1 = (f32[3,64,128]{2,1,0:T(8,128)S(1)}, f32[3,64,128]{2,1,0:T(8,128)S(1)}, f32[1,128]{1,0:T(1,128)S(1)}, f32[2,128]{1,0:T(2,128)S(1)}, f32[2,128]{1,0:T(2,128)S(1)}) custom-call(f32[3,128,128]{2,1,0:T(8,128)S(1)} %get-tuple-element.27.refs_0_, s32[3,128,128]{2,1,0:T(8,128)S(1)} %get-tuple-element.28.refs_1_, ...), custom_call_target="tpu_custom_call" | custom-call | flops 16777216 | bytes 1048576 | tf_op jit(solution)/shard_map/patch_faces/pallas_call | solution.py:412
  13.9 0.9 %collective-permute-done.4.refs_11_ = f32[2,128]{1,0:T(2,128)S(1)} collective-permute-done((f32[2,128]{1,0:T(2,128)S(1)}, f32[2,128]{1,0:T(2,128)S(1)}, u32[]{:S(2)}, u32[]{:S(2)}) %collective-permute-start.4) | collective-permute-done | bytes 1056 | tf_op jit(solution)/shard_map/ppermute | solution.py:26
  14.8 1.4 %group_faces.1 = (f32[64,128]{1,0:T(8,128)S(1)}, f32[1,128]{1,0:T(1,128)S(1)}, f32[1,128]{1,0:T(1,128)S(1)}, f32[2,128]{1,0:T(2,128)S(1)}) custom-call(f32[3,128,128]{2,1,0:T(8,128)S(1)} %get-tuple-element.27.refs_0_, s32[3,128,128]{2,1,0:T(8,128)S(1)} %get-tuple-element.28.refs_1_, f32[3,128,128]{2,1,0:T(8,128)S(1)} %get-tuple-element.29.refs_2_, ...), custom_call_target="tpu_custom_call" | custom-call | flops 16777216 | bytes 1048576 | tf_op jit(solution)/shard_map/group_faces/pallas_call | solution.py:437
  16.2 1.5 %collective-permute-start.8 = (f32[2,128]{1,0:T(2,128)S(1)}, f32[2,128]{1,0:T(2,128)S(1)}, u32[]{:S(2)}, u32[]{:S(2)}) collective-permute-start(f32[2,128]{1,0:T(2,128)S(1)} %get-tuple-element.47), channel_id=1, source_target_pairs={{0,2},{1,3},{2,0},{3,1},{4,6},{5,7},{6,4},{7,5},{8,10},{9,11},{10,... | collective-permute-start | bytes 3080 | tf_op jit(solution)/shard_map/ppermute | solution.py:26
  17.7 0.0 collective-permute-start.5
  17.7 2.5 %collective-permute-start.6 = (f32[2,128]{1,0:T(2,128)S(1)}, f32[2,128]{1,0:T(2,128)S(1)}, u32[]{:S(2)}, u32[]{:S(2)}) collective-permute-start(f32[2,128]{1,0:T(2,128)S(1)} %get-tuple-element.45), channel_id=1, source_target_pairs={{8,16},{12,20},{24,0},{28,4},{16,8},{20,12},{0,24},{4,28},{9,17},{... | collective-permute-start | bytes 3080 | tf_op jit(solution)/shard_map/ppermute | solution.py:21
  20.2 0.0 collective-permute-done.8.refs_7_
  20.2 0.1 collective-permute-start.9
  20.3 1.0 %collective-permute-done.5.refs_5_ = f32[2,128]{1,0:T(2,128)S(1)} collective-permute-done((f32[2,128]{1,0:T(2,128)S(1)}, f32[2,128]{1,0:T(2,128)S(1)}, u32[]{:S(2)}, u32[]{:S(2)}) %collective-permute-start.5) | collective-permute-done | bytes 1056 | tf_op jit(solution)/shard_map/ppermute | solution.py:21
  21.3 1.8 %collective-permute-done.6.refs_4_ = f32[2,128]{1,0:T(2,128)S(1)} collective-permute-done((f32[2,128]{1,0:T(2,128)S(1)}, f32[2,128]{1,0:T(2,128)S(1)}, u32[]{:S(2)}, u32[]{:S(2)}) %collective-permute-start.6) | collective-permute-done | bytes 1056 | tf_op jit(solution)/shard_map/ppermute | solution.py:21
  23.1 0.7 %collective-permute-start.7 = (f32[2,128]{1,0:T(2,128)S(1)}, f32[2,128]{1,0:T(2,128)S(1)}, u32[]{:S(2)}, u32[]{:S(2)}) collective-permute-start(f32[2,128]{1,0:T(2,128)S(1)} %pad_maximum_fusion.2), channel_id=1, source_target_pairs={{0,4},{4,0},{8,12},{12,8},{16,20},{20,16},{24,28},{28,24},{1,5},{5... | collective-permute-start | bytes 3080 | tf_op jit(solution)/shard_map/ppermute | solution.py:26
  23.8 0.0 collective-permute-done.9.refs_8_
  23.9 2.9 %collective-permute-done.7.refs_3_ = f32[2,128]{1,0:T(2,128)S(1)} collective-permute-done((f32[2,128]{1,0:T(2,128)S(1)}, f32[2,128]{1,0:T(2,128)S(1)}, u32[]{:S(2)}, u32[]{:S(2)}) %collective-permute-start.7) | collective-permute-done | bytes 1056 | tf_op jit(solution)/shard_map/ppermute | solution.py:26
  26.7 0.8 %scatter_back.1 = f32[64,128]{1,0:T(8,128)} custom-call(f32[64,128]{1,0:T(8,128)S(1)} %get-tuple-element.40.refs_0_, s32[1,128]{1,0:T(1,128)S(1)} %get-tuple-element.41.refs_1_, s32[4,128]{1,0:T(4,128)S(1)} %get-tuple-element.42.refs_2_, f32[2,128]{1,0:T(2,128)S(1)} %collective-permute-done.7.refs_3_, f32[2,128]{1,0:T(2,128)S(1)} %collective-permute-done.6.refs_4_, ...), custom_call_target="tpu_custom_call" | custom-call | tf_op jit(solution)/shard_map/scatter_back/pallas_call | solution.py:571
  (7 shorter events, 0.1 us)
Async XLA Ops:
  1.0 10.2 %collective-permute-start.3 = (f32[1,128]{1,0:T(1,128)S(1)}, f32[1,128]{1,0:T(1,128)S(1)}, u32[]{:S(2)}, u32[]{:S(2)}) collective-permute-start(f32[1,128]{1,0:T(1,128)S(1)} %get-tuple-element.39.refs_9_), channel_id=1, source_target_pairs={{0,1},{1,0},{2,3},{3,2},{4,5},{5,4},{6,7},{7,6},{8,9},{9,8},{10,11... | collective-permute-start | bytes 1544 | tf_op jit(solution)/shard_map/ppermute | solution.py:26
  1.5 7.2 %collective-permute-start = (f32[2,128]{1,0:T(2,128)S(1)}, f32[2,128]{1,0:T(2,128)S(1)}, u32[]{:S(2)}, u32[]{:S(2)}) collective-permute-start(f32[2,128]{1,0:T(2,128)S(1)} %get-tuple-element.35), channel_id=1, source_target_pairs={{0,8},{4,12},{16,24},{20,28},{8,0},{12,4},{24,16},{28,20},{1,9},{5... | collective-permute-start | bytes 3080 | tf_op jit(solution)/shard_map/ppermute | solution.py:21
  4.1 5.4 %collective-permute-start.1 = (f32[2,128]{1,0:T(2,128)S(1)}, f32[2,128]{1,0:T(2,128)S(1)}, u32[]{:S(2)}, u32[]{:S(2)}) collective-permute-start(f32[2,128]{1,0:T(2,128)S(1)} %get-tuple-element.36), channel_id=1, source_target_pairs={{8,16},{12,20},{24,0},{28,4},{16,8},{20,12},{0,24},{4,28},{9,17},{... | collective-permute-start | bytes 3080 | tf_op jit(solution)/shard_map/ppermute | solution.py:21
  9.5 3.6 %collective-permute-start.2 = (f32[2,128]{1,0:T(2,128)S(1)}, f32[2,128]{1,0:T(2,128)S(1)}, u32[]{:S(2)}, u32[]{:S(2)}) collective-permute-start(f32[2,128]{1,0:T(2,128)S(1)} %pad_maximum_fusion), channel_id=1, source_target_pairs={{0,4},{4,0},{8,12},{12,8},{16,20},{20,16},{24,28},{28,24},{1,5},{5... | collective-permute-start | bytes 3080 | tf_op jit(solution)/shard_map/ppermute | solution.py:26
  11.1 3.6 %collective-permute-start.4 = (f32[2,128]{1,0:T(2,128)S(1)}, f32[2,128]{1,0:T(2,128)S(1)}, u32[]{:S(2)}, u32[]{:S(2)}) collective-permute-start(f32[2,128]{1,0:T(2,128)S(1)} %pad_maximum_fusion.1), channel_id=1, source_target_pairs={{0,2},{1,3},{2,0},{3,1},{4,6},{5,7},{6,4},{7,5},{8,10},{9,11},{10,... | collective-permute-start | bytes 3080 | tf_op jit(solution)/shard_map/ppermute | solution.py:26
  16.2 4.0 %collective-permute-start.8 = (f32[2,128]{1,0:T(2,128)S(1)}, f32[2,128]{1,0:T(2,128)S(1)}, u32[]{:S(2)}, u32[]{:S(2)}) collective-permute-start(f32[2,128]{1,0:T(2,128)S(1)} %get-tuple-element.47), channel_id=1, source_target_pairs={{0,2},{1,3},{2,0},{3,1},{4,6},{5,7},{6,4},{7,5},{8,10},{9,11},{10,... | collective-permute-start | bytes 3080 | tf_op jit(solution)/shard_map/ppermute | solution.py:26
  17.7 3.6 %collective-permute-start.5 = (f32[2,128]{1,0:T(2,128)S(1)}, f32[2,128]{1,0:T(2,128)S(1)}, u32[]{:S(2)}, u32[]{:S(2)}) collective-permute-start(f32[2,128]{1,0:T(2,128)S(1)} %get-tuple-element.44), channel_id=1, source_target_pairs={{0,8},{4,12},{16,24},{20,28},{8,0},{12,4},{24,16},{28,20},{1,9},{5... | collective-permute-start | bytes 3080 | tf_op jit(solution)/shard_map/ppermute | solution.py:21
  17.7 5.4 %collective-permute-start.6 = (f32[2,128]{1,0:T(2,128)S(1)}, f32[2,128]{1,0:T(2,128)S(1)}, u32[]{:S(2)}, u32[]{:S(2)}) collective-permute-start(f32[2,128]{1,0:T(2,128)S(1)} %get-tuple-element.45), channel_id=1, source_target_pairs={{8,16},{12,20},{24,0},{28,4},{16,8},{20,12},{0,24},{4,28},{9,17},{... | collective-permute-start | bytes 3080 | tf_op jit(solution)/shard_map/ppermute | solution.py:21
  20.2 3.6 %collective-permute-start.9 = (f32[2,128]{1,0:T(2,128)S(1)}, f32[2,128]{1,0:T(2,128)S(1)}, u32[]{:S(2)}, u32[]{:S(2)}) collective-permute-start(f32[2,128]{1,0:T(2,128)S(1)} %pad_maximum_fusion.3), channel_id=1, source_target_pairs={{0,1},{1,0},{2,3},{3,2},{4,5},{5,4},{6,7},{7,6},{8,9},{9,8},{10,11... | collective-permute-start | bytes 3080 | tf_op jit(solution)/shard_map/ppermute | solution.py:26
  23.1 3.6 %collective-permute-start.7 = (f32[2,128]{1,0:T(2,128)S(1)}, f32[2,128]{1,0:T(2,128)S(1)}, u32[]{:S(2)}, u32[]{:S(2)}) collective-permute-start(f32[2,128]{1,0:T(2,128)S(1)} %pad_maximum_fusion.2), channel_id=1, source_target_pairs={{0,4},{4,0},{8,12},{12,8},{16,20},{20,16},{24,28},{28,24},{1,5},{5... | collective-permute-start | bytes 3080 | tf_op jit(solution)/shard_map/ppermute | solution.py:26

commit v7 on v6

--- a/solution.py
+++ b/solution.py
@@ -21,9 +21,26 @@
     return lax.ppermute(x, axis, [(i, (i + 2) % n) for i in low] + [((i + 2) % n, i) for i in low])
 
 
-def swap(x, axis, bit):
+def swap(x, axis, mask):
     n = lax.axis_size(axis)
-    return lax.ppermute(x, axis, [(i, i ^ bit) for i in range(n)])
+    return lax.ppermute(x, axis, [(i, i ^ mask) for i in range(n)])
+
+
+def mask_of(bit):
+    return (2 << bit) - 1
+
+
+def owner_of(i):
+    mask, bit = 0, 0
+    while i >> bit:
+        mask ^= mask_of(bit) if i >> bit & 1 else 0
+        bit += 1
+    return mask
+
+
+def shift(x, axis, by):
+    n = lax.axis_size(axis)
+    return lax.ppermute(x, axis, [(i, (i + by) % n) for i in range(n)])
 
 
 def iota(shape, dim, dtype=jnp.int32):
@@ -47,22 +64,25 @@
     ]
     for copy in copies:
         copy.start()
-    for copy in copies:
-        copy.wait()
+    copies[1].wait()
+    copies[2].wait()
     blocks = rows // 8
     sub_iota = iota((8, LANES), 0)
     odd = lax.axis_index("patch") & 1
-    high = (lax.axis_index("patch") >> 1) & 1
+    wanted = []
     for j in range(5):
         if j == 0:
             index = sub_ref[0:1, :]
         else:
-            index = read(pat_ref, (3 - 2 * high, 1 + 2 * high, 2 * odd, 2 - 2 * odd)[j - 1])
+            index = read(pat_ref, (1, 3, 2 * odd, 2 - 2 * odd)[j - 1])
         index = jnp.broadcast_to(index, (8, index.shape[1]))
         if index.shape[1] < LANES:
             index = jnp.concatenate([index] * (LANES // index.shape[1]), axis=1)
         lane = index & (LANES - 1)
         row = index >> 7
+        wanted.append((lane, row))
+    copies[0].wait()
+    for j, (lane, row) in enumerate(wanted):
         total = jnp.zeros((8, LANES), jnp.float32)
         for a in range(blocks):
             got = lane_gather(heat_ref[8 * a : 8 * a + 8, :], lane)
@@ -330,7 +350,7 @@
     is_odd = jnp.broadcast_to(odd, (1, LANES)) == 1
     is_high = jnp.broadcast_to(high, (1, LANES)) == 1
     direct = direct_ref[0:1, :]
-    below, above = by_side(high, outer_ref, inner_ref)
+    below, above = outer_ref[...], inner_ref[...]
     relayed = direct_ref[1:2, :]
     remote_ref[0:1, :] = jnp.where(is_odd, direct, relayed)
     remote_ref[1:2, :] = below[0:1]
@@ -363,6 +383,7 @@
         parts = []
         for e in range(per_row):
             from_me = me ^ (q * per_row + e)
+            from_me = from_me ^ (from_me >> 1)
             part = group_refs[0][...]
             for bit in range(bits):
                 got = read(group_refs[bit + 1], from_me & ((1 << bit) - 1))
@@ -379,7 +400,7 @@
     others = tuple(r for r in range(blocks) if r not in classes)
     owned_sums(others, blocks, per_class, part_ref, lane_ref, patch_hi, patch_lo, sums_s)
     for i in range(group):
-        owner = me ^ i
+        owner = me ^ owner_of(i)
         row = read(remote_out, owner // per_row)
         if per_row > 1:
             turn = (LANES - (owner % per_row) * group_size) % LANES
@@ -513,9 +534,10 @@
     block_size = send_pat.shape[1]
     offsets = send_pat.shape[0]
     remote_len = group * group_size + offsets * block_size
+    blocks = remote_len // (2 * LANES)
     assert offsets == 4 and block_size == LANES and LANES % group_size == 0
     assert group & (group - 1) == 0 and group * group_size % (2 * LANES) == 0
-    assert lax.axis_size("patch") % 4 == 0
+    assert lax.axis_size("patch") % 4 == 0 and corners.shape[1] % (8 * blocks * LANES) == 0
     bits = group.bit_length() - 1
     f32 = jnp.float32
     heat2 = heat.reshape(rows, LANES)
@@ -540,17 +562,16 @@
         compiler_params=pltpu.CompilerParams(vmem_limit_bytes=2 * 2**20),
         name="send_gather",
     )(*in_hbm(heat2, sub2, send_pat))
-    blocks = remote_len // (2 * LANES)
     prepared = prepare_call(live_faces, heat2, corners, basis, area, blocks)
     place = lax.axis_index("patch")
     take_inner = ((place >> 1) & 1) == (place & 1)
-    outer = swap_far(outer, "patch", True)
-    inner = swap_far(inner, "patch", False)
-    relay = jnp.where(take_inner, inner[1:2], outer[1:2])
+    outer = shift(outer, "patch", 2)
+    inner = shift(inner, "patch", -2)
+    relay = jnp.where((place & 1) == 0, inner[1:2], outer[1:2])
     direct = swap(jnp.concatenate([near, relay]), "patch", 1)
     held = [mine]
     for bit in range(bits):
-        held.append(swap(stack(held), "sub", 1 << bit))
+        held.append(swap(stack(held), "sub", mask_of(bit)))
 
     *patch_terms, near, outer, inner = patch_faces_call(prepared, blocks, (direct, outer, inner))
     own_sums, keep, *outs = group_faces_call(prepared, blocks, patch_terms, rows, group, group_size, held)
@@ -562,7 +583,7 @@
     pieces, group_back = [], []
     for bit in reversed(range(bits)):
         width = 1 << bit
-        got = swap(stack([outs[bit]] + [p[width : 2 * width] for p in pieces]), "sub", width)
+        got = swap(stack([outs[bit]] + [p[width : 2 * width] for p in pieces]), "sub", mask_of(bit))
         group_back.append(got)
         pieces = [p[:width] for p in pieces] + [
             got[at : at + width] for at in range(0, got.shape[0], width)

time: 27.8 us -> 27.9 us (level)
  waiting for transfers between devices: 7.88 us -> 12 us
  starting transfers between devices: 13.6 us -> 9.6 us
    ppermute x4 -> x2, starting transfers between devices: 7.59 us -> 1.07 us  [swap_far(): lax.ppermute(x, axis, [(i, (i + 2) % n) for i in low] + [((i + 2) % n, i)...]
    ppermute x6 -> x8, waiting for transfers between devices: 4.26 us -> 9.65 us  [the longest x6 6.36 us: swap(): return lax.ppermute(x, axis, [(i, i ^ mask) for i in range(n)])]
    ppermute x6 -> x8, starting transfers between devices: 6.02 us -> 8.53 us  [the longest x2 4.65 us: shift(): return lax.ppermute(x, axis, [(i, (i + by) % n) for i in range(n)])]
    ppermute x4 -> x2, waiting for transfers between devices: 3.62 us -> 2.37 us  [swap_far(): lax.ppermute(x, axis, [(i, (i + 2) % n) for i in low] + [((i + 2) % n, i)...]
  transfers between devices with their start and end apart: 10 -> 10, of which waited for: 6 -> 7; matrix products, arithmetic and copies ran while one was open for 0% -> 0% of each run, Pallas kernels for 8% -> 8%
where the time goes in v7:
time: 27.9 us; the launch traced here: 27.7 us
  waiting for transfers between devices  12 us (43%)
  starting transfers between devices  9.6 us (34%)
  Pallas kernels  5.33 us (19%)
  between operations  0.7 us (3%)
    ppermute x6, waiting for transfers between devices, swap(): return lax.ppermute(x, axis, [(i, i ^ mask) for i in range(n)])  6.36 us
    ppermute x2, starting transfers between devices, shift(): return lax.ppermute(x, axis, [(i, (i + by) % n) for i in range(n)])  4.65 us
    ppermute x6, starting transfers between devices, swap(): return lax.ppermute(x, axis, [(i, i ^ mask) for i in range(n)])  3.88 us
    ppermute x2, waiting for transfers between devices, shift(): return lax.ppermute(x, axis, [(i, (i + by) % n) for i in range(n)])  3.29 us
    ppermute x2, waiting for transfers between devices, swap_far(): lax.ppermute(x, axis, [(i, (i + 2) % n) for i in low] + [((i + 2) % n, i)...  2.37 us
    pallas_call x1, Pallas kernels, group_faces_call(): pl.pallas_call(lambda *refs: group_faces_kernel(classes, blocks, group, *...  1.43 us
    pallas_call x1, Pallas kernels, prepare_call(): pl.pallas_call(lambda *refs: prepare_kernel(rows * LANES, tiles, blocks,...  1.41 us
    ppermute x2, starting transfers between devices, swap_far(): lax.ppermute(x, axis, [(i, (i + 2) % n) for i in low] + [((i + 2) % n, i)...  1.07 us
  transfers between devices with their start and end apart: 10, of which 7 were waited for; matrix products, arithmetic and copies ran while one was open for 0% of the time, Pallas kernels for 8%

profile of v7, /device:TPU:0, one launch (start us, length us, event | category | flops | bytes accessed | tf_op | source)
XLA Modules:
  0.0 27.7 jit_solution(946637643412871026)
XLA Ops:
  0.0 0.9 %send_gather.1 = (f32[1,128]{1,0:T(1,128)S(1)}, f32[1,128]{1,0:T(1,128)S(1)}, f32[2,128]{1,0:T(2,128)S(1)}, f32[2,128]{1,0:T(2,128)S(1)}, s32[1,128]{1,0:T(1,128)S(1)}, /*index=5*/s32[4,128]{1,0:T(4,128)S(1)}) custom-call(f32[64,128]{1,0:T(8,128)} %bitcast.4, s32[1,128]{1,0:T(1,128)} %bitcast.7, s32[4,128]{1,0:T(4,128)} %refs_2_.3), custom_call_target="tpu_custom_call" | custom-call | tf_op jit(solution)/shard_map/send_gather/pallas_call | solution.py:546
  0.9 0.6 %collective-permute-start.3 = (f32[1,128]{1,0:T(1,128)S(1)}, f32[1,128]{1,0:T(1,128)S(1)}, u32[]{:S(2)}, u32[]{:S(2)}) collective-permute-start(f32[1,128]{1,0:T(1,128)S(1)} %get-tuple-element.39.refs_9_), channel_id=1, source_target_pairs={{0,1},{1,0},{2,3},{3,2},{4,5},{5,4},{6,7},{7,6},{8,9},{9,8},{10,11... | collective-permute-start | bytes 1544 | tf_op jit(solution)/shard_map/ppermute | solution.py:26
  1.5 4.7 %collective-permute-start = (f32[2,128]{1,0:T(2,128)S(1)}, f32[2,128]{1,0:T(2,128)S(1)}, u32[]{:S(2)}, u32[]{:S(2)}) collective-permute-start(f32[2,128]{1,0:T(2,128)S(1)} %get-tuple-element.35), channel_id=1, source_target_pairs={{0,24},{4,28},{8,0},{12,4},{16,8},{20,12},{24,16},{28,20},{1,25},{... | collective-permute-start | bytes 3080 | tf_op jit(solution)/shard_map/ppermute | solution.py:43
  6.2 0.0 collective-permute-start.1
  6.8 1.4 %prepare.1 = (f32[3,128,128]{2,1,0:T(8,128)S(1)}, s32[3,128,128]{2,1,0:T(8,128)S(1)}, f32[3,128,128]{2,1,0:T(8,128)S(1)}, f32[3,128,128]{2,1,0:T(8,128)S(1)}, f3...) custom-call(s32[1]{0:T(128)S(6)} %copy.8.refs_0_, f32[64,128]{1,0:T(8,128)} %bitcast.5, ...), custom_call_target="tpu_custom_call" | custom-call | flops 16777216 | bytes 1048576 | tf_op jit(solution)/shard_map/prepare/pallas_call | solution.py:204
  8.2 0.0 collective-permute-done.refs_9_
  8.2 3.3 %collective-permute-done.1.refs_8_ = f32[2,128]{1,0:T(2,128)S(1)} collective-permute-done((f32[2,128]{1,0:T(2,128)S(1)}, f32[2,128]{1,0:T(2,128)S(1)}, u32[]{:S(2)}, u32[]{:S(2)}) %collective-permute-start.1) | collective-permute-done | bytes 1056 | tf_op jit(solution)/shard_map/ppermute | solution.py:43
  11.5 1.6 %collective-permute-start.2 = (f32[2,128]{1,0:T(2,128)S(1)}, f32[2,128]{1,0:T(2,128)S(1)}, u32[]{:S(2)}, u32[]{:S(2)}) collective-permute-start(f32[2,128]{1,0:T(2,128)S(1)} %pad_maximum_fusion), channel_id=1, source_target_pairs={{0,4},{4,0},{8,12},{12,8},{16,20},{20,16},{24,28},{28,24},{1,5},{5... | collective-permute-start | bytes 3080 | tf_op jit(solution)/shard_map/ppermute | solution.py:26
  13.1 0.0 collective-permute-done.3.refs_10_
  13.1 0.1 collective-permute-start.4
  13.2 2.0 %collective-permute-done.2.refs_7_ = f32[2,128]{1,0:T(2,128)S(1)} collective-permute-done((f32[2,128]{1,0:T(2,128)S(1)}, f32[2,128]{1,0:T(2,128)S(1)}, u32[]{:S(2)}, u32[]{:S(2)}) %collective-permute-start.2) | collective-permute-done | bytes 1056 | tf_op jit(solution)/shard_map/ppermute | solution.py:26
  15.2 0.7 %patch_faces.1 = (f32[3,64,128]{2,1,0:T(8,128)S(1)}, f32[3,64,128]{2,1,0:T(8,128)S(1)}, f32[1,128]{1,0:T(1,128)S(1)}, f32[2,128]{1,0:T(2,128)S(1)}, f32[2,128]{1,0:T(2,128)S(1)}) custom-call(f32[3,128,128]{2,1,0:T(8,128)S(1)} %get-tuple-element.27.refs_0_, s32[3,128,128]{2,1,0:T(8,128)S(1)} %get-tuple-element.28.refs_1_, ...), custom_call_target="tpu_custom_call" | custom-call | flops 16777216 | bytes 1048576 | tf_op jit(solution)/shard_map/patch_faces/pallas_call | solution.py:433
  15.9 0.3 %collective-permute-done.4.refs_11_ = f32[2,128]{1,0:T(2,128)S(1)} collective-permute-done((f32[2,128]{1,0:T(2,128)S(1)}, f32[2,128]{1,0:T(2,128)S(1)}, u32[]{:S(2)}, u32[]{:S(2)}) %collective-permute-start.4) | collective-permute-done | bytes 1056 | tf_op jit(solution)/shard_map/ppermute | solution.py:26
  16.2 1.4 %group_faces.1 = (f32[64,128]{1,0:T(8,128)S(1)}, f32[1,128]{1,0:T(1,128)S(1)}, f32[1,128]{1,0:T(1,128)S(1)}, f32[2,128]{1,0:T(2,128)S(1)}) custom-call(f32[3,128,128]{2,1,0:T(8,128)S(1)} %get-tuple-element.27.refs_0_, s32[3,128,128]{2,1,0:T(8,128)S(1)} %get-tuple-element.28.refs_1_, f32[3,128,128]{2,1,0:T(8,128)S(1)} %get-tuple-element.29.refs_2_, ...), custom_call_target="tpu_custom_call" | custom-call | flops 16777216 | bytes 1048576 | tf_op jit(solution)/shard_map/group_faces/pallas_call | solution.py:458
  17.6 0.2 collective-permute-start.8
  17.8 0.0 collective-permute-start.5
  17.8 1.1 %collective-permute-start.6 = (f32[2,128]{1,0:T(2,128)S(1)}, f32[2,128]{1,0:T(2,128)S(1)}, u32[]{:S(2)}, u32[]{:S(2)}) collective-permute-start(f32[2,128]{1,0:T(2,128)S(1)} %get-tuple-element.45), channel_id=1, source_target_pairs={{8,16},{12,20},{24,0},{28,4},{16,8},{20,12},{0,24},{4,28},{9,17},{... | collective-permute-start | bytes 3080 | tf_op jit(solution)/shard_map/ppermute | solution.py:21
  18.9 1.7 %collective-permute-done.8.refs_7_ = f32[2,128]{1,0:T(2,128)S(1)} collective-permute-done((f32[2,128]{1,0:T(2,128)S(1)}, f32[2,128]{1,0:T(2,128)S(1)}, u32[]{:S(2)}, u32[]{:S(2)}) %collective-permute-start.8) | collective-permute-done | bytes 1056 | tf_op jit(solution)/shard_map/ppermute | solution.py:26
  20.7 0.2 collective-permute-start.9
  20.8 0.6 %collective-permute-done.5.refs_5_ = f32[2,128]{1,0:T(2,128)S(1)} collective-permute-done((f32[2,128]{1,0:T(2,128)S(1)}, f32[2,128]{1,0:T(2,128)S(1)}, u32[]{:S(2)}, u32[]{:S(2)}) %collective-permute-start.5) | collective-permute-done | bytes 1056 | tf_op jit(solution)/shard_map/ppermute | solution.py:21
  21.4 1.8 %collective-permute-done.6.refs_4_ = f32[2,128]{1,0:T(2,128)S(1)} collective-permute-done((f32[2,128]{1,0:T(2,128)S(1)}, f32[2,128]{1,0:T(2,128)S(1)}, u32[]{:S(2)}, u32[]{:S(2)}) %collective-permute-start.6) | collective-permute-done | bytes 1056 | tf_op jit(solution)/shard_map/ppermute | solution.py:21
  23.2 1.3 %collective-permute-start.7 = (f32[2,128]{1,0:T(2,128)S(1)}, f32[2,128]{1,0:T(2,128)S(1)}, u32[]{:S(2)}, u32[]{:S(2)}) collective-permute-start(f32[2,128]{1,0:T(2,128)S(1)} %pad_maximum_fusion.2), channel_id=1, source_target_pairs={{0,4},{4,0},{8,12},{12,8},{16,20},{20,16},{24,28},{28,24},{1,5},{5... | collective-permute-start | bytes 3080 | tf_op jit(solution)/shard_map/ppermute | solution.py:26
  24.5 0.0 collective-permute-done.9.refs_8_
  24.5 2.4 %collective-permute-done.7.refs_3_ = f32[2,128]{1,0:T(2,128)S(1)} collective-permute-done((f32[2,128]{1,0:T(2,128)S(1)}, f32[2,128]{1,0:T(2,128)S(1)}, u32[]{:S(2)}, u32[]{:S(2)}) %collective-permute-start.7) | collective-permute-done | bytes 1056 | tf_op jit(solution)/shard_map/ppermute | solution.py:26
  26.9 0.8 %scatter_back.1 = f32[64,128]{1,0:T(8,128)} custom-call(f32[64,128]{1,0:T(8,128)S(1)} %get-tuple-element.40.refs_0_, s32[1,128]{1,0:T(1,128)S(1)} %get-tuple-element.41.refs_1_, s32[4,128]{1,0:T(4,128)S(1)} %get-tuple-element.42.refs_2_, f32[2,128]{1,0:T(2,128)S(1)} %collective-permute-done.7.refs_3_, f32[2,128]{1,0:T(2,128)S(1)} %collective-permute-done.6.refs_4_, ...), custom_call_target="tpu_custom_call" | custom-call | tf_op jit(solution)/shard_map/scatter_back/pallas_call | solution.py:592
  (7 shorter events, 0.1 us)
Async XLA Ops:
  0.9 12.2 %collective-permute-start.3 = (f32[1,128]{1,0:T(1,128)S(1)}, f32[1,128]{1,0:T(1,128)S(1)}, u32[]{:S(2)}, u32[]{:S(2)}) collective-permute-start(f32[1,128]{1,0:T(1,128)S(1)} %get-tuple-element.39.refs_9_), channel_id=1, source_target_pairs={{0,1},{1,0},{2,3},{3,2},{4,5},{5,4},{6,7},{7,6},{8,9},{9,8},{10,11... | collective-permute-start | bytes 1544 | tf_op jit(solution)/shard_map/ppermute | solution.py:26
  1.5 6.7 %collective-permute-start = (f32[2,128]{1,0:T(2,128)S(1)}, f32[2,128]{1,0:T(2,128)S(1)}, u32[]{:S(2)}, u32[]{:S(2)}) collective-permute-start(f32[2,128]{1,0:T(2,128)S(1)} %get-tuple-element.35), channel_id=1, source_target_pairs={{0,24},{4,28},{8,0},{12,4},{16,8},{20,12},{24,16},{28,20},{1,25},{... | collective-permute-start | bytes 3080 | tf_op jit(solution)/shard_map/ppermute | solution.py:43
  6.2 5.4 %collective-permute-start.1 = (f32[2,128]{1,0:T(2,128)S(1)}, f32[2,128]{1,0:T(2,128)S(1)}, u32[]{:S(2)}, u32[]{:S(2)}) collective-permute-start(f32[2,128]{1,0:T(2,128)S(1)} %get-tuple-element.36), channel_id=1, source_target_pairs={{0,8},{4,12},{8,16},{12,20},{16,24},{20,28},{24,0},{28,4},{1,9},{5... | collective-permute-start | bytes 3080 | tf_op jit(solution)/shard_map/ppermute | solution.py:43
  11.5 3.6 %collective-permute-start.2 = (f32[2,128]{1,0:T(2,128)S(1)}, f32[2,128]{1,0:T(2,128)S(1)}, u32[]{:S(2)}, u32[]{:S(2)}) collective-permute-start(f32[2,128]{1,0:T(2,128)S(1)} %pad_maximum_fusion), channel_id=1, source_target_pairs={{0,4},{4,0},{8,12},{12,8},{16,20},{20,16},{24,28},{28,24},{1,5},{5... | collective-permute-start | bytes 3080 | tf_op jit(solution)/shard_map/ppermute | solution.py:26
  13.1 3.1 %collective-permute-start.4 = (f32[2,128]{1,0:T(2,128)S(1)}, f32[2,128]{1,0:T(2,128)S(1)}, u32[]{:S(2)}, u32[]{:S(2)}) collective-permute-start(f32[2,128]{1,0:T(2,128)S(1)} %pad_maximum_fusion.1), channel_id=1, source_target_pairs={{0,3},{1,2},{2,1},{3,0},{4,7},{5,6},{6,5},{7,4},{8,11},{9,10},{10,... | collective-permute-start | bytes 3080 | tf_op jit(solution)/shard_map/ppermute | solution.py:26
  17.6 3.0 %collective-permute-start.8 = (f32[2,128]{1,0:T(2,128)S(1)}, f32[2,128]{1,0:T(2,128)S(1)}, u32[]{:S(2)}, u32[]{:S(2)}) collective-permute-start(f32[2,128]{1,0:T(2,128)S(1)} %get-tuple-element.47), channel_id=1, source_target_pairs={{0,3},{1,2},{2,1},{3,0},{4,7},{5,6},{6,5},{7,4},{8,11},{9,10},{10,... | collective-permute-start | bytes 3080 | tf_op jit(solution)/shard_map/ppermute | solution.py:26
  17.8 3.6 %collective-permute-start.5 = (f32[2,128]{1,0:T(2,128)S(1)}, f32[2,128]{1,0:T(2,128)S(1)}, u32[]{:S(2)}, u32[]{:S(2)}) collective-permute-start(f32[2,128]{1,0:T(2,128)S(1)} %get-tuple-element.44), channel_id=1, source_target_pairs={{0,8},{4,12},{16,24},{20,28},{8,0},{12,4},{24,16},{28,20},{1,9},{5... | collective-permute-start | bytes 3080 | tf_op jit(solution)/shard_map/ppermute | solution.py:21
  17.8 5.4 %collective-permute-start.6 = (f32[2,128]{1,0:T(2,128)S(1)}, f32[2,128]{1,0:T(2,128)S(1)}, u32[]{:S(2)}, u32[]{:S(2)}) collective-permute-start(f32[2,128]{1,0:T(2,128)S(1)} %get-tuple-element.45), channel_id=1, source_target_pairs={{8,16},{12,20},{24,0},{28,4},{16,8},{20,12},{0,24},{4,28},{9,17},{... | collective-permute-start | bytes 3080 | tf_op jit(solution)/shard_map/ppermute | solution.py:21
  20.7 3.9 %collective-permute-start.9 = (f32[2,128]{1,0:T(2,128)S(1)}, f32[2,128]{1,0:T(2,128)S(1)}, u32[]{:S(2)}, u32[]{:S(2)}) collective-permute-start(f32[2,128]{1,0:T(2,128)S(1)} %pad_maximum_fusion.3), channel_id=1, source_target_pairs={{0,1},{1,0},{2,3},{3,2},{4,5},{5,4},{6,7},{7,6},{8,9},{9,8},{10,11... | collective-permute-start | bytes 3080 | tf_op jit(solution)/shard_map/ppermute | solution.py:26
  23.2 3.6 %collective-permute-start.7 = (f32[2,128]{1,0:T(2,128)S(1)}, f32[2,128]{1,0:T(2,128)S(1)}, u32[]{:S(2)}, u32[]{:S(2)}) collective-permute-start(f32[2,128]{1,0:T(2,128)S(1)} %pad_maximum_fusion.2), channel_id=1, source_target_pairs={{0,4},{4,0},{8,12},{12,8},{16,20},{20,16},{24,28},{28,24},{1,5},{5... | collective-permute-start | bytes 3080 | tf_op jit(solution)/shard_map/ppermute | solution.py:26
